TPU v7x, 32 devices: a whole 2x2x4 slice. The times are simulated.
32 devices in a mesh: dp: 8 (over z, y), tensor: 4 (over x, core).
Axes of the slice: x: 2, y: 2, z: 4, core: 2. Of those that a mesh axis runs over, the one named last changes fastest.
Arguments:
- qkv: bfloat16 [3, 2048, 4096], P(None, 'dp', 'tensor'), may hold values from -6 to 6
- segment_ids: int32 [8, 4, 64], P('dp'), may hold values from 0 to 1, never falling along the last dimension, each value on 1 to 63 neighbouring positions
- out_weight: bfloat16 [4096, 4096], P(None, 'tensor'), may hold values from -0.09375 to 0.09375
- out_bias: bfloat16 [4096], replicated, may hold values from -3 to 3
- upstream: bfloat16 [2048, 4096], P(('dp', 'tensor')), may hold values from -6 to 6
- pre_act: bfloat16 [2048, 8192], P('dp', 'tensor'), may hold values from -6 to 6
- down_weight: bfloat16 [4096, 8192], P('dp', 'tensor'), may hold values from -0.0625 to 0.0625
Outputs:
- attention_out: float32 [2048, 4096], P(('dp', 'tensor'))
- act_grad: float32 [2048, 8192], P('dp', 'tensor')
- weight_grad: float32 [4096, 8192], P('dp', 'tensor')
Inputs may be any that keep to these rules, and one draw needn't show every extreme that they name: `segment_ids`: within each pack the ids never fall; 2 images a pack, each of 1 to 63 tokens.
All inputs are finite; a program needn't handle non-finite values.
Results may differ from a plain program's by a relative error of at most 0.0055.
Values may be sent and summed in bfloat16 or wider, within the bound.
No kernel may reach another device: no remote copies, remote signals or barrier semaphores. Data moves between devices by JAX's collectives and lax.ppermute only.
A program may use at most 128 MiB of HBM per device.

v0:
```python
import math

import jax
import jax.numpy as jnp
from jax import lax
from jax.sharding import PartitionSpec as P


HEAD = 128
ROWS_DEV = 64


root_half = 1.0 / math.sqrt(2.0)
inv_root_tau = 1.0 / math.sqrt(2.0 * math.pi)
f32, bf16 = jnp.float32, jnp.bfloat16


def gelu_exact(argument):
    return 0.5 * argument * (1.0 + lax.erf(argument * root_half))


def gelu_slope(argument):
    return (
        0.5 * (1.0 + lax.erf(argument * root_half))
        + argument * jnp.exp(-0.5 * argument * argument) * inv_root_tau
    )


def attend(qkv, labels):
    length = qkv.shape[1]
    head_count = qkv.shape[2] // HEAD
    queries = qkv[0].reshape(length, head_count, HEAD)
    key_rows = qkv[1].reshape(length, head_count, HEAD)
    value_rows = qkv[2].reshape(length, head_count, HEAD)
    scores = jnp.einsum("qhd,khd->hqk", queries, key_rows, preferred_element_type=jnp.float32) * (
        1.0 / math.sqrt(HEAD)
    )
    pack_of = jnp.arange(length, dtype=jnp.int32) // ROWS_DEV
    same_image = ((labels[:, None] == labels[None, :]) & (pack_of[:, None] == pack_of[None, :]))[
        None
    ]
    masked = jnp.where(same_image, scores, -1e30)
    row_top = jnp.max(masked, axis=2, keepdims=True)
    exponent = jnp.where(same_image, jnp.exp(masked - row_top), 0.0)
    weights = (exponent / jnp.sum(exponent, axis=2, keepdims=True)).astype(jnp.bfloat16)
    context = jnp.einsum("hqk,khd->qhd", weights, value_rows, preferred_element_type=jnp.float32)
    return context.reshape(length, head_count * HEAD).astype(jnp.bfloat16)


def make_body(n_dp, n_tensor):
    line, cross = n_dp // 2, n_tensor // 2

    def along_line(value, shift, keep=lambda z: True):
        pairs = []
        for z in range(line):
            if keep(z):
                for side in range(2):
                    pairs.append((2 * z + side, 2 * ((z + shift) % line) + side))
        return lax.ppermute(value, "dp", pairs)

    def across_side(value):
        return lax.ppermute(value, "dp", [(i, i ^ 1) for i in range(n_dp)])

    def across_core(value):
        return lax.ppermute(value, "tensor", [(t, t ^ 1) for t in range(n_tensor)])

    def along_cross(value, shift):
        return lax.ppermute(
            value, "tensor", [(t, (t + 2 * shift) % n_tensor) for t in range(n_tensor)]
        )

    def place(own, other, index, axis):
        first = jnp.where(index == 0, own, other)
        second = jnp.where(index == 0, other, own)
        return jnp.concatenate([first, second], axis=axis)

    def body(qkv, segment_ids, out_weight, out_bias, upstream, pre_act, down_weight):
        dp = lax.axis_index("dp")
        z, side = dp // 2, dp % 2
        t = lax.axis_index("tensor")
        x, core = t // 2, t % 2
        mine, d_model = upstream.shape
        tokens, hidden = pre_act.shape
        d_line = d_model // line
        d_side = d_line // 2
        half = hidden // 2

        groups = [sorted({1, line - 1}), [*range(2, line - 1), 0]]
        shifted = []
        for k in [*groups[0], *groups[1]]:
            columns = lax.dynamic_slice(
                upstream, (0, ((z + k) % line) * d_line), (mine, d_line)
            )
            shifted.append(columns if k == 0 else along_line(columns, k))
        count = len(groups[0])
        grads = []
        for blocks in (shifted[:count], shifted[count:]):
            grad = jnp.stack(blocks)
            grad = jnp.stack([grad, across_side(grad)], axis=1)
            rolled = jnp.stack([grad] + [along_cross(grad, k) for k in range(1, cross)])
            swapped = across_core(rolled)
            placed = []
            for to_x in range(cross):
                for to_core in range(2):
                    value = None
                    for k in range(cross):
                        part = jnp.where(core == to_core, rolled[k], swapped[k])
                        value = (
                            part
                            if value is None
                            else jnp.where((x - to_x) % cross == k, part, value)
                        )
                    placed.append(value)
            grad = jnp.stack(placed, axis=2)
            grads.append(grad.reshape(len(blocks), 2, tokens, d_line))
        block_of = {}
        for g, blocks in enumerate(groups):
            for i, k in enumerate(blocks):
                block_of[k] = (g, i)

        preact = pre_act.astype(f32)
        activation, slope = lax.optimization_barrier(
            (gelu_exact(preact).astype(bf16), gelu_slope(preact))
        )
        quarter = half // 2
        acts = []
        for q in range(2):
            keep = lax.dynamic_slice(
                activation, (0, side * half + q * quarter), (tokens, quarter)
            )
            give = lax.dynamic_slice(
                activation, (0, (1 - side) * half + q * quarter), (tokens, quarter)
            )
            acts.append(jnp.concatenate([keep, across_side(give)], axis=0))

        stored_rows = down_weight.shape[0]
        w_keep = lax.dynamic_slice(down_weight, (0, side * half), (stored_rows, half))
        w_got = []
        for q in range(2):
            w_give = lax.dynamic_slice(
                down_weight,
                (q * (stored_rows // 2), (1 - side) * half),
                (stored_rows // 2, half),
            )
            w_got.append(across_side(w_give))
        weight = place(w_keep, jnp.concatenate(w_got, axis=0), side, 0)

        context = attend(qkv, segment_ids[0].reshape(-1))
        partial = lax.dot_general(
            context, out_weight, (((1,), (1,)), ((), ())), preferred_element_type=f32
        ).astype(bf16)
        share = partial.shape[0] // n_tensor
        total = lax.dynamic_slice(partial, (t * share, 0), (share, d_model)).astype(f32)
        for k in range(1, n_tensor):
            rows = lax.dynamic_slice(
                partial, (((t + k) % n_tensor) * share, 0), (share, d_model)
            )
            pairs = [(i, (i + k) % n_tensor) for i in range(n_tensor)]
            total = total + lax.ppermute(rows, "tensor", pairs).astype(f32)
        attention_out = total + out_bias.astype(f32)

        products = {}
        for g in range(2):
            for h in (1, 0):
                product = lax.dot_general(
                    grads[g][:, h], weight, (((2,), (0,)), ((), ())), preferred_element_type=f32
                )
                products[g, h] = lax.optimization_barrier(product)

        def part(k, h):
            g, i = block_of[k]
            return products[g, h][i]

        sums = {}
        for h in (1, 0):
            right = left = None
            for s in range(1, line):
                out_right, out_left = part(s, h), part(line - s, h)
                if right is not None:
                    out_right = out_right + right.astype(f32)
                    out_left = out_left + left.astype(f32)
                right = along_line(out_right.astype(bf16), 1, lambda p, s=s: p < s and p < line - 1)
                left = along_line(
                    out_left.astype(bf16), -1, lambda p, s=s: p > line - 1 - s and p > 0
                )
            sums[h] = part(0, h) + right.astype(f32) + left.astype(f32)
        other_h = across_side(sums[1].astype(bf16)).astype(f32)
        act_grad = place(sums[0], other_h, side, 1) * slope

        outs = []
        for q in range(2):
            ups, downs = [], []
            right = left = acts[q]
            for s in range(1, line):
                right = along_line(right, 1, lambda p, s=s: s - 1 <= p < line - 1)
                left = along_line(left, -1, lambda p, s=s: 0 < p <= line - s)
                ups.append(right)
                downs.append(left)
            product = None
            for g, blocks in enumerate(groups):
                chunk = jnp.concatenate(
                    [
                        acts[q] if k == 0 else jnp.where(z >= k, ups[k - 1], downs[line - k - 1])
                        for k in blocks
                    ],
                    axis=0,
                )
                term = lax.dot_general(
                    grads[g].reshape(-1, d_line),
                    chunk,
                    (((0,), (0,)), ((), ())),
                    preferred_element_type=f32,
                )
                product = term if product is None else product + term
            product = product * (1.0 / n_dp)
            own = lax.dynamic_slice(product, (side * d_side, 0), (d_side, quarter))
            other = lax.dynamic_slice(product, ((1 - side) * d_side, 0), (d_side, quarter))
            outs.append((own, across_side(other.astype(bf16)).astype(f32)))
        own = jnp.concatenate([o[0] for o in outs], axis=1)
        other = jnp.concatenate([o[1] for o in outs], axis=1)
        weight_grad = place(own, other, side, 1)
        return (attention_out, act_grad, weight_grad)

    return body


def solution(mesh):
    n_dp, n_tensor = mesh.shape["dp"], mesh.shape["tensor"]
    return jax.shard_map(
        make_body(n_dp, n_tensor),
        mesh=mesh,
        in_specs=(
            P(None, "dp", "tensor"),
            P("dp", None, None),
            P(None, "tensor"),
            P(),
            P(("dp", "tensor"), None),
            P("dp", "tensor"),
            P("dp", "tensor"),
        ),
        out_specs=(P(("dp", "tensor"), None), P("dp", "tensor"), P("dp", "tensor")),
        check_vma=False,
    )
```

profile of v0, /device:TPU:0, one launch (start us, length us, event | category | flops | bytes accessed | tf_op | source)
XLA Modules:
  0.0 213.2 jit_solution(17362148718351115489)
XLA Ops:
  0.7 2.1 fusion.7
  3.7 3.0 %collective-permute-start.27 = (bf16[256,512]{1,0:T(8,128)(2,1)}, bf16[256,512]{1,0:T(8,128)(2,1)}, u32[]{:S(2)}, u32[]{:S(2)}) collective-permute-start(bf16[256,512]{1,0:T(8,128)(2,1)} %get-tuple-element.42), channel_id=1, source_target_pairs={{0,4},{4,0},{8,12},{12,8},{16,20},{20,16},{24,28},{28,24},{1,5},{5... | collective-permute-start | bytes 786440 | tf_op jit(solution)/shard_map/ppermute | solution.py:62
  6.7 1.9 constant_dynamic-slice_fusion.7
  8.6 2.6 %collective-permute-start.3 = (bf16[64,1024]{1,0:T(8,128)(2,1)}, bf16[64,1024]{1,0:T(8,128)(2,1)}, u32[]{:S(2)}, u32[]{:S(2)}) collective-permute-start(bf16[64,1024]{1,0:T(8,128)(2,1)} %get-tuple-element.49), channel_id=1, source_target_pairs={{0,16},{4,20},{8,24},{12,28},{16,0},{20,4},{24,8},{28,12},{1,17},{... | collective-permute-start | bytes 393224 | tf_op jit(solution)/shard_map/ppermute | solution.py:59
  11.2 1.6 collective-permute-start.9
  12.7 2.2 %collective-permute-start.10 = (bf16[64,1024]{1,0:T(8,128)(2,1)}, bf16[64,1024]{1,0:T(8,128)(2,1)}, u32[]{:S(2)}, u32[]{:S(2)}) collective-permute-start(bf16[64,1024]{1,0:T(8,128)(2,1)} %get-tuple-element.50), channel_id=1, source_target_pairs={{0,24},{4,28},{8,0},{12,4},{16,8},{20,12},{24,16},{28,20},{1,25},{... | collective-permute-start | bytes 393224 | tf_op jit(solution)/shard_map/ppermute | solution.py:59
  15.5 2.3 %fusion.55 = (bf16[1,256,1024]{2,1,0:T(8,128)(2,1)S(1)}, bf16[1,256,1024]{2,1,0:T(8,128)(2,1)}, bf16[1,256,1024]{2,1,0:T(8,128)(2,1)S(1)}) fusion(bf16[3,256,1024]{2,1,0:T(8,128)(2,1)} %param.7), kind=kLoop, calls=%fused_computation.158 | loop fusion | bytes 3145728 | tf_op jit(solution)/shard_map/slice | solution.py:33
  17.8 2.0 copy.43
  21.3 3.5 %fusion.56 = (f32[8,256]{1,0:T(8,128)S(1)}, f32[8,256,256]{1,2,0:T(8,128)}) fusion(pred[256,256]{0,1:T(8,128)(4,1)S(1)} %compare_and_fusion, bf16[256,8,128]{0,2,1:T(8,128)(2,1)} %bitcast.206, bf16[256,8,128]{0,2,1:T(8,128)(2,1)} %bitcast.207), kind=kOutput, calls=%fused_computation.159 | convolution fusion | flops 136839424 | bytes 3219456 | tf_op jit(solution)/shard_map/sub | solution.py:44
  24.8 1.9 convolution_convert_fusion.1
  26.7 5.8 %convolution_convert_fusion = bf16[256,4096]{1,0:T(8,128)(2,1)S(1)} fusion(bf16[256,1024]{0,1:T(8,128)(2,1)S(1)} %bitcast.209, bf16[4096,1024]{1,0:T(8,128)(2,1)} %param.9), kind=kOutput, calls=%fused_computation.1 | convolution fusion | flops 2148532224 | bytes 11010048 | tf_op jit(solution)/shard_map/dot_general | solution.py:149
  32.6 1.3 copy-done.2
  33.9 1.2 constant_dynamic-slice_fusion.12
  38.0 1.6 collective-permute-start.1
  39.6 1.4 collective-permute-start.2
  41.0 1.5 collective-permute-start.4
  42.5 1.0 fusion.51
  46.1 4.1 %collective-permute-done.4 = bf16[2,64,1024]{2,1,0:T(8,128)(2,1)S(1)} collective-permute-done((bf16[2,64,1024]{2,1,0:T(8,128)(2,1)S(1)}, bf16[2,64,1024]{2,1,0:T(8,128)(2,1)S(1)}, u32[]{:S(2)}, u32[]{:S(2)}) %collective-permute-start.4) | collective-permute-done | bytes 262176 | tf_op jit(solution)/shard_map/ppermute | solution.py:62
  50.2 1.5 collective-permute-start.7
  51.8 4.0 %collective-permute-done.11 = bf16[2,64,1024]{2,1,0:T(8,128)(2,1)S(1)} collective-permute-done((bf16[2,64,1024]{2,1,0:T(8,128)(2,1)S(1)}, bf16[2,64,1024]{2,1,0:T(8,128)(2,1)S(1)}, u32[]{:S(2)}, u32[]{:S(2)}) %collective-permute-start.11) | collective-permute-done | bytes 262176 | tf_op jit(solution)/shard_map/ppermute | solution.py:62
  55.8 1.5 collective-permute-start.8
  57.4 1.4 collective-permute-start.29
  58.8 4.6 %collective-permute-start.28 = (bf16[512,512]{1,0:T(8,128)(2,1)S(1)}, bf16[512,512]{1,0:T(8,128)(2,1)S(1)}, u32[]{:S(2)}, u32[]{:S(2)}) collective-permute-start(bf16[512,512]{1,0:T(8,128)(2,1)S(1)} %pad_maximum_fusion.9), channel_id=1, source_target_pairs={{0,8},{4,12},{8,16},{12,20},{16,24},{20,28},{1,9},{5,13},{9,17},{1... | collective-permute-start | bytes 1572872 | tf_op jit(solution)/shard_map/ppermute | solution.py:59
  63.4 1.3 collective-permute-start.36
  64.7 2.3 %add_add_fusion = f32[64,4096]{1,0:T(8,128)} fusion(bf16[64,4096]{1,0:T(8,128)(2,1)S(1)} %collective-permute-done.2, bf16[64,4096]{1,0:T(8,128)(2,1)S(1)} %collective-permute-done.1, bf16[64,4096]{1,0:T(8,128)(2,1)S(1)} %collective-permute-done, f32[4096]{0:T(1024)S(1)} %convert_element_type.131, bf16[256,4096]{1,0:T(8,128)(2,1)} %copy-done.2, s32[]{:T(128)S(6)} %select_n.292), kind=kLoop, calls=%fused_computation.83 | loop fusion | flops 2097152 | bytes 3162116 | tf_op jit(solution)/shard_map/add | solution.py:160
  67.0 4.6 %collective-permute-start.35 = (bf16[512,512]{1,0:T(8,128)(2,1)S(1)}, bf16[512,512]{1,0:T(8,128)(2,1)S(1)}, u32[]{:S(2)}, u32[]{:S(2)}) collective-permute-start(bf16[512,512]{1,0:T(8,128)(2,1)S(1)} %pad_maximum_fusion.10), channel_id=1, source_target_pairs={{0,8},{4,12},{8,16},{12,20},{16,24},{20,28},{1,9},{5,13},{9,17},{1... | collective-permute-start | bytes 1572872 | tf_op jit(solution)/shard_map/ppermute | solution.py:59
  71.6 4.8 %collective-permute-done.8 = bf16[256,1024]{1,0:T(8,128)(2,1)S(1)} collective-permute-done((bf16[256,1024]{1,0:T(8,128)(2,1)S(1)}, bf16[256,1024]{1,0:T(8,128)(2,1)S(1)}, u32[]{:S(2)}, u32[]{:S(2)}) %collective-permute-start.8) | collective-permute-done | bytes 524320 | tf_op jit(solution)/shard_map/ppermute | solution.py:62
  76.4 1.4 collective-permute-start.5
  78.6 1.3 collective-permute-start.30
  81.9 3.5 %collective-permute-done.35 = bf16[512,512]{1,0:T(8,128)(2,1)S(1)} collective-permute-done((bf16[512,512]{1,0:T(8,128)(2,1)S(1)}, bf16[512,512]{1,0:T(8,128)(2,1)S(1)}, u32[]{:S(2)}, u32[]{:S(2)}) %collective-permute-start.35) | collective-permute-done | bytes 524320 | tf_op jit(solution)/shard_map/ppermute | solution.py:59
  85.4 1.3 collective-permute-start.37
  86.7 4.5 %collective-permute-done.5 = bf16[2,2,64,1024]{3,2,1,0:T(8,128)(2,1)S(1)} collective-permute-done((bf16[2,2,64,1024]{3,2,1,0:T(8,128)(2,1)S(1)}, bf16[2,2,64,1024]{3,2,1,0:T(8,128)(2,1)S(1)}, u32[]{:S(2)}, u32[]{:S(2)}) %collective-permute-start.5) | collective-permute-done | bytes 524320 | tf_op jit(solution)/shard_map/ppermute | solution.py:68
  92.0 8.2 %collective-permute-done.12 = bf16[2,2,64,1024]{3,2,1,0:T(8,128)(2,1)S(1)} collective-permute-done((bf16[2,2,64,1024]{3,2,1,0:T(8,128)(2,1)S(1)}, bf16[2,2,64,1024]{3,2,1,0:T(8,128)(2,1)S(1)}, u32[]{:S(2)}, u32[]{:S(2)}) %collective-permute-start.12) | collective-permute-done | bytes 524320 | tf_op jit(solution)/shard_map/ppermute | solution.py:68
  101.6 2.1 collective-permute-done.37
  103.7 1.3 collective-permute-start.31
  105.8 1.5 collective-permute-start.38
  107.4 13.0 %collective-permute-done.31 = bf16[512,512]{1,0:T(8,128)(2,1)S(1)} collective-permute-done((bf16[512,512]{1,0:T(8,128)(2,1)S(1)}, bf16[512,512]{1,0:T(8,128)(2,1)S(1)}, u32[]{:S(2)}, u32[]{:S(2)}) %collective-permute-start.31) | collective-permute-done | bytes 524320 | tf_op jit(solution)/shard_map/ppermute | solution.py:59
  120.4 8.2 %collective-permute-done.38 = bf16[512,512]{1,0:T(8,128)(2,1)S(1)} collective-permute-done((bf16[512,512]{1,0:T(8,128)(2,1)S(1)}, bf16[512,512]{1,0:T(8,128)(2,1)S(1)}, u32[]{:S(2)}, u32[]{:S(2)}) %collective-permute-start.38) | collective-permute-done | bytes 524320 | tf_op jit(solution)/shard_map/ppermute | solution.py:59
  130.5 1.3 fusion.14
  131.8 1.3 fusion.9
  133.0 1.3 fusion.17
  134.3 1.3 fusion.13
  135.6 2.2 %fusion.21 = f32[1024,512]{1,0:T(8,128)S(1)} fusion(bf16[1024,1024]{1,0:T(8,128)(2,1)S(1)} %bitcast.200, bf16[256,512]{1,0:T(8,128)(2,1)} %collective-permute-done.27, bf16[256,512]{1,0:T(8,128)(2,1)S(1)} %copy-done.3, bf16[512,512]{1,0:T(8,128)(2,1)S(1)} %broadcast_select_fusion.3), kind=kOutput, calls=%fused_computation.57 | convolution fusion | flops 1076887552 | bytes 5242880 | tf_op jit(solution)/shard_map/dot_general | solution.py:208
  137.8 1.3 add_multiply_fusion.1
  139.2 1.6 collective-permute-start.41
  140.9 1.5 collective-permute-start.20
  143.3 1.3 collective-permute-start.14
  145.3 2.2 %fusion.30 = f32[1024,512]{1,0:T(8,128)S(1)} fusion(bf16[1024,1024]{1,0:T(8,128)(2,1)S(1)} %bitcast.201, bf16[256,512]{1,0:T(8,128)(2,1)} %collective-permute-done.34, bf16[256,512]{1,0:T(8,128)(2,1)S(1)} %get-tuple-element.41, bf16[512,512]{1,0:T(8,128)(2,1)S(1)} %broadcast_select_fusion.2), kind=kOutput, calls=%fused_computation.66 | convolution fusion | flops 1076887552 | bytes 5242880 | tf_op jit(solution)/shard_map/dot_general | solution.py:208
  147.5 7.1 %collective-permute-done.20 = bf16[256,1024]{1,0:T(8,128)(2,1)S(1)} collective-permute-done((bf16[256,1024]{1,0:T(8,128)(2,1)S(1)}, bf16[256,1024]{1,0:T(8,128)(2,1)S(1)}, u32[]{:S(2)}, u32[]{:S(2)}) %collective-permute-start.20) | collective-permute-done | bytes 524320 | tf_op jit(solution)/shard_map/ppermute | solution.py:59
  155.0 4.4 %collective-permute-start.21 = (bf16[256,1024]{1,0:T(8,128)(2,1)S(1)}, bf16[256,1024]{1,0:T(8,128)(2,1)S(1)}, u32[]{:S(2)}, u32[]{:S(2)}) collective-permute-start(bf16[256,1024]{1,0:T(8,128)(2,1)S(1)} %get-tuple-element.21), channel_id=1, source_target_pairs={{0,8},{4,12},{8,16},{12,20},{1,9},{5,13},{9,17},{13,21},{2,10},{6,... | collective-permute-start | bytes 1572872 | tf_op jit(solution)/shard_map/ppermute | solution.py:59
  160.1 1.3 add_multiply_fusion
  161.4 4.5 %collective-permute-done.14 = bf16[256,1024]{1,0:T(8,128)(2,1)S(1)} collective-permute-done((bf16[256,1024]{1,0:T(8,128)(2,1)S(1)}, bf16[256,1024]{1,0:T(8,128)(2,1)S(1)}, u32[]{:S(2)}, u32[]{:S(2)}) %collective-permute-start.14) | collective-permute-done | bytes 524320 | tf_op jit(solution)/shard_map/ppermute | solution.py:59
  166.2 4.4 %collective-permute-start.15 = (bf16[256,1024]{1,0:T(8,128)(2,1)S(1)}, bf16[256,1024]{1,0:T(8,128)(2,1)S(1)}, u32[]{:S(2)}, u32[]{:S(2)}) collective-permute-start(bf16[256,1024]{1,0:T(8,128)(2,1)S(1)} %get-tuple-element.15), channel_id=1, source_target_pairs={{0,8},{4,12},{8,16},{12,20},{1,9},{5,13},{9,17},{13,21},{2,10},{6,... | collective-permute-start | bytes 1572872 | tf_op jit(solution)/shard_map/ppermute | solution.py:59
  171.4 5.8 %collective-permute-done.21 = bf16[256,1024]{1,0:T(8,128)(2,1)S(1)} collective-permute-done((bf16[256,1024]{1,0:T(8,128)(2,1)S(1)}, bf16[256,1024]{1,0:T(8,128)(2,1)S(1)}, u32[]{:S(2)}, u32[]{:S(2)}) %collective-permute-start.21) | collective-permute-done | bytes 524320 | tf_op jit(solution)/shard_map/ppermute | solution.py:59
  177.5 4.6 %collective-permute-start.22 = (bf16[256,1024]{1,0:T(8,128)(2,1)S(1)}, bf16[256,1024]{1,0:T(8,128)(2,1)S(1)}, u32[]{:S(2)}, u32[]{:S(2)}) collective-permute-start(bf16[256,1024]{1,0:T(8,128)(2,1)S(1)} %get-tuple-element.19), channel_id=1, source_target_pairs={{0,8},{4,12},{8,16},{12,20},{16,24},{20,28},{1,9},{5,13},{9,17},{1... | collective-permute-start | bytes 1572872 | tf_op jit(solution)/shard_map/ppermute | solution.py:59
  182.2 1.3 collective-permute-start.25
  183.8 4.6 %collective-permute-done.15 = bf16[256,1024]{1,0:T(8,128)(2,1)S(1)} collective-permute-done((bf16[256,1024]{1,0:T(8,128)(2,1)S(1)}, bf16[256,1024]{1,0:T(8,128)(2,1)S(1)}, u32[]{:S(2)}, u32[]{:S(2)}) %collective-permute-start.15) | collective-permute-done | bytes 524320 | tf_op jit(solution)/shard_map/ppermute | solution.py:59
  189.3 4.4 %collective-permute-start.16 = (bf16[256,1024]{1,0:T(8,128)(2,1)S(1)}, bf16[256,1024]{1,0:T(8,128)(2,1)S(1)}, u32[]{:S(2)}, u32[]{:S(2)}) collective-permute-start(bf16[256,1024]{1,0:T(8,128)(2,1)S(1)} %get-tuple-element.13), channel_id=1, source_target_pairs={{0,8},{4,12},{8,16},{12,20},{16,24},{20,28},{1,9},{5,13},{9,17},{1... | collective-permute-start | bytes 1572872 | tf_op jit(solution)/shard_map/ppermute | solution.py:59
  193.7 5.9 %collective-permute-done.22 = bf16[256,1024]{1,0:T(8,128)(2,1)S(1)} collective-permute-done((bf16[256,1024]{1,0:T(8,128)(2,1)S(1)}, bf16[256,1024]{1,0:T(8,128)(2,1)S(1)}, u32[]{:S(2)}, u32[]{:S(2)}) %collective-permute-start.22) | collective-permute-done | bytes 524320 | tf_op jit(solution)/shard_map/ppermute | solution.py:59
  199.6 1.3 collective-permute-start.19
  202.4 2.5 %pad_maximum_fusion = f32[512,2048]{1,0:T(8,128)} fusion(f32[512,1024]{1,0:T(8,128)S(1)} %get-tuple-element.10, f32[512,1024]{1,0:T(8,128)S(1)} %get-tuple-element.9), kind=kLoop, calls=%fused_computation.2 | loop fusion | flops 1048576 | bytes 8388608 | tf_op jit(solution)/shard_map/concatenate | solution.py:75
  204.9 1.9 collective-permute-done.16
  206.8 4.3 %collective-permute-done.19 = bf16[256,1024]{1,0:T(8,128)(2,1)S(1)} collective-permute-done((bf16[256,1024]{1,0:T(8,128)(2,1)S(1)}, bf16[256,1024]{1,0:T(8,128)(2,1)S(1)}, u32[]{:S(2)}, u32[]{:S(2)}) %collective-permute-start.19) | collective-permute-done | bytes 524320 | tf_op jit(solution)/shard_map/ppermute | solution.py:59
  211.5 1.7 maximum_multiply_fusion
  (101 shorter events, 23.5 us)
Async XLA Ops:
  3.7 37.3 %collective-permute-start.27 = (bf16[256,512]{1,0:T(8,128)(2,1)}, bf16[256,512]{1,0:T(8,128)(2,1)}, u32[]{:S(2)}, u32[]{:S(2)}) collective-permute-start(bf16[256,512]{1,0:T(8,128)(2,1)} %get-tuple-element.42), channel_id=1, source_target_pairs={{0,4},{4,0},{8,12},{12,8},{16,20},{20,16},{24,28},{28,24},{1,5},{5... | collective-permute-start | bytes 786440 | tf_op jit(solution)/shard_map/ppermute | solution.py:62
  8.6 28.4 %collective-permute-start.3 = (bf16[64,1024]{1,0:T(8,128)(2,1)}, bf16[64,1024]{1,0:T(8,128)(2,1)}, u32[]{:S(2)}, u32[]{:S(2)}) collective-permute-start(bf16[64,1024]{1,0:T(8,128)(2,1)} %get-tuple-element.49), channel_id=1, source_target_pairs={{0,16},{4,20},{8,24},{12,28},{16,0},{20,4},{24,8},{28,12},{1,17},{... | collective-permute-start | bytes 393224 | tf_op jit(solution)/shard_map/ppermute | solution.py:59
  11.2 26.8 %collective-permute-start.9 = (bf16[64,1024]{1,0:T(8,128)(2,1)}, bf16[64,1024]{1,0:T(8,128)(2,1)}, u32[]{:S(2)}, u32[]{:S(2)}) collective-permute-start(bf16[64,1024]{1,0:T(8,128)(2,1)} %get-tuple-element.47), channel_id=1, source_target_pairs={{0,8},{4,12},{8,16},{12,20},{16,24},{20,28},{24,0},{28,4},{1,9},{5... | collective-permute-start | bytes 393224 | tf_op jit(solution)/shard_map/ppermute | solution.py:59
  12.7 26.8 %collective-permute-start.10 = (bf16[64,1024]{1,0:T(8,128)(2,1)}, bf16[64,1024]{1,0:T(8,128)(2,1)}, u32[]{:S(2)}, u32[]{:S(2)}) collective-permute-start(bf16[64,1024]{1,0:T(8,128)(2,1)} %get-tuple-element.50), channel_id=1, source_target_pairs={{0,24},{4,28},{8,0},{12,4},{16,8},{20,12},{24,16},{28,20},{1,25},{... | collective-permute-start | bytes 393224 | tf_op jit(solution)/shard_map/ppermute | solution.py:59
  15.0 28.5 %collective-permute-start.34 = (bf16[256,512]{1,0:T(8,128)(2,1)}, bf16[256,512]{1,0:T(8,128)(2,1)}, u32[]{:S(2)}, u32[]{:S(2)}) collective-permute-start(bf16[256,512]{1,0:T(8,128)(2,1)} %get-tuple-element.40), channel_id=1, source_target_pairs={{0,4},{4,0},{8,12},{12,8},{16,20},{20,16},{24,28},{28,24},{1,5},{5... | collective-permute-start | bytes 786440 | tf_op jit(solution)/shard_map/ppermute | solution.py:62
  15.5 5.4 %copy-start.6 = (s32[1,4,64]{2,1,0:T(4,128)S(1)}, s32[1,4,64]{2,1,0:T(4,128)}, u32[]{:S(2)}) copy-start(s32[1,4,64]{2,1,0:T(4,128)} %param.8) | copy-start | bytes 3076
  32.6 1.3 copy-start.2
  33.9 2.2 %copy-start = (bf16[512,2048]{1,0:T(8,128)(2,1)S(1)}, bf16[512,2048]{1,0:T(8,128)(2,1)}, u32[]{:S(2)}) copy-start(bf16[512,2048]{1,0:T(8,128)(2,1)} %param.13) | copy-start | bytes 6291460
  33.9 3.0 %copy-start.5 = (bf16[4096]{0:T(1024)(128)(2,1)S(1)}, bf16[4096]{0:T(1024)(128)(2,1)}, u32[]{:S(2)}) copy-start(bf16[4096]{0:T(1024)(128)(2,1)} %param.10) | copy-start | bytes 24580
  36.0 8.1 %copy-start.3 = (bf16[256,512]{1,0:T(8,128)(2,1)S(1)}, bf16[256,512]{1,0:T(8,128)(2,1)}, u32[]{:S(2)}) copy-start(bf16[256,512]{1,0:T(8,128)(2,1)} %get-tuple-element.39) | copy-start | bytes 786436
  36.9 13.2 %copy-start.4 = (bf16[256,1024]{1,0:T(8,128)(2,1)S(1)}, bf16[256,1024]{1,0:T(8,128)(2,1)}, u32[]{:S(2)}) copy-start(bf16[256,1024]{1,0:T(8,128)(2,1)} %get-tuple-element.29) | copy-start | bytes 1572868
  36.9 20.4 %collective-permute-start = (bf16[64,4096]{1,0:T(8,128)(2,1)}, bf16[64,4096]{1,0:T(8,128)(2,1)S(1)}, u32[]{:S(2)}, u32[]{:S(2)}) collective-permute-start(bf16[64,4096]{1,0:T(8,128)(2,1)} %get-tuple-element.33), channel_id=1, source_target_pairs={{0,1},{1,2},{2,3},{3,0},{4,5},{5,6},{6,7},{7,4},{8,9},{9,10},{10,1... | collective-permute-start | bytes 1572872 | tf_op jit(solution)/shard_map/ppermute | solution.py:159
  38.0 20.8 %collective-permute-start.1 = (bf16[64,4096]{1,0:T(8,128)(2,1)}, bf16[64,4096]{1,0:T(8,128)(2,1)S(1)}, u32[]{:S(2)}, u32[]{:S(2)}) collective-permute-start(bf16[64,4096]{1,0:T(8,128)(2,1)} %get-tuple-element.35), channel_id=1, source_target_pairs={{0,2},{1,3},{2,0},{3,1},{4,6},{5,7},{6,4},{7,5},{8,10},{9,11},{10,... | collective-permute-start | bytes 1572872 | tf_op jit(solution)/shard_map/ppermute | solution.py:159
  39.6 23.9 %collective-permute-start.2 = (bf16[64,4096]{1,0:T(8,128)(2,1)}, bf16[64,4096]{1,0:T(8,128)(2,1)S(1)}, u32[]{:S(2)}, u32[]{:S(2)}) collective-permute-start(bf16[64,4096]{1,0:T(8,128)(2,1)} %get-tuple-element.34), channel_id=1, source_target_pairs={{0,3},{1,0},{2,1},{3,2},{4,7},{5,4},{6,5},{7,6},{8,11},{9,8},{10,9... | collective-permute-start | bytes 1572872 | tf_op jit(solution)/shard_map/ppermute | solution.py:159
  41.0 9.2 %collective-permute-start.4 = (bf16[2,64,1024]{2,1,0:T(8,128)(2,1)S(1)}, bf16[2,64,1024]{2,1,0:T(8,128)(2,1)S(1)}, u32[]{:S(2)}, u32[]{:S(2)}) collective-permute-start(bf16[2,64,1024]{2,1,0:T(8,128)(2,1)S(1)} %get-tuple-element.56), channel_id=1, source_target_pairs={{0,4},{4,0},{8,12},{12,8},{16,20},{20,16},{24,28},{28,24},{1,5},{5... | collective-permute-start | bytes 786440 | tf_op jit(solution)/shard_map/ppermute | solution.py:62
  43.5 12.3 %collective-permute-start.11 = (bf16[2,64,1024]{2,1,0:T(8,128)(2,1)S(1)}, bf16[2,64,1024]{2,1,0:T(8,128)(2,1)S(1)}, u32[]{:S(2)}, u32[]{:S(2)}) collective-permute-start(bf16[2,64,1024]{2,1,0:T(8,128)(2,1)S(1)} %get-tuple-element.54), channel_id=1, source_target_pairs={{0,4},{4,0},{8,12},{12,8},{16,20},{20,16},{24,28},{28,24},{1,5},{5... | collective-permute-start | bytes 786440 | tf_op jit(solution)/shard_map/ppermute | solution.py:62
  50.2 16.9 %collective-permute-start.7 = (bf16[256,1024]{1,0:T(8,128)(2,1)S(1)}, bf16[256,1024]{1,0:T(8,128)(2,1)S(1)}, u32[]{:S(2)}, u32[]{:S(2)}) collective-permute-start(bf16[256,1024]{1,0:T(8,128)(2,1)S(1)} %copy-done.4), channel_id=1, source_target_pairs={{0,4},{4,0},{8,12},{12,8},{16,20},{20,16},{24,28},{28,24},{1,5},{5... | collective-permute-start | bytes 1572872 | tf_op jit(solution)/shard_map/ppermute | solution.py:62
  55.8 20.6 %collective-permute-start.8 = (bf16[256,1024]{1,0:T(8,128)(2,1)S(1)}, bf16[256,1024]{1,0:T(8,128)(2,1)S(1)}, u32[]{:S(2)}, u32[]{:S(2)}) collective-permute-start(bf16[256,1024]{1,0:T(8,128)(2,1)S(1)} %get-tuple-element.28), channel_id=1, source_target_pairs={{0,4},{4,0},{8,12},{12,8},{16,20},{20,16},{24,28},{28,24},{1,5},{5... | collective-permute-start | bytes 1572872 | tf_op jit(solution)/shard_map/ppermute | solution.py:62
  57.4 23.9 %copy-start.1 = (bf16[512,2048]{1,0:T(8,128)(2,1)S(1)}, bf16[512,2048]{1,0:T(8,128)(2,1)}, u32[]{:S(2)}) copy-start(bf16[512,2048]{1,0:T(8,128)(2,1)} %param.13) | copy-start | bytes 6291460
  57.4 20.4 %collective-permute-start.29 = (bf16[512,512]{1,0:T(8,128)(2,1)S(1)}, bf16[512,512]{1,0:T(8,128)(2,1)S(1)}, u32[]{:S(2)}, u32[]{:S(2)}) collective-permute-start(bf16[512,512]{1,0:T(8,128)(2,1)S(1)} %pad_maximum_fusion.9), channel_id=1, source_target_pairs={{8,0},{12,4},{16,8},{20,12},{24,16},{28,20},{9,1},{13,5},{17,9},{2... | collective-permute-start | bytes 1572872 | tf_op jit(solution)/shard_map/ppermute | solution.py:59
  58.8 19.7 %collective-permute-start.28 = (bf16[512,512]{1,0:T(8,128)(2,1)S(1)}, bf16[512,512]{1,0:T(8,128)(2,1)S(1)}, u32[]{:S(2)}, u32[]{:S(2)}) collective-permute-start(bf16[512,512]{1,0:T(8,128)(2,1)S(1)} %pad_maximum_fusion.9), channel_id=1, source_target_pairs={{0,8},{4,12},{8,16},{12,20},{16,24},{20,28},{1,9},{5,13},{9,17},{1... | collective-permute-start | bytes 1572872 | tf_op jit(solution)/shard_map/ppermute | solution.py:59
  63.4 17.1 %collective-permute-start.36 = (bf16[512,512]{1,0:T(8,128)(2,1)S(1)}, bf16[512,512]{1,0:T(8,128)(2,1)S(1)}, u32[]{:S(2)}, u32[]{:S(2)}) collective-permute-start(bf16[512,512]{1,0:T(8,128)(2,1)S(1)} %pad_maximum_fusion.10), channel_id=1, source_target_pairs={{8,0},{12,4},{16,8},{20,12},{24,16},{28,20},{9,1},{13,5},{17,9},{2... | collective-permute-start | bytes 1572872 | tf_op jit(solution)/shard_map/ppermute | solution.py:59
  67.0 18.3 %collective-permute-start.35 = (bf16[512,512]{1,0:T(8,128)(2,1)S(1)}, bf16[512,512]{1,0:T(8,128)(2,1)S(1)}, u32[]{:S(2)}, u32[]{:S(2)}) collective-permute-start(bf16[512,512]{1,0:T(8,128)(2,1)S(1)} %pad_maximum_fusion.10), channel_id=1, source_target_pairs={{0,8},{4,12},{8,16},{12,20},{16,24},{20,28},{1,9},{5,13},{9,17},{1... | collective-permute-start | bytes 1572872 | tf_op jit(solution)/shard_map/ppermute | solution.py:59
  76.4 14.8 %collective-permute-start.5 = (bf16[2,2,64,1024]{3,2,1,0:T(8,128)(2,1)S(1)}, bf16[2,2,64,1024]{3,2,1,0:T(8,128)(2,1)S(1)}, u32[]{:S(2)}, u32[]{:S(2)}) collective-permute-start(bf16[2,2,64,1024]{3,2,1,0:T(8,128)(2,1)S(1)} %get-tuple-element.52), channel_id=1, source_target_pairs={{0,2},{1,3},{2,0},{3,1},{4,6},{5,7},{6,4},{7,5},{8,10},{9,11},{10,... | collective-permute-start | bytes 1572872 | tf_op jit(solution)/shard_map/ppermute | solution.py:68
  77.8 22.4 %collective-permute-start.12 = (bf16[2,2,64,1024]{3,2,1,0:T(8,128)(2,1)S(1)}, bf16[2,2,64,1024]{3,2,1,0:T(8,128)(2,1)S(1)}, u32[]{:S(2)}, u32[]{:S(2)}) collective-permute-start(bf16[2,2,64,1024]{3,2,1,0:T(8,128)(2,1)S(1)} %get-tuple-element.46), channel_id=1, source_target_pairs={{0,2},{1,3},{2,0},{3,1},{4,6},{5,7},{6,4},{7,5},{8,10},{9,11},{10,... | collective-permute-start | bytes 1572872 | tf_op jit(solution)/shard_map/ppermute | solution.py:68
  78.6 21.7 %collective-permute-start.30 = (bf16[512,512]{1,0:T(8,128)(2,1)S(1)}, bf16[512,512]{1,0:T(8,128)(2,1)S(1)}, u32[]{:S(2)}, u32[]{:S(2)}) collective-permute-start(bf16[512,512]{1,0:T(8,128)(2,1)S(1)} %collective-permute-done.29), channel_id=1, source_target_pairs={{8,0},{12,4},{16,8},{20,12},{9,1},{13,5},{17,9},{21,13},{10,2},{14... | collective-permute-start | bytes 1572872 | tf_op jit(solution)/shard_map/ppermute | solution.py:59
  80.6 20.3 %collective-permute-start.32 = (bf16[512,512]{1,0:T(8,128)(2,1)S(1)}, bf16[512,512]{1,0:T(8,128)(2,1)S(1)}, u32[]{:S(2)}, u32[]{:S(2)}) collective-permute-start(bf16[512,512]{1,0:T(8,128)(2,1)S(1)} %collective-permute-done.28), channel_id=1, source_target_pairs={{8,16},{12,20},{16,24},{20,28},{9,17},{13,21},{17,25},{21,29},{10,... | collective-permute-start | bytes 1572872 | tf_op jit(solution)/shard_map/ppermute | solution.py:59
  85.4 18.3 %collective-permute-start.37 = (bf16[512,512]{1,0:T(8,128)(2,1)S(1)}, bf16[512,512]{1,0:T(8,128)(2,1)S(1)}, u32[]{:S(2)}, u32[]{:S(2)}) collective-permute-start(bf16[512,512]{1,0:T(8,128)(2,1)S(1)} %collective-permute-done.36), channel_id=1, source_target_pairs={{8,0},{12,4},{16,8},{20,12},{9,1},{13,5},{17,9},{21,13},{10,2},{14... | collective-permute-start | bytes 1572872 | tf_op jit(solution)/shard_map/ppermute | solution.py:59
  91.2 13.8 %collective-permute-start.39 = (bf16[512,512]{1,0:T(8,128)(2,1)S(1)}, bf16[512,512]{1,0:T(8,128)(2,1)S(1)}, u32[]{:S(2)}, u32[]{:S(2)}) collective-permute-start(bf16[512,512]{1,0:T(8,128)(2,1)S(1)} %collective-permute-done.35), channel_id=1, source_target_pairs={{8,16},{12,20},{16,24},{20,28},{9,17},{13,21},{17,25},{21,29},{10,... | collective-permute-start | bytes 1572872 | tf_op jit(solution)/shard_map/ppermute | solution.py:59
  100.2 28.5 %collective-permute-start.6 = (bf16[2,2,2,64,1024]{4,3,2,1,0:T(8,128)(2,1)S(1)}, bf16[2,2,2,64,1024]{4,3,2,1,0:T(8,128)(2,1)S(1)}, u32[]{:S(2)}, u32[]{:S(2)}) collective-permute-start(bf16[2,2,2,64,1024]{4,3,2,1,0:T(8,128)(2,1)S(1)} %pad_maximum_fusion.4), channel_id=1, source_target_pairs={{0,1},{1,0},{2,3},{3,2},{4,5},{5,4},{6,7},{7,6},{8,9},{9,8},{10,11... | collective-permute-start | bytes 3145736 | tf_op jit(solution)/shard_map/ppermute | solution.py:65
  100.3 29.5 %collective-permute-start.13 = (bf16[2,2,2,64,1024]{4,3,2,1,0:T(8,128)(2,1)S(1)}, bf16[2,2,2,64,1024]{4,3,2,1,0:T(8,128)(2,1)S(1)}, u32[]{:S(2)}, u32[]{:S(2)}) collective-permute-start(bf16[2,2,2,64,1024]{4,3,2,1,0:T(8,128)(2,1)S(1)} %pad_maximum_fusion.5), channel_id=1, source_target_pairs={{0,1},{1,0},{2,3},{3,2},{4,5},{5,4},{6,7},{7,6},{8,9},{9,8},{10,11... | collective-permute-start | bytes 3145736 | tf_op jit(solution)/shard_map/ppermute | solution.py:65
  100.8 4.9 %collective-permute-start.33 = (bf16[512,512]{1,0:T(8,128)(2,1)S(1)}, bf16[512,512]{1,0:T(8,128)(2,1)S(1)}, u32[]{:S(2)}, u32[]{:S(2)}) collective-permute-start(bf16[512,512]{1,0:T(8,128)(2,1)S(1)} %collective-permute-done.32), channel_id=1, source_target_pairs={{16,24},{20,28},{17,25},{21,29},{18,26},{22,30},{19,27},{23,31}} | collective-permute-start | bytes 1572872 | tf_op jit(solution)/shard_map/ppermute | solution.py:59
  103.7 16.7 %collective-permute-start.31 = (bf16[512,512]{1,0:T(8,128)(2,1)S(1)}, bf16[512,512]{1,0:T(8,128)(2,1)S(1)}, u32[]{:S(2)}, u32[]{:S(2)}) collective-permute-start(bf16[512,512]{1,0:T(8,128)(2,1)S(1)} %collective-permute-done.30), channel_id=1, source_target_pairs={{8,0},{12,4},{9,1},{13,5},{10,2},{14,6},{11,3},{15,7}} | collective-permute-start | bytes 1572872 | tf_op jit(solution)/shard_map/ppermute | solution.py:59
  105.0 2.3 %collective-permute-start.40 = (bf16[512,512]{1,0:T(8,128)(2,1)S(1)}, bf16[512,512]{1,0:T(8,128)(2,1)S(1)}, u32[]{:S(2)}, u32[]{:S(2)}) collective-permute-start(bf16[512,512]{1,0:T(8,128)(2,1)S(1)} %collective-permute-done.39), channel_id=1, source_target_pairs={{16,24},{20,28},{17,25},{21,29},{18,26},{22,30},{19,27},{23,31}} | collective-permute-start | bytes 1572872 | tf_op jit(solution)/shard_map/ppermute | solution.py:59
  105.8 22.8 %collective-permute-start.38 = (bf16[512,512]{1,0:T(8,128)(2,1)S(1)}, bf16[512,512]{1,0:T(8,128)(2,1)S(1)}, u32[]{:S(2)}, u32[]{:S(2)}) collective-permute-start(bf16[512,512]{1,0:T(8,128)(2,1)S(1)} %collective-permute-done.37), channel_id=1, source_target_pairs={{8,0},{12,4},{9,1},{13,5},{10,2},{14,6},{11,3},{15,7}} | collective-permute-start | bytes 1572872 | tf_op jit(solution)/shard_map/ppermute | solution.py:59
  139.2 62.6 %collective-permute-start.41 = (bf16[512,512]{1,0:T(8,128)(2,1)S(1)}, bf16[512,512]{1,0:T(8,128)(2,1)S(1)}, u32[]{:S(2)}, u32[]{:S(2)}) collective-permute-start(bf16[512,512]{1,0:T(8,128)(2,1)S(1)} %dynamic-slice_convert_fusion.1), channel_id=1, source_target_pairs={{0,4},{4,0},{8,12},{12,8},{16,20},{20,16},{24,28},{28,24},{1,5},{5... | collective-permute-start | bytes 1572872 | tf_op jit(solution)/shard_map/ppermute | solution.py:62
  140.9 13.8 %collective-permute-start.20 = (bf16[256,1024]{1,0:T(8,128)(2,1)S(1)}, bf16[256,1024]{1,0:T(8,128)(2,1)S(1)}, u32[]{:S(2)}, u32[]{:S(2)}) collective-permute-start(bf16[256,1024]{1,0:T(8,128)(2,1)S(1)} %get-tuple-element.23), channel_id=1, source_target_pairs={{0,8},{4,12},{1,9},{5,13},{2,10},{6,14},{3,11},{7,15}} | collective-permute-start | bytes 1572872 | tf_op jit(solution)/shard_map/ppermute | solution.py:59
  142.4 12.3 %collective-permute-start.23 = (bf16[256,1024]{1,0:T(8,128)(2,1)S(1)}, bf16[256,1024]{1,0:T(8,128)(2,1)S(1)}, u32[]{:S(2)}, u32[]{:S(2)}) collective-permute-start(bf16[256,1024]{1,0:T(8,128)(2,1)S(1)} %get-tuple-element.24), channel_id=1, source_target_pairs={{24,16},{28,20},{25,17},{29,21},{26,18},{30,22},{27,19},{31,23}} | collective-permute-start | bytes 1572872 | tf_op jit(solution)/shard_map/ppermute | solution.py:59
  143.3 22.6 %collective-permute-start.14 = (bf16[256,1024]{1,0:T(8,128)(2,1)S(1)}, bf16[256,1024]{1,0:T(8,128)(2,1)S(1)}, u32[]{:S(2)}, u32[]{:S(2)}) collective-permute-start(bf16[256,1024]{1,0:T(8,128)(2,1)S(1)} %get-tuple-element.17), channel_id=1, source_target_pairs={{0,8},{4,12},{1,9},{5,13},{2,10},{6,14},{3,11},{7,15}} | collective-permute-start | bytes 1572872 | tf_op jit(solution)/shard_map/ppermute | solution.py:59
  144.6 21.3 %collective-permute-start.17 = (bf16[256,1024]{1,0:T(8,128)(2,1)S(1)}, bf16[256,1024]{1,0:T(8,128)(2,1)S(1)}, u32[]{:S(2)}, u32[]{:S(2)}) collective-permute-start(bf16[256,1024]{1,0:T(8,128)(2,1)S(1)} %get-tuple-element.18), channel_id=1, source_target_pairs={{24,16},{28,20},{25,17},{29,21},{26,18},{30,22},{27,19},{31,23}} | collective-permute-start | bytes 1572872 | tf_op jit(solution)/shard_map/ppermute | solution.py:59
  155.0 22.2 %collective-permute-start.21 = (bf16[256,1024]{1,0:T(8,128)(2,1)S(1)}, bf16[256,1024]{1,0:T(8,128)(2,1)S(1)}, u32[]{:S(2)}, u32[]{:S(2)}) collective-permute-start(bf16[256,1024]{1,0:T(8,128)(2,1)S(1)} %get-tuple-element.21), channel_id=1, source_target_pairs={{0,8},{4,12},{8,16},{12,20},{1,9},{5,13},{9,17},{13,21},{2,10},{6,... | collective-permute-start | bytes 1572872 | tf_op jit(solution)/shard_map/ppermute | solution.py:59
  159.4 17.7 %collective-permute-start.24 = (bf16[256,1024]{1,0:T(8,128)(2,1)S(1)}, bf16[256,1024]{1,0:T(8,128)(2,1)S(1)}, u32[]{:S(2)}, u32[]{:S(2)}) collective-permute-start(bf16[256,1024]{1,0:T(8,128)(2,1)S(1)} %get-tuple-element.22), channel_id=1, source_target_pairs={{16,8},{20,12},{24,16},{28,20},{17,9},{21,13},{25,17},{29,21},{18,... | collective-permute-start | bytes 1572872 | tf_op jit(solution)/shard_map/ppermute | solution.py:59
  166.2 22.2 %collective-permute-start.15 = (bf16[256,1024]{1,0:T(8,128)(2,1)S(1)}, bf16[256,1024]{1,0:T(8,128)(2,1)S(1)}, u32[]{:S(2)}, u32[]{:S(2)}) collective-permute-start(bf16[256,1024]{1,0:T(8,128)(2,1)S(1)} %get-tuple-element.15), channel_id=1, source_target_pairs={{0,8},{4,12},{8,16},{12,20},{1,9},{5,13},{9,17},{13,21},{2,10},{6,... | collective-permute-start | bytes 1572872 | tf_op jit(solution)/shard_map/ppermute | solution.py:59
  170.7 18.2 %collective-permute-start.18 = (bf16[256,1024]{1,0:T(8,128)(2,1)S(1)}, bf16[256,1024]{1,0:T(8,128)(2,1)S(1)}, u32[]{:S(2)}, u32[]{:S(2)}) collective-permute-start(bf16[256,1024]{1,0:T(8,128)(2,1)S(1)} %get-tuple-element.16), channel_id=1, source_target_pairs={{16,8},{20,12},{24,16},{28,20},{17,9},{21,13},{25,17},{29,21},{18,... | collective-permute-start | bytes 1572872 | tf_op jit(solution)/shard_map/ppermute | solution.py:59
  177.5 22.1 %collective-permute-start.22 = (bf16[256,1024]{1,0:T(8,128)(2,1)S(1)}, bf16[256,1024]{1,0:T(8,128)(2,1)S(1)}, u32[]{:S(2)}, u32[]{:S(2)}) collective-permute-start(bf16[256,1024]{1,0:T(8,128)(2,1)S(1)} %get-tuple-element.19), channel_id=1, source_target_pairs={{0,8},{4,12},{8,16},{12,20},{16,24},{20,28},{1,9},{5,13},{9,17},{1... | collective-permute-start | bytes 1572872 | tf_op jit(solution)/shard_map/ppermute | solution.py:59
  182.2 18.7 %collective-permute-start.25 = (bf16[256,1024]{1,0:T(8,128)(2,1)S(1)}, bf16[256,1024]{1,0:T(8,128)(2,1)S(1)}, u32[]{:S(2)}, u32[]{:S(2)}) collective-permute-start(bf16[256,1024]{1,0:T(8,128)(2,1)S(1)} %get-tuple-element.20), channel_id=1, source_target_pairs={{8,0},{12,4},{16,8},{20,12},{24,16},{28,20},{9,1},{13,5},{17,9},{2... | collective-permute-start | bytes 1572872 | tf_op jit(solution)/shard_map/ppermute | solution.py:59
  188.4 13.4 %collective-permute-start.42 = (bf16[512,512]{1,0:T(8,128)(2,1)S(1)}, bf16[512,512]{1,0:T(8,128)(2,1)S(1)}, u32[]{:S(2)}, u32[]{:S(2)}) collective-permute-start(bf16[512,512]{1,0:T(8,128)(2,1)S(1)} %dynamic-slice_convert_fusion), channel_id=1, source_target_pairs={{0,4},{4,0},{8,12},{12,8},{16,20},{20,16},{24,28},{28,24},{1,5},{5... | collective-permute-start | bytes 1572872 | tf_op jit(solution)/shard_map/ppermute | solution.py:62
  189.3 17.5 %collective-permute-start.16 = (bf16[256,1024]{1,0:T(8,128)(2,1)S(1)}, bf16[256,1024]{1,0:T(8,128)(2,1)S(1)}, u32[]{:S(2)}, u32[]{:S(2)}) collective-permute-start(bf16[256,1024]{1,0:T(8,128)(2,1)S(1)} %get-tuple-element.13), channel_id=1, source_target_pairs={{0,8},{4,12},{8,16},{12,20},{16,24},{20,28},{1,9},{5,13},{9,17},{1... | collective-permute-start | bytes 1572872 | tf_op jit(solution)/shard_map/ppermute | solution.py:59
  199.6 11.5 %collective-permute-start.19 = (bf16[256,1024]{1,0:T(8,128)(2,1)S(1)}, bf16[256,1024]{1,0:T(8,128)(2,1)S(1)}, u32[]{:S(2)}, u32[]{:S(2)}) collective-permute-start(bf16[256,1024]{1,0:T(8,128)(2,1)S(1)} %get-tuple-element.14), channel_id=1, source_target_pairs={{8,0},{12,4},{16,8},{20,12},{24,16},{28,20},{9,1},{13,5},{17,9},{2... | collective-permute-start | bytes 1572872 | tf_op jit(solution)/shard_map/ppermute | solution.py:59
  201.2 10.0 %collective-permute-start.26 = (bf16[256,1024]{1,0:T(8,128)(2,1)S(1)}, bf16[256,1024]{1,0:T(8,128)(2,1)S(1)}, u32[]{:S(2)}, u32[]{:S(2)}) collective-permute-start(bf16[256,1024]{1,0:T(8,128)(2,1)S(1)} %fusion.12), channel_id=1, source_target_pairs={{0,4},{4,0},{8,12},{12,8},{16,20},{20,16},{24,28},{28,24},{1,5},{5... | collective-permute-start | bytes 1572872 | tf_op jit(solution)/shard_map/ppermute | solution.py:62
where the time goes:
time: 216 us; the launch traced here: 213 us
  waiting for transfers between devices  87.2 us (40%)
  starting transfers between devices  69.4 us (32%)
  matrix products  23.3 us (11%)
  other arithmetic  17.7 us (8%)
  local copies, waits for them, and re-layouts  14.3 us (7%)
    ppermute x27, waiting for transfers between devices, along_line(): return lax.ppermute(value, 'dp', pairs)  61.6 us
    ppermute x27, starting transfers between devices, along_line(): return lax.ppermute(value, 'dp', pairs)  52.4 us
    ppermute x9, waiting for transfers between devices, across_side(): return lax.ppermute(value, 'dp', [(i, i ^ 1) for i in range(n_dp)])  12.9 us
    ppermute x2, waiting for transfers between devices, along_cross(): lax.ppermute(value, 'tensor', [(t, (t + 2 * shift) % n_tensor) for t in r...  12.7 us
    ppermute x9, starting transfers between devices, across_side(): return lax.ppermute(value, 'dp', [(i, i ^ 1) for i in range(n_dp)])  11.3 us
    dot_general x4, matrix products, body(): lax.dot_general(grads[g].reshape(-1, d_line), chunk, (((0,), (0,)), ((),...  7.04 us
    dot_general x1, matrix products, body(): lax.dot_general(context, out_weight, (((1,), (1,)), ((), ())), preferred_...  5.8 us
    unnamed x17, local copies, waits for them, and re-layouts  5.37 us
  transfers between devices with their start and end apart: 43, of which 17 were waited for; matrix products, arithmetic and copies ran while one was open for 18% of the time, Pallas kernels for 0%

commit v1 on v0

v1 whole, which is shorter than its diff:
```python
import math

import jax
import jax.numpy as jnp
from jax import lax
from jax.sharding import PartitionSpec as P


HEAD = 128
ROWS_DEV = 64


root_half = 1.0 / math.sqrt(2.0)
inv_root_tau = 1.0 / math.sqrt(2.0 * math.pi)
f32, bf16 = jnp.float32, jnp.bfloat16


def gelu_exact(argument):
    return 0.5 * argument * (1.0 + lax.erf(argument * root_half))


def gelu_slope(argument):
    return (
        0.5 * (1.0 + lax.erf(argument * root_half))
        + argument * jnp.exp(-0.5 * argument * argument) * inv_root_tau
    )


def attend(qkv, labels):
    length = qkv.shape[1]
    head_count = qkv.shape[2] // HEAD
    queries = qkv[0].reshape(length, head_count, HEAD)
    key_rows = qkv[1].reshape(length, head_count, HEAD)
    value_rows = qkv[2].reshape(length, head_count, HEAD)
    scores = jnp.einsum("qhd,khd->hqk", queries, key_rows, preferred_element_type=jnp.float32) * (
        1.0 / math.sqrt(HEAD)
    )
    pack_of = jnp.arange(length, dtype=jnp.int32) // ROWS_DEV
    same_image = ((labels[:, None] == labels[None, :]) & (pack_of[:, None] == pack_of[None, :]))[
        None
    ]
    masked = jnp.where(same_image, scores, -1e30)
    row_top = jnp.max(masked, axis=2, keepdims=True)
    exponent = jnp.where(same_image, jnp.exp(masked - row_top), 0.0)
    weights = (exponent / jnp.sum(exponent, axis=2, keepdims=True)).astype(jnp.bfloat16)
    context = jnp.einsum("hqk,khd->qhd", weights, value_rows, preferred_element_type=jnp.float32)
    return context.reshape(length, head_count * HEAD).astype(jnp.bfloat16)


STREAMS = 2


def make_body(n_dp, n_tensor):
    line, cross = n_dp // 2, n_tensor // 2

    def along_line(value, shift, keep=lambda z: True):
        pairs = []
        for z in range(line):
            if keep(z):
                for side in range(2):
                    pairs.append((2 * z + side, 2 * ((z + shift) % line) + side))
        return lax.ppermute(value, "dp", pairs)

    def across_side(value):
        return lax.ppermute(value, "dp", [(i, i ^ 1) for i in range(n_dp)])

    def across_core(value):
        return lax.ppermute(value, "tensor", [(t, t ^ 1) for t in range(n_tensor)])

    def along_cross(value, shift):
        return lax.ppermute(
            value, "tensor", [(t, (t + 2 * shift) % n_tensor) for t in range(n_tensor)]
        )

    def place(own, other, index, axis):
        first = jnp.where(index == 0, own, other)
        second = jnp.where(index == 0, other, own)
        return jnp.concatenate([first, second], axis=axis)

    def body(qkv, segment_ids, out_weight, out_bias, upstream, pre_act, down_weight):
        dp = lax.axis_index("dp")
        z, side = dp // 2, dp % 2
        t = lax.axis_index("tensor")
        x, core = t // 2, t % 2
        mine, d_model = upstream.shape
        tokens, hidden = pre_act.shape
        d_line = d_model // line
        d_side = d_line // 2
        half = hidden // 2

        def weight_grad_of(grads, act, ups, downs):
            product = None
            for g, blocks in enumerate(groups):
                chunk = jnp.concatenate(
                    [
                        act if k == 0 else jnp.where(z >= k, ups[k - 1], downs[line - k - 1])
                        for k in blocks
                    ],
                    axis=0,
                )
                term = lax.dot_general(
                    grads[g].reshape(-1, d_line),
                    chunk,
                    (((0,), (0,)), ((), ())),
                    preferred_element_type=f32,
                )
                product = term if product is None else product + term
            product = product * (1.0 / n_dp)
            own = lax.dynamic_slice(product, (side * d_side, 0), (d_side, width))
            other = lax.dynamic_slice(product, ((1 - side) * d_side, 0), (d_side, width))
            other = other.astype(bf16)
            return own, across_side(other)

        groups = [sorted({1, line - 1}), [*range(2, line - 1), 0]]
        shifted = []
        for k in [*groups[0], *groups[1]]:
            columns = lax.dynamic_slice(
                upstream, (0, ((z + k) % line) * d_line), (mine, d_line)
            )
            shifted.append(columns if k == 0 else along_line(columns, k))
        block_of = {k: (g, i) for g, blocks in enumerate(groups) for i, k in enumerate(blocks)}

        def gather_grad(g):
            blocks = shifted[: len(groups[0])] if g == 0 else shifted[len(groups[0]) :]
            grad = jnp.stack(blocks)
            grad = jnp.stack([grad, across_side(grad)], axis=1)
            got = [along_cross(grad, k) for k in range(1, cross)]
            rolled = jnp.stack([grad] + got)
            swapped = across_core(rolled)
            placed = []
            for to_x in range(cross):
                for to_core in range(2):
                    value = None
                    for k in range(cross):
                        part = jnp.where(core == to_core, rolled[k], swapped[k])
                        value = (
                            part
                            if value is None
                            else jnp.where((x - to_x) % cross == k, part, value)
                        )
                    placed.append(value)
            grad = jnp.stack(placed, axis=2)
            return grad.reshape(len(blocks), 2 * tokens, d_line)

        preact = pre_act.astype(f32)
        activation, slope = lax.optimization_barrier(
            (gelu_exact(preact).astype(bf16), gelu_slope(preact))
        )
        width = half // STREAMS
        acts = []
        for q in range(STREAMS):
            keep = lax.dynamic_slice(activation, (0, side * half + q * width), (tokens, width))
            give = lax.dynamic_slice(
                activation, (0, (1 - side) * half + q * width), (tokens, width)
            )
            acts.append(jnp.concatenate([keep, across_side(give)], axis=0))

        stored_rows = down_weight.shape[0]
        pieces = lax.optimization_barrier(
            [
                lax.dynamic_slice(down_weight, (0, s * half + q * width), (stored_rows, width))
                for q in range(STREAMS)
                for s in (side, 1 - side)
            ]
        )
        got_rows = [across_side(pieces[2 * q + 1]) for q in range(STREAMS)]

        weights, grads, products = [], [], {}

        def multiply(g, q):
            product = lax.dot_general(
                grads[g], weights[q], (((2,), (0,)), ((), ())), preferred_element_type=f32
            )
            products[g, q] = lax.optimization_barrier(product)

        grads.append(gather_grad(0))
        for q in range(STREAMS):
            weights.append(place(pieces[2 * q], got_rows[q], side, 0))
            multiply(0, q)
        grads.append(gather_grad(1))
        for q in range(STREAMS):
            multiply(1, q)

        def part(k, q):
            g, i = block_of[k]
            return products[g, q][i]

        moving = [(acts[q], acts[q]) for q in range(STREAMS)]
        ups, downs = [[] for _ in moving], [[] for _ in moving]
        outs, own_h, other_h = [], [], []
        for s in range(1, line + 1):
            for q in range(STREAMS):
                right, left = moving[q]
                if s > 1:
                    ups[q].append(right)
                    downs[q].append(left)
                    right = right.astype(f32) + jnp.where(z < s - 1, part(s - 1, q), 0.0)
                    left = left.astype(f32) + jnp.where(z > line - s, part(line - s + 1, q), 0.0)
                    right, left = right.astype(bf16), left.astype(bf16)
                if s == line:
                    outs.append(weight_grad_of(grads, acts[q], ups[q], downs[q]))
                right = along_line(right, 1, lambda p: p < line - 1)
                left = along_line(left, -1, lambda p: p > 0)
                moving[q] = right, left
        for q in range(STREAMS):
            right, left = moving[q]
            total = part(0, q) + right.astype(f32) + left.astype(f32)
            own_h.append(total[:tokens])
            give = total[tokens:].astype(bf16)
            other_h.append(across_side(give).astype(f32))
        act_grad = (
            place(jnp.concatenate(own_h, axis=1), jnp.concatenate(other_h, axis=1), side, 1)
            * slope
        )
        own = jnp.concatenate([o[0] for o in outs], axis=1)
        other = jnp.concatenate([o[1].astype(f32) for o in outs], axis=1)
        weight_grad = place(own, other, side, 1)

        qkv, _ = lax.optimization_barrier((qkv, products[0, 0]))
        context = attend(qkv, segment_ids[0].reshape(-1))
        partial = lax.dot_general(
            context, out_weight, (((1,), (1,)), ((), ())), preferred_element_type=f32
        ).astype(bf16)
        share = partial.shape[0] // n_tensor
        total = lax.dynamic_slice(partial, (t * share, 0), (share, d_model)).astype(f32)
        for k in range(1, n_tensor):
            rows = lax.dynamic_slice(
                partial, (((t + k) % n_tensor) * share, 0), (share, d_model)
            )
            pairs = [(i, (i + k) % n_tensor) for i in range(n_tensor)]
            total = total + lax.ppermute(rows, "tensor", pairs).astype(f32)
        attention_out = total + out_bias.astype(f32)
        return (attention_out, act_grad, weight_grad)

    return body


def solution(mesh):
    n_dp, n_tensor = mesh.shape["dp"], mesh.shape["tensor"]
    return jax.shard_map(
        make_body(n_dp, n_tensor),
        mesh=mesh,
        in_specs=(
            P(None, "dp", "tensor"),
            P("dp", None, None),
            P(None, "tensor"),
            P(),
            P(("dp", "tensor"), None),
            P("dp", "tensor"),
            P("dp", "tensor"),
        ),
        out_specs=(P(("dp", "tensor"), None), P("dp", "tensor"), P("dp", "tensor")),
        check_vma=False,
    )
```

time: 216 us -> 221 us (1.023)
  waiting for transfers between devices: 87.2 us -> 74.2 us
  other arithmetic: 17.7 us -> 29.9 us
  local copies, waits for them, and re-layouts: 14.3 us -> 19.5 us
    ppermute x27 -> x19, waiting for transfers between devices: 61.6 us -> 26.9 us  [along_line(): return lax.ppermute(value, 'dp', pairs)]
    ppermute x9 -> x10, waiting for transfers between devices: 12.9 us -> 35.6 us  [across_side(): return lax.ppermute(value, 'dp', [(i, i ^ 1) for i in range(n_dp)])]
    select_n x3 -> x4, other arithmetic: 1.59 us -> 5.15 us  [place(): first = jnp.where(index == 0, own, other)]
    another operation x12, other arithmetic: 3.4 us -> 6.91 us  [the longest x6 3.52 us: gather_grad(): grad = jnp.stack(placed, axis=2)]
    convert_element_type x5 -> x6, other arithmetic: 1.65 us -> 4.74 us  [body(): right, left = (right.astype(bf16), left.astype(bf16))]
    optimization_barrier x0 -> x1, local copies, waits for them, and re-layouts: none -> 2.64 us  [body(): qkv, _ = lax.optimization_barrier((qkv, products[0, 0]))]
    unnamed x17 -> x57, local copies, waits for them, and re-layouts: 5.37 us -> 6.86 us
    ppermute x27 -> x19, starting transfers between devices: 52.4 us -> 53.4 us  [along_line(): return lax.ppermute(value, 'dp', pairs)]
  transfers between devices with their start and end apart: 43 -> 36, of which waited for: 17 -> 13; matrix products, arithmetic and copies ran while one was open for 18% -> 31% of each run, Pallas kernels for 0% -> 0%
where the time goes in v1:
time: 221 us; the launch traced here: 219 us
  waiting for transfers between devices  74.2 us (34%)
  starting transfers between devices  70.3 us (32%)
  other arithmetic  29.9 us (14%)
  matrix products  23.8 us (11%)
  local copies, waits for them, and re-layouts  19.5 us (9%)
    ppermute x19, starting transfers between devices, along_line(): return lax.ppermute(value, 'dp', pairs)  53.4 us
    ppermute x10, waiting for transfers between devices, across_side(): return lax.ppermute(value, 'dp', [(i, i ^ 1) for i in range(n_dp)])  35.6 us
    ppermute x19, waiting for transfers between devices, along_line(): return lax.ppermute(value, 'dp', pairs)  26.9 us
    ppermute x2, waiting for transfers between devices, along_cross(): lax.ppermute(value, 'tensor', [(t, (t + 2 * shift) % n_tensor) for t in r...  11.6 us
    ppermute x10, starting transfers between devices, across_side(): return lax.ppermute(value, 'dp', [(i, i ^ 1) for i in range(n_dp)])  11.5 us
    unnamed x57, local copies, waits for them, and re-layouts  6.86 us
    dot_general x4, matrix products, multiply(): lax.dot_general(grads[g], weights[q], (((2,), (0,)), ((), ())), preferred...  6.27 us
    dot_general x4, matrix products, weight_grad_of(): lax.dot_general(grads[g].reshape(-1, d_line), chunk, (((0,), (0,)), ((),...  6.24 us
  transfers between devices with their start and end apart: 36, of which 13 were waited for; matrix products, arithmetic and copies ran while one was open for 31% of the time, Pallas kernels for 0%

profile of v1, /device:TPU:0, one launch (start us, length us, event | category | flops | bytes accessed | tf_op | source)
XLA Modules:
  0.0 219.4 jit_solution(6566706390666059577)
XLA Ops:
  0.7 1.1 constant_dynamic-slice_fusion.6
  1.9 5.1 %collective-permute-start.1 = (bf16[64,1024]{1,0:T(8,128)(2,1)S(1)}, bf16[64,1024]{1,0:T(8,128)(2,1)S(1)}, u32[]{:S(2)}, u32[]{:S(2)}) collective-permute-start(bf16[64,1024]{1,0:T(8,128)(2,1)S(1)} %get-tuple-element.67), channel_id=1, source_target_pairs={{0,24},{4,28},{8,0},{12,4},{16,8},{20,12},{24,16},{28,20},{1,25},{... | collective-permute-start | bytes 393224 | tf_op jit(solution)/shard_map/ppermute | solution.py:62
  7.0 3.0 %constant_dynamic-slice_fusion.10 = (bf16[512,512]{1,0:T(8,128)(2,1)}, bf16[512,512]{1,0:T(8,128)(2,1)}, bf16[512,512]{1,0:T(8,128)(2,1)}, bf16[512,512]{1,0:T(8,128)(2,1)}) fusion(bf16[512,2048]{1,0:T(8,128)(2,1)} %param.13, s32[]{:T(128)S(6)} %select_n.422, s32[]{:T(128)S(6)} %select_n.420, s32[]{:T(128)S(6)} %select_n.419, s32[]{:T(128)S(6)} %select_n.421), kind=kLoop, calls=%fused_computation.146 | loop fusion | bytes 4194320 | tf_op jit(solution)/shard_map/dynamic_slice | solution.py:161
  10.0 1.5 collective-permute-start.5
  13.8 1.6 collective-permute-start.2
  16.5 23.9 %collective-permute-done.2 = bf16[2,64,1024]{2,1,0:T(8,128)(2,1)S(1)} collective-permute-done((bf16[2,64,1024]{2,1,0:T(8,128)(2,1)S(1)}, bf16[2,64,1024]{2,1,0:T(8,128)(2,1)S(1)}, u32[]{:S(2)}, u32[]{:S(2)}) %collective-permute-start.2) | collective-permute-done | bytes 262176 | tf_op jit(solution)/shard_map/ppermute | solution.py:65
  41.5 1.5 collective-permute-start.3
  44.0 1.5 collective-permute-start.23
  46.5 7.7 %collective-permute-done.3 = bf16[2,2,64,1024]{3,2,1,0:T(8,128)(2,1)S(1)} collective-permute-done((bf16[2,2,64,1024]{3,2,1,0:T(8,128)(2,1)}, bf16[2,2,64,1024]{3,2,1,0:T(8,128)(2,1)S(1)}, u32[]{:S(2)}, u32[]{:S(2)}) %collective-permute-start.3) | collective-permute-done | bytes 524320 | tf_op jit(solution)/shard_map/ppermute | solution.py:71
  54.2 1.5 collective-permute-start.10
  55.7 1.1 pad_maximum_fusion.4
  57.0 1.8 pad_maximum_fusion.11
  58.8 2.1 collective-permute-start.24
  61.0 1.8 pad_maximum_fusion.10
  62.8 1.4 collective-permute-start.28
  64.3 1.6 collective-permute-start.11
  67.0 5.5 %collective-permute-start.14 = (bf16[512,512]{1,0:T(8,128)(2,1)}, bf16[512,512]{1,0:T(8,128)(2,1)}, u32[]{:S(2)}, u32[]{:S(2)}) collective-permute-start(bf16[512,512]{1,0:T(8,128)(2,1)} %pad_maximum_fusion.10), channel_id=1, source_target_pairs={{0,8},{4,12},{8,16},{12,20},{16,24},{20,28},{1,9},{5,13},{9,17},{1... | collective-permute-start | bytes 1572872 | tf_op jit(solution)/shard_map/ppermute | solution.py:62
  72.5 2.2 broadcast_select_fusion.7
  74.7 3.9 %collective-permute-done.11 = bf16[2,2,64,1024]{3,2,1,0:T(8,128)(2,1)S(1)} collective-permute-done((bf16[2,2,64,1024]{3,2,1,0:T(8,128)(2,1)S(1)}, bf16[2,2,64,1024]{3,2,1,0:T(8,128)(2,1)S(1)}, u32[]{:S(2)}, u32[]{:S(2)}) %collective-permute-start.11) | collective-permute-done | bytes 524320 | tf_op jit(solution)/shard_map/ppermute | solution.py:71
  78.6 1.3 collective-permute-start.18
  81.6 2.5 %fusion.49 = f32[2,512,512]{2,1,0:T(8,128)} fusion(bf16[2,512,1024]{2,1,0:T(8,128)(2,1)S(1)} %bitcast.198, bf16[512,512]{1,0:T(8,128)(2,1)S(1)} %get-tuple-element.63, bf16[512,512]{1,0:T(8,128)(2,1)S(1)} %get-tuple-element.62), kind=kOutput, calls=%fused_computation.93 | convolution fusion | flops 1075838976 | bytes 5242880 | tf_op jit(solution)/shard_map/dot_general | solution.py:171
  84.1 2.6 %copy.20 = bf16[3,256,1024]{1,2,0:T(8,128)(2,1)} copy(bf16[3,256,1024]{2,1,0:T(8,128)(2,1)} %param.7) | data formatting | bytes 3145728 | tf_op jit(solution)/shard_map/optimization_barrier | solution.py:219
  87.8 2.2 %fusion.66 = (bf16[1,256,1024]{1,2,0:T(8,128)(2,1)}, bf16[1,256,1024]{1,2,0:T(8,128)(2,1)}) fusion(bf16[3,256,1024]{1,2,0:T(8,128)(2,1)} %copy.20), kind=kLoop, calls=%fused_computation.170 | loop fusion | bytes 2097152 | tf_op jit(solution)/shard_map/slice | solution.py:33
  90.0 3.6 %fusion.67 = (f32[8,256]{1,0:T(8,128)S(1)}, f32[8,256,256]{1,2,0:T(8,128)}) fusion(pred[256,256]{0,1:T(8,128)(4,1)S(1)} %compare_and_fusion, bf16[256,8,128]{0,2,1:T(8,128)(2,1)} %bitcast.208, bf16[256,8,128]{0,2,1:T(8,128)(2,1)} %bitcast.207), kind=kOutput, calls=%fused_computation.171 | convolution fusion | flops 136839424 | bytes 3219456 | tf_op jit(solution)/shard_map/sub | solution.py:44
  93.6 1.9 convolution_convert_fusion.1
  95.5 5.8 %convolution_convert_fusion = bf16[256,4096]{1,0:T(8,128)(2,1)S(1)} fusion(bf16[256,1024]{0,1:T(8,128)(2,1)S(1)} %bitcast.212, bf16[4096,1024]{1,0:T(8,128)(2,1)} %param.9), kind=kOutput, calls=%fused_computation.1 | convolution fusion | flops 2148532224 | bytes 11010048 | tf_op jit(solution)/shard_map/dot_general | solution.py:221
  101.5 1.8 collective-permute-start.8
  103.3 1.4 select_bitcast_fusion.3
  104.7 1.3 select_bitcast_fusion.2
  107.5 1.2 fusion.47
  109.1 1.2 fusion.46
  110.4 1.8 fusion.36
  112.1 4.9 %collective-permute-start.25 = (bf16[512,512]{1,0:T(8,128)(2,1)S(1)}, bf16[512,512]{1,0:T(8,128)(2,1)S(1)}, u32[]{:S(2)}, u32[]{:S(2)}) collective-permute-start(bf16[512,512]{1,0:T(8,128)(2,1)S(1)} %get-tuple-element.35), channel_id=1, source_target_pairs={{0,8},{4,12},{8,16},{12,20},{16,24},{20,28},{1,9},{5,13},{9,17},{1... | collective-permute-start | bytes 1572872 | tf_op jit(solution)/shard_map/ppermute | solution.py:62
  117.1 1.4 collective-permute-start.29
  118.6 1.6 fusion.42
  120.2 4.7 %collective-permute-start.15 = (bf16[512,512]{1,0:T(8,128)(2,1)S(1)}, bf16[512,512]{1,0:T(8,128)(2,1)S(1)}, u32[]{:S(2)}, u32[]{:S(2)}) collective-permute-start(bf16[512,512]{1,0:T(8,128)(2,1)S(1)} %get-tuple-element.29), channel_id=1, source_target_pairs={{0,8},{4,12},{8,16},{12,20},{16,24},{20,28},{1,9},{5,13},{9,17},{1... | collective-permute-start | bytes 1572872 | tf_op jit(solution)/shard_map/ppermute | solution.py:62
  124.9 1.3 collective-permute-start.19
  126.2 1.2 fusion.48
  127.5 1.8 collective-permute-done.25
  129.9 4.2 %collective-permute-done.29 = bf16[512,512]{1,0:T(8,128)(2,1)S(1)} collective-permute-done((bf16[512,512]{1,0:T(8,128)(2,1)S(1)}, bf16[512,512]{1,0:T(8,128)(2,1)S(1)}, u32[]{:S(2)}, u32[]{:S(2)}) %collective-permute-start.29) | collective-permute-done | bytes 524320 | tf_op jit(solution)/shard_map/ppermute | solution.py:62
  134.4 4.8 %collective-permute-done.15 = bf16[512,512]{1,0:T(8,128)(2,1)S(1)} collective-permute-done((bf16[512,512]{1,0:T(8,128)(2,1)S(1)}, bf16[512,512]{1,0:T(8,128)(2,1)S(1)}, u32[]{:S(2)}, u32[]{:S(2)}) %collective-permute-start.15) | collective-permute-done | bytes 524320 | tf_op jit(solution)/shard_map/ppermute | solution.py:62
  139.2 4.4 %collective-permute-start.26 = (bf16[512,512]{1,0:T(8,128)(2,1)S(1)}, bf16[512,512]{1,0:T(8,128)(2,1)S(1)}, u32[]{:S(2)}, u32[]{:S(2)}) collective-permute-start(bf16[512,512]{1,0:T(8,128)(2,1)S(1)} %get-tuple-element.33), channel_id=1, source_target_pairs={{0,8},{4,12},{8,16},{12,20},{16,24},{20,28},{1,9},{5,13},{9,17},{1... | collective-permute-start | bytes 1572872 | tf_op jit(solution)/shard_map/ppermute | solution.py:62
  143.9 1.4 collective-permute-start.30
  145.7 2.3 %fusion.25 = f32[1024,512]{0,1:T(8,128)S(1)} fusion(bf16[1024,1024]{1,0:T(8,128)(2,1)S(1)} %bitcast.204, bf16[256,512]{1,0:T(8,128)(2,1)} %collective-permute-done.23, bf16[256,512]{1,0:T(8,128)(2,1)S(1)} %copy-done.15, bf16[512,512]{1,0:T(8,128)(2,1)S(1)} %broadcast_select_fusion), kind=kOutput, calls=%fused_computation.53 | convolution fusion | flops 1076887552 | bytes 5242880 | tf_op jit(solution)/shard_map/dot_general | solution.py:101
  148.0 5.4 %collective-permute-start.16 = (bf16[512,512]{1,0:T(8,128)(2,1)S(1)}, bf16[512,512]{1,0:T(8,128)(2,1)S(1)}, u32[]{:S(2)}, u32[]{:S(2)}) collective-permute-start(bf16[512,512]{1,0:T(8,128)(2,1)S(1)} %get-tuple-element.27), channel_id=1, source_target_pairs={{0,8},{4,12},{8,16},{12,20},{16,24},{20,28},{1,9},{5,13},{9,17},{1... | collective-permute-start | bytes 1572872 | tf_op jit(solution)/shard_map/ppermute | solution.py:62
  153.3 1.4 collective-permute-start.20
  154.8 1.3 add_add_fusion
  156.1 1.3 fusion.16
  157.5 4.0 %collective-permute-done.30 = bf16[512,512]{1,0:T(8,128)(2,1)S(1)} collective-permute-done((bf16[512,512]{1,0:T(8,128)(2,1)S(1)}, bf16[512,512]{1,0:T(8,128)(2,1)S(1)}, u32[]{:S(2)}, u32[]{:S(2)}) %collective-permute-start.30) | collective-permute-done | bytes 524320 | tf_op jit(solution)/shard_map/ppermute | solution.py:62
  161.8 1.3 collective-permute-start.31
  163.1 4.6 %collective-permute-start.27 = (bf16[512,512]{1,0:T(8,128)(2,1)S(1)}, bf16[512,512]{1,0:T(8,128)(2,1)S(1)}, u32[]{:S(2)}, u32[]{:S(2)}) collective-permute-start(bf16[512,512]{1,0:T(8,128)(2,1)S(1)} %get-tuple-element.31), channel_id=1, source_target_pairs={{0,8},{4,12},{8,16},{12,20},{16,24},{20,28},{1,9},{5,13},{9,17},{1... | collective-permute-start | bytes 1572872 | tf_op jit(solution)/shard_map/ppermute | solution.py:62
  167.7 5.0 %collective-permute-done.20 = bf16[512,512]{1,0:T(8,128)(2,1)S(1)} collective-permute-done((bf16[512,512]{1,0:T(8,128)(2,1)S(1)}, bf16[512,512]{1,0:T(8,128)(2,1)S(1)}, u32[]{:S(2)}, u32[]{:S(2)}) %collective-permute-start.20) | collective-permute-done | bytes 524320 | tf_op jit(solution)/shard_map/ppermute | solution.py:62
  173.1 1.3 collective-permute-start.21
  174.4 4.8 %collective-permute-start.17 = (bf16[512,512]{1,0:T(8,128)(2,1)S(1)}, bf16[512,512]{1,0:T(8,128)(2,1)S(1)}, u32[]{:S(2)}, u32[]{:S(2)}) collective-permute-start(bf16[512,512]{1,0:T(8,128)(2,1)S(1)} %get-tuple-element.25), channel_id=1, source_target_pairs={{0,8},{4,12},{8,16},{12,20},{16,24},{20,28},{1,9},{5,13},{9,17},{1... | collective-permute-start | bytes 1572872 | tf_op jit(solution)/shard_map/ppermute | solution.py:62
  180.4 1.3 add_multiply_fusion
  183.6 1.3 add_multiply_fusion.1
  185.3 1.6 collective-permute-start.34
  187.1 6.1 %collective-permute-done.21 = bf16[512,512]{1,0:T(8,128)(2,1)S(1)} collective-permute-done((bf16[512,512]{1,0:T(8,128)(2,1)S(1)}, bf16[512,512]{1,0:T(8,128)(2,1)S(1)}, u32[]{:S(2)}, u32[]{:S(2)}) %collective-permute-start.21) | collective-permute-done | bytes 524320 | tf_op jit(solution)/shard_map/ppermute | solution.py:62
  194.7 1.5 collective-permute-start.32
  196.7 11.2 %collective-permute-done.34 = bf16[512,512]{0,1:T(8,128)(2,1)S(1)} collective-permute-done((bf16[512,512]{0,1:T(8,128)(2,1)S(1)}, bf16[512,512]{0,1:T(8,128)(2,1)S(1)}, u32[]{:S(2)}, u32[]{:S(2)}) %collective-permute-start.34) | collective-permute-done | bytes 524320 | tf_op jit(solution)/shard_map/ppermute | solution.py:65
  208.5 2.5 %pad_maximum_fusion = f32[512,2048]{0,1:T(8,128)} fusion(f32[512,1024]{0,1:T(8,128)S(1)} %get-tuple-element.24, f32[512,1024]{0,1:T(8,128)S(1)} %get-tuple-element.23), kind=kLoop, calls=%fused_computation.2 | loop fusion | flops 1048576 | bytes 8388608 | tf_op jit(solution)/shard_map/concatenate | solution.py:78
  211.0 5.4 %copy.28 = f32[512,2048]{1,0:T(8,128)} copy(f32[512,2048]{0,1:T(8,128)} %pad_maximum_fusion) | data formatting | bytes 8388608
  216.4 1.3 convert_select_fusion.3
  217.7 1.7 maximum_multiply_fusion
  (135 shorter events, 20.5 us)
Async XLA Ops:
  1.9 11.1 %collective-permute-start.1 = (bf16[64,1024]{1,0:T(8,128)(2,1)S(1)}, bf16[64,1024]{1,0:T(8,128)(2,1)S(1)}, u32[]{:S(2)}, u32[]{:S(2)}) collective-permute-start(bf16[64,1024]{1,0:T(8,128)(2,1)S(1)} %get-tuple-element.67), channel_id=1, source_target_pairs={{0,24},{4,28},{8,0},{12,4},{16,8},{20,12},{24,16},{28,20},{1,25},{... | collective-permute-start | bytes 393224 | tf_op jit(solution)/shard_map/ppermute | solution.py:62
  7.0 6.8 %collective-permute-start = (bf16[64,1024]{1,0:T(8,128)(2,1)S(1)}, bf16[64,1024]{1,0:T(8,128)(2,1)S(1)}, u32[]{:S(2)}, u32[]{:S(2)}) collective-permute-start(bf16[64,1024]{1,0:T(8,128)(2,1)S(1)} %get-tuple-element.68), channel_id=1, source_target_pairs={{0,8},{4,12},{8,16},{12,20},{16,24},{20,28},{24,0},{28,4},{1,9},{5... | collective-permute-start | bytes 393224 | tf_op jit(solution)/shard_map/ppermute | solution.py:62
  7.0 8.4 %copy-start.16 = (bf16[256,2048]{1,0:T(8,128)(2,1)S(1)}, bf16[256,2048]{1,0:T(8,128)(2,1)}, u32[]{:S(2)}) copy-start(bf16[256,2048]{1,0:T(8,128)(2,1)} %param.12) | copy-start | bytes 3145732
  10.0 54.3 %collective-permute-start.5 = (bf16[512,512]{1,0:T(8,128)(2,1)}, bf16[512,512]{1,0:T(8,128)(2,1)}, u32[]{:S(2)}, u32[]{:S(2)}) collective-permute-start(bf16[512,512]{1,0:T(8,128)(2,1)} %get-tuple-element.11), channel_id=1, source_target_pairs={{0,4},{4,0},{8,12},{12,8},{16,20},{20,16},{24,28},{28,24},{1,5},{5... | collective-permute-start | bytes 1572872 | tf_op jit(solution)/shard_map/ppermute | solution.py:65
  11.5 34.4 %collective-permute-start.9 = (bf16[64,1024]{1,0:T(8,128)(2,1)S(1)}, bf16[64,1024]{1,0:T(8,128)(2,1)S(1)}, u32[]{:S(2)}, u32[]{:S(2)}) collective-permute-start(bf16[64,1024]{1,0:T(8,128)(2,1)S(1)} %get-tuple-element.66), channel_id=1, source_target_pairs={{0,16},{4,20},{8,24},{12,28},{16,0},{20,4},{24,8},{28,12},{1,17},{... | collective-permute-start | bytes 393224 | tf_op jit(solution)/shard_map/ppermute | solution.py:62
  12.5 54.5 %collective-permute-start.22 = (bf16[512,512]{1,0:T(8,128)(2,1)}, bf16[512,512]{1,0:T(8,128)(2,1)}, u32[]{:S(2)}, u32[]{:S(2)}) collective-permute-start(bf16[512,512]{1,0:T(8,128)(2,1)} %get-tuple-element.15), channel_id=1, source_target_pairs={{0,4},{4,0},{8,12},{12,8},{16,20},{20,16},{24,28},{28,24},{1,5},{5... | collective-permute-start | bytes 1572872 | tf_op jit(solution)/shard_map/ppermute | solution.py:65
  13.8 26.6 %collective-permute-start.2 = (bf16[2,64,1024]{2,1,0:T(8,128)(2,1)S(1)}, bf16[2,64,1024]{2,1,0:T(8,128)(2,1)S(1)}, u32[]{:S(2)}, u32[]{:S(2)}) collective-permute-start(bf16[2,64,1024]{2,1,0:T(8,128)(2,1)S(1)} %get-tuple-element.75), channel_id=1, source_target_pairs={{0,4},{4,0},{8,12},{12,8},{16,20},{20,16},{24,28},{28,24},{1,5},{5... | collective-permute-start | bytes 786440 | tf_op jit(solution)/shard_map/ppermute | solution.py:65
  16.5 29.0 %copy-start.27 = (s32[1,4,64]{2,1,0:T(4,128)S(1)}, s32[1,4,64]{2,1,0:T(4,128)}, u32[]{:S(2)}) copy-start(s32[1,4,64]{2,1,0:T(4,128)} %param.8) | copy-start | bytes 3076
  16.5 29.3 %copy-start.26 = (bf16[4096]{0:T(1024)(128)(2,1)S(1)}, bf16[4096]{0:T(1024)(128)(2,1)}, u32[]{:S(2)}) copy-start(bf16[4096]{0:T(1024)(128)(2,1)} %param.10) | copy-start | bytes 24580
  40.4 3.5 %copy-start.5 = (bf16[2,64,1024]{2,1,0:T(8,128)(2,1)}, bf16[2,64,1024]{2,1,0:T(8,128)(2,1)S(1)}, u32[]{:S(2)}) copy-start(bf16[2,64,1024]{2,1,0:T(8,128)(2,1)S(1)} %collective-permute-done.2) | copy-start | bytes 786436
  41.5 12.7 %collective-permute-start.3 = (bf16[2,2,64,1024]{3,2,1,0:T(8,128)(2,1)}, bf16[2,2,64,1024]{3,2,1,0:T(8,128)(2,1)S(1)}, u32[]{:S(2)}, u32[]{:S(2)}) collective-permute-start(bf16[2,2,64,1024]{3,2,1,0:T(8,128)(2,1)} %get-tuple-element.71), channel_id=1, source_target_pairs={{0,2},{1,3},{2,0},{3,1},{4,6},{5,7},{6,4},{7,5},{8,10},{9,11},{10,... | collective-permute-start | bytes 1572872 | tf_op jit(solution)/shard_map/ppermute | solution.py:71
  44.0 12.9 %collective-permute-start.23 = (bf16[256,512]{1,0:T(8,128)(2,1)}, bf16[256,512]{1,0:T(8,128)(2,1)}, u32[]{:S(2)}, u32[]{:S(2)}) collective-permute-start(bf16[256,512]{1,0:T(8,128)(2,1)} %get-tuple-element.55), channel_id=1, source_target_pairs={{0,4},{4,0},{8,12},{12,8},{16,20},{20,16},{24,28},{28,24},{1,5},{5... | collective-permute-start | bytes 786440 | tf_op jit(solution)/shard_map/ppermute | solution.py:65
  45.9 11.1 %copy-start.14 = (bf16[256,512]{1,0:T(8,128)(2,1)S(1)}, bf16[256,512]{1,0:T(8,128)(2,1)}, u32[]{:S(2)}) copy-start(bf16[256,512]{1,0:T(8,128)(2,1)} %get-tuple-element.56) | copy-start | bytes 786436
  45.9 13.0 %collective-permute-start.13 = (bf16[256,512]{1,0:T(8,128)(2,1)}, bf16[256,512]{1,0:T(8,128)(2,1)S(1)}, u32[]{:S(2)}, u32[]{:S(2)}) collective-permute-start(bf16[256,512]{1,0:T(8,128)(2,1)} %get-tuple-element.57), channel_id=1, source_target_pairs={{0,4},{4,0},{8,12},{12,8},{16,20},{20,16},{24,28},{28,24},{1,5},{5... | collective-permute-start | bytes 786440 | tf_op jit(solution)/shard_map/ppermute | solution.py:65
  46.5 17.7 %copy-start.1 = (bf16[2,1,64,1024]{3,2,1,0:T(8,128)(2,1)}, bf16[2,1,64,1024]{3,2,1,0:T(8,128)(2,1)S(1)}, u32[]{:S(2)}) copy-start(bf16[2,1,64,1024]{3,2,1,0:T(8,128)(2,1)S(1)} %get-tuple-element.72) | copy-start | bytes 786436
  54.2 8.6 %collective-permute-start.10 = (bf16[2,64,1024]{2,1,0:T(8,128)(2,1)S(1)}, bf16[2,64,1024]{2,1,0:T(8,128)(2,1)S(1)}, u32[]{:S(2)}, u32[]{:S(2)}) collective-permute-start(bf16[2,64,1024]{2,1,0:T(8,128)(2,1)S(1)} %get-tuple-element.73), channel_id=1, source_target_pairs={{0,4},{4,0},{8,12},{12,8},{16,20},{20,16},{24,28},{28,24},{1,5},{5... | collective-permute-start | bytes 786440 | tf_op jit(solution)/shard_map/ppermute | solution.py:65
  56.9 9.0 %copy-start.12 = (bf16[512,512]{1,0:T(8,128)(2,1)S(1)}, bf16[512,512]{1,0:T(8,128)(2,1)}, u32[]{:S(2)}) copy-start(bf16[512,512]{1,0:T(8,128)(2,1)} %get-tuple-element.10) | copy-start | bytes 1572868
  56.9 24.1 %collective-permute-start.4 = (bf16[2,2,2,64,1024]{4,3,2,1,0:T(8,128)(2,1)S(1)}, bf16[2,2,2,64,1024]{4,3,2,1,0:T(8,128)(2,1)S(1)}, u32[]{:S(2)}, u32[]{:S(2)}) collective-permute-start(bf16[2,2,2,64,1024]{4,3,2,1,0:T(8,128)(2,1)S(1)} %pad_maximum_fusion.4), channel_id=1, source_target_pairs={{0,1},{1,0},{2,3},{3,2},{4,5},{5,4},{6,7},{7,6},{8,9},{9,8},{10,11... | collective-permute-start | bytes 3145736 | tf_op jit(solution)/shard_map/ppermute | solution.py:68
  58.8 5.4 %copy-start.24 = (bf16[256,512]{1,0:T(8,128)(2,1)}, bf16[256,512]{1,0:T(8,128)(2,1)S(1)}, u32[]{:S(2)}) copy-start(bf16[256,512]{1,0:T(8,128)(2,1)S(1)} %collective-permute-done.13) | copy-start | bytes 786436
  58.8 51.5 %collective-permute-start.24 = (bf16[512,512]{1,0:T(8,128)(2,1)}, bf16[512,512]{1,0:T(8,128)(2,1)}, u32[]{:S(2)}, u32[]{:S(2)}) collective-permute-start(bf16[512,512]{1,0:T(8,128)(2,1)} %pad_maximum_fusion.11), channel_id=1, source_target_pairs={{0,8},{4,12},{8,16},{12,20},{16,24},{20,28},{1,9},{5,13},{9,17},{1... | collective-permute-start | bytes 1572872 | tf_op jit(solution)/shard_map/ppermute | solution.py:62
  62.8 9.8 %copy-start.11 = (bf16[512,512]{1,0:T(8,128)(2,1)S(1)}, bf16[512,512]{1,0:T(8,128)(2,1)}, u32[]{:S(2)}) copy-start(bf16[512,512]{1,0:T(8,128)(2,1)} %get-tuple-element.14) | copy-start | bytes 1572868
  62.8 47.6 %collective-permute-start.28 = (bf16[512,512]{1,0:T(8,128)(2,1)}, bf16[512,512]{1,0:T(8,128)(2,1)}, u32[]{:S(2)}, u32[]{:S(2)}) collective-permute-start(bf16[512,512]{1,0:T(8,128)(2,1)} %pad_maximum_fusion.11), channel_id=1, source_target_pairs={{8,0},{12,4},{16,8},{20,12},{24,16},{28,20},{9,1},{13,5},{17,9},{2... | collective-permute-start | bytes 1572872 | tf_op jit(solution)/shard_map/ppermute | solution.py:62
  64.3 14.3 %collective-permute-start.11 = (bf16[2,2,64,1024]{3,2,1,0:T(8,128)(2,1)S(1)}, bf16[2,2,64,1024]{3,2,1,0:T(8,128)(2,1)S(1)}, u32[]{:S(2)}, u32[]{:S(2)}) collective-permute-start(bf16[2,2,64,1024]{3,2,1,0:T(8,128)(2,1)S(1)} %get-tuple-element.65), channel_id=1, source_target_pairs={{0,2},{1,3},{2,0},{3,1},{4,6},{5,7},{6,4},{7,5},{8,10},{9,11},{10,... | collective-permute-start | bytes 1572872 | tf_op jit(solution)/shard_map/ppermute | solution.py:71
  67.0 14.6 %copy-start.17 = (bf16[512,512]{1,0:T(8,128)(2,1)}, bf16[512,512]{1,0:T(8,128)(2,1)S(1)}, u32[]{:S(2)}) copy-start(bf16[512,512]{1,0:T(8,128)(2,1)S(1)} %get-tuple-element.62) | copy-start | bytes 1572868
  67.0 14.6 %copy-start.19 = (bf16[512,512]{1,0:T(8,128)(2,1)}, bf16[512,512]{1,0:T(8,128)(2,1)S(1)}, u32[]{:S(2)}) copy-start(bf16[512,512]{1,0:T(8,128)(2,1)S(1)} %get-tuple-element.63) | copy-start | bytes 1572868
  67.0 14.0 %copy-start.6 = (bf16[2,64,1024]{2,1,0:T(8,128)(2,1)S(1)}, bf16[2,64,1024]{2,1,0:T(8,128)(2,1)}, u32[]{:S(2)}) copy-start(bf16[2,64,1024]{2,1,0:T(8,128)(2,1)} %copy-done.5) | copy-start | bytes 786436
  67.0 51.5 %collective-permute-start.14 = (bf16[512,512]{1,0:T(8,128)(2,1)}, bf16[512,512]{1,0:T(8,128)(2,1)}, u32[]{:S(2)}, u32[]{:S(2)}) collective-permute-start(bf16[512,512]{1,0:T(8,128)(2,1)} %pad_maximum_fusion.10), channel_id=1, source_target_pairs={{0,8},{4,12},{8,16},{12,20},{16,24},{20,28},{1,9},{5,13},{9,17},{1... | collective-permute-start | bytes 1572872 | tf_op jit(solution)/shard_map/ppermute | solution.py:62
  78.6 39.9 %collective-permute-start.18 = (bf16[512,512]{1,0:T(8,128)(2,1)}, bf16[512,512]{1,0:T(8,128)(2,1)}, u32[]{:S(2)}, u32[]{:S(2)}) collective-permute-start(bf16[512,512]{1,0:T(8,128)(2,1)} %pad_maximum_fusion.10), channel_id=1, source_target_pairs={{8,0},{12,4},{16,8},{20,12},{24,16},{28,20},{9,1},{13,5},{17,9},{2... | collective-permute-start | bytes 1572872 | tf_op jit(solution)/shard_map/ppermute | solution.py:62
  81.0 20.5 %collective-permute-start.12 = (bf16[2,2,2,64,1024]{4,3,2,1,0:T(8,128)(2,1)}, bf16[2,2,2,64,1024]{4,3,2,1,0:T(8,128)(2,1)}, u32[]{:S(2)}, u32[]{:S(2)}) collective-permute-start(bf16[2,2,2,64,1024]{4,3,2,1,0:T(8,128)(2,1)} %pad_maximum_fusion.5), channel_id=1, source_target_pairs={{0,1},{1,0},{2,3},{3,2},{4,5},{5,4},{6,7},{7,6},{8,9},{9,8},{10,11... | collective-permute-start | bytes 3145736 | tf_op jit(solution)/shard_map/ppermute | solution.py:68
  81.6 2.6 %copy-start.9 = (bf16[2,2,4,64,1024]{4,3,2,1,0:T(8,128)(2,1)}, bf16[2,2,4,64,1024]{4,3,2,1,0:T(8,128)(2,1)S(1)}, u32[]{:S(2)}) copy-start(bf16[2,2,4,64,1024]{4,3,2,1,0:T(8,128)(2,1)S(1)} %pad_maximum_fusion.1) | copy-start | bytes 6291460
  84.1 2.6 %slice-start.2 = ((bf16[3,256,1024]{2,1,0:T(8,128)(2,1)}), bf16[1,256,1024]{2,1,0:T(8,128)(2,1)S(1)}, s32[]{:S(2)}) async-start(bf16[3,256,1024]{2,1,0:T(8,128)(2,1)} %param.7), calls=%async_computation.2 | async-start | bytes 1048576 | tf_op jit(solution)/shard_map/slice | solution.py:34
  90.0 3.6 %copy-start.23 = (bf16[1,256,1024]{1,2,0:T(8,128)(2,1)S(1)}, bf16[1,256,1024]{1,2,0:T(8,128)(2,1)}, u32[]{:S(2)}) copy-start(bf16[1,256,1024]{1,2,0:T(8,128)(2,1)} %copy.19) | copy-start | bytes 1572868
  101.3 2.0 copy-start.2
  101.3 2.0 copy-start.8
  101.5 46.5 %collective-permute-start.8 = (bf16[64,4096]{1,0:T(8,128)(2,1)S(1)}, bf16[64,4096]{1,0:T(8,128)(2,1)S(1)}, u32[]{:S(2)}, u32[]{:S(2)}) collective-permute-start(bf16[64,4096]{1,0:T(8,128)(2,1)S(1)} %get-tuple-element.41), channel_id=1, source_target_pairs={{0,3},{1,0},{2,1},{3,2},{4,7},{5,4},{6,5},{7,6},{8,11},{9,8},{10,9... | collective-permute-start | bytes 1572872 | tf_op jit(solution)/shard_map/ppermute | solution.py:231
  107.5 1.6 copy-start.10
  110.3 8.2 %copy-start = (f32[2,512,512]{2,1,0:T(8,128)S(1)}, f32[2,512,512]{2,1,0:T(8,128)}, u32[]{:S(2)}) copy-start(f32[2,512,512]{2,1,0:T(8,128)} %fusion.49) | copy-start | bytes 6291460
  112.1 17.2 %collective-permute-start.25 = (bf16[512,512]{1,0:T(8,128)(2,1)S(1)}, bf16[512,512]{1,0:T(8,128)(2,1)S(1)}, u32[]{:S(2)}, u32[]{:S(2)}) collective-permute-start(bf16[512,512]{1,0:T(8,128)(2,1)S(1)} %get-tuple-element.35), channel_id=1, source_target_pairs={{0,8},{4,12},{8,16},{12,20},{16,24},{20,28},{1,9},{5,13},{9,17},{1... | collective-permute-start | bytes 1572872 | tf_op jit(solution)/shard_map/ppermute | solution.py:62
  117.1 9.2 %copy-start.18 = (bf16[512,512]{1,0:T(8,128)(2,1)S(1)}, bf16[512,512]{1,0:T(8,128)(2,1)}, u32[]{:S(2)}) copy-start(bf16[512,512]{1,0:T(8,128)(2,1)} %copy-done.17) | copy-start | bytes 1572868
  117.1 9.2 %copy-start.20 = (bf16[512,512]{1,0:T(8,128)(2,1)S(1)}, bf16[512,512]{1,0:T(8,128)(2,1)}, u32[]{:S(2)}) copy-start(bf16[512,512]{1,0:T(8,128)(2,1)} %copy-done.19) | copy-start | bytes 1572868
  117.1 17.0 %collective-permute-start.29 = (bf16[512,512]{1,0:T(8,128)(2,1)S(1)}, bf16[512,512]{1,0:T(8,128)(2,1)S(1)}, u32[]{:S(2)}, u32[]{:S(2)}) collective-permute-start(bf16[512,512]{1,0:T(8,128)(2,1)S(1)} %get-tuple-element.36), channel_id=1, source_target_pairs={{8,0},{12,4},{16,8},{20,12},{24,16},{28,20},{9,1},{13,5},{17,9},{2... | collective-permute-start | bytes 1572872 | tf_op jit(solution)/shard_map/ppermute | solution.py:62
  120.2 19.0 %collective-permute-start.15 = (bf16[512,512]{1,0:T(8,128)(2,1)S(1)}, bf16[512,512]{1,0:T(8,128)(2,1)S(1)}, u32[]{:S(2)}, u32[]{:S(2)}) collective-permute-start(bf16[512,512]{1,0:T(8,128)(2,1)S(1)} %get-tuple-element.29), channel_id=1, source_target_pairs={{0,8},{4,12},{8,16},{12,20},{16,24},{20,28},{1,9},{5,13},{9,17},{1... | collective-permute-start | bytes 1572872 | tf_op jit(solution)/shard_map/ppermute | solution.py:62
  124.9 19.0 %collective-permute-start.19 = (bf16[512,512]{1,0:T(8,128)(2,1)S(1)}, bf16[512,512]{1,0:T(8,128)(2,1)S(1)}, u32[]{:S(2)}, u32[]{:S(2)}) collective-permute-start(bf16[512,512]{1,0:T(8,128)(2,1)S(1)} %get-tuple-element.30), channel_id=1, source_target_pairs={{8,0},{12,4},{16,8},{20,12},{24,16},{28,20},{9,1},{13,5},{17,9},{2... | collective-permute-start | bytes 1572872 | tf_op jit(solution)/shard_map/ppermute | solution.py:62
  129.3 24.0 %collective-permute-start.7 = (bf16[64,4096]{1,0:T(8,128)(2,1)S(1)}, bf16[64,4096]{1,0:T(8,128)(2,1)S(1)}, u32[]{:S(2)}, u32[]{:S(2)}) collective-permute-start(bf16[64,4096]{1,0:T(8,128)(2,1)S(1)} %get-tuple-element.42), channel_id=1, source_target_pairs={{0,2},{1,3},{2,0},{3,1},{4,6},{5,7},{6,4},{7,5},{8,10},{9,11},{10,... | collective-permute-start | bytes 1572872 | tf_op jit(solution)/shard_map/ppermute | solution.py:231
  134.1 20.7 %collective-permute-start.6 = (bf16[64,4096]{1,0:T(8,128)(2,1)S(1)}, bf16[64,4096]{1,0:T(8,128)(2,1)S(1)}, u32[]{:S(2)}, u32[]{:S(2)}) collective-permute-start(bf16[64,4096]{1,0:T(8,128)(2,1)S(1)} %get-tuple-element.40), channel_id=1, source_target_pairs={{0,1},{1,2},{2,3},{3,0},{4,5},{5,6},{6,7},{7,4},{8,9},{9,10},{10,1... | collective-permute-start | bytes 1572872 | tf_op jit(solution)/shard_map/ppermute | solution.py:231
  139.2 18.3 %collective-permute-start.26 = (bf16[512,512]{1,0:T(8,128)(2,1)S(1)}, bf16[512,512]{1,0:T(8,128)(2,1)S(1)}, u32[]{:S(2)}, u32[]{:S(2)}) collective-permute-start(bf16[512,512]{1,0:T(8,128)(2,1)S(1)} %get-tuple-element.33), channel_id=1, source_target_pairs={{0,8},{4,12},{8,16},{12,20},{16,24},{20,28},{1,9},{5,13},{9,17},{1... | collective-permute-start | bytes 1572872 | tf_op jit(solution)/shard_map/ppermute | solution.py:62
  143.9 1.8 copy-start.15
  143.9 17.6 %collective-permute-start.30 = (bf16[512,512]{1,0:T(8,128)(2,1)S(1)}, bf16[512,512]{1,0:T(8,128)(2,1)S(1)}, u32[]{:S(2)}, u32[]{:S(2)}) collective-permute-start(bf16[512,512]{1,0:T(8,128)(2,1)S(1)} %get-tuple-element.34), channel_id=1, source_target_pairs={{8,0},{12,4},{16,8},{20,12},{24,16},{28,20},{9,1},{13,5},{17,9},{2... | collective-permute-start | bytes 1572872 | tf_op jit(solution)/shard_map/ppermute | solution.py:62
  148.0 19.8 %collective-permute-start.16 = (bf16[512,512]{1,0:T(8,128)(2,1)S(1)}, bf16[512,512]{1,0:T(8,128)(2,1)S(1)}, u32[]{:S(2)}, u32[]{:S(2)}) collective-permute-start(bf16[512,512]{1,0:T(8,128)(2,1)S(1)} %get-tuple-element.27), channel_id=1, source_target_pairs={{0,8},{4,12},{8,16},{12,20},{16,24},{20,28},{1,9},{5,13},{9,17},{1... | collective-permute-start | bytes 1572872 | tf_op jit(solution)/shard_map/ppermute | solution.py:62
  153.3 2.8 %copy-start.13 = (bf16[256,512]{1,0:T(8,128)(2,1)S(1)}, bf16[256,512]{1,0:T(8,128)(2,1)}, u32[]{:S(2)}) copy-start(bf16[256,512]{1,0:T(8,128)(2,1)} %get-tuple-element.54) | copy-start | bytes 786436
  153.3 2.8 %copy-start.25 = (bf16[256,512]{1,0:T(8,128)(2,1)S(1)}, bf16[256,512]{1,0:T(8,128)(2,1)}, u32[]{:S(2)}) copy-start(bf16[256,512]{1,0:T(8,128)(2,1)} %copy-done.24) | copy-start | bytes 786436
  153.3 19.4 %collective-permute-start.20 = (bf16[512,512]{1,0:T(8,128)(2,1)S(1)}, bf16[512,512]{1,0:T(8,128)(2,1)S(1)}, u32[]{:S(2)}, u32[]{:S(2)}) collective-permute-start(bf16[512,512]{1,0:T(8,128)(2,1)S(1)} %get-tuple-element.28), channel_id=1, source_target_pairs={{8,0},{12,4},{16,8},{20,12},{24,16},{28,20},{9,1},{13,5},{17,9},{2... | collective-permute-start | bytes 1572872 | tf_op jit(solution)/shard_map/ppermute | solution.py:62
  161.8 23.4 %collective-permute-start.31 = (bf16[512,512]{1,0:T(8,128)(2,1)S(1)}, bf16[512,512]{1,0:T(8,128)(2,1)S(1)}, u32[]{:S(2)}, u32[]{:S(2)}) collective-permute-start(bf16[512,512]{1,0:T(8,128)(2,1)S(1)} %get-tuple-element.32), channel_id=1, source_target_pairs={{8,0},{12,4},{16,8},{20,12},{24,16},{28,20},{9,1},{13,5},{17,9},{2... | collective-permute-start | bytes 1572872 | tf_op jit(solution)/shard_map/ppermute | solution.py:62
  163.1 23.7 %collective-permute-start.27 = (bf16[512,512]{1,0:T(8,128)(2,1)S(1)}, bf16[512,512]{1,0:T(8,128)(2,1)S(1)}, u32[]{:S(2)}, u32[]{:S(2)}) collective-permute-start(bf16[512,512]{1,0:T(8,128)(2,1)S(1)} %get-tuple-element.31), channel_id=1, source_target_pairs={{0,8},{4,12},{8,16},{12,20},{16,24},{20,28},{1,9},{5,13},{9,17},{1... | collective-permute-start | bytes 1572872 | tf_op jit(solution)/shard_map/ppermute | solution.py:62
  173.1 20.1 %collective-permute-start.21 = (bf16[512,512]{1,0:T(8,128)(2,1)S(1)}, bf16[512,512]{1,0:T(8,128)(2,1)S(1)}, u32[]{:S(2)}, u32[]{:S(2)}) collective-permute-start(bf16[512,512]{1,0:T(8,128)(2,1)S(1)} %get-tuple-element.26), channel_id=1, source_target_pairs={{8,0},{12,4},{16,8},{20,12},{24,16},{28,20},{9,1},{13,5},{17,9},{2... | collective-permute-start | bytes 1572872 | tf_op jit(solution)/shard_map/ppermute | solution.py:62
  174.4 18.8 %collective-permute-start.17 = (bf16[512,512]{1,0:T(8,128)(2,1)S(1)}, bf16[512,512]{1,0:T(8,128)(2,1)S(1)}, u32[]{:S(2)}, u32[]{:S(2)}) collective-permute-start(bf16[512,512]{1,0:T(8,128)(2,1)S(1)} %get-tuple-element.25), channel_id=1, source_target_pairs={{0,8},{4,12},{8,16},{12,20},{16,24},{20,28},{1,9},{5,13},{9,17},{1... | collective-permute-start | bytes 1572872 | tf_op jit(solution)/shard_map/ppermute | solution.py:62
  181.8 14.9 %collective-permute-start.35 = (bf16[512,512]{0,1:T(8,128)(2,1)S(1)}, bf16[512,512]{0,1:T(8,128)(2,1)S(1)}, u32[]{:S(2)}, u32[]{:S(2)}) collective-permute-start(bf16[512,512]{0,1:T(8,128)(2,1)S(1)} %dynamic-slice_convert_fusion), channel_id=1, source_target_pairs={{0,4},{4,0},{8,12},{12,8},{16,20},{20,16},{24,28},{28,24},{1,5},{5... | collective-permute-start | bytes 1572872 | tf_op jit(solution)/shard_map/ppermute | solution.py:65
  185.3 22.7 %collective-permute-start.34 = (bf16[512,512]{0,1:T(8,128)(2,1)S(1)}, bf16[512,512]{0,1:T(8,128)(2,1)S(1)}, u32[]{:S(2)}, u32[]{:S(2)}) collective-permute-start(bf16[512,512]{0,1:T(8,128)(2,1)S(1)} %dynamic-slice_convert_fusion.1), channel_id=1, source_target_pairs={{0,4},{4,0},{8,12},{12,8},{16,20},{20,16},{24,28},{28,24},{1,5},{5... | collective-permute-start | bytes 1572872 | tf_op jit(solution)/shard_map/ppermute | solution.py:65
  187.1 6.4 %copy-start.3 = (f32[512,512]{1,0:T(8,128)}, f32[512,512]{1,0:T(8,128)S(1)}, u32[]{:S(2)}) copy-start(f32[512,512]{1,0:T(8,128)S(1)} %fusion.10) | copy-start | bytes 3145732
  193.4 14.5 %copy-start.4 = (f32[512,512]{1,0:T(8,128)}, f32[512,512]{1,0:T(8,128)S(1)}, u32[]{:S(2)}) copy-start(f32[512,512]{1,0:T(8,128)S(1)} %fusion.12) | copy-start | bytes 3145732
  194.2 22.2 %collective-permute-start.33 = (bf16[256,512]{1,0:T(8,128)(2,1)S(1)}, bf16[256,512]{1,0:T(8,128)(2,1)}, u32[]{:S(2)}, u32[]{:S(2)}) collective-permute-start(bf16[256,512]{1,0:T(8,128)(2,1)S(1)} %slice.190), channel_id=1, source_target_pairs={{0,4},{4,0},{8,12},{12,8},{16,20},{20,16},{24,28},{28,24},{1,5},{5... | collective-permute-start | bytes 786440 | tf_op jit(solution)/shard_map/ppermute | solution.py:65
  194.7 21.7 %collective-permute-start.32 = (bf16[256,512]{1,0:T(8,128)(2,1)}, bf16[256,512]{1,0:T(8,128)(2,1)}, u32[]{:S(2)}, u32[]{:S(2)}) collective-permute-start(bf16[256,512]{1,0:T(8,128)(2,1)} %slice.191), channel_id=1, source_target_pairs={{0,4},{4,0},{8,12},{12,8},{16,20},{20,16},{24,28},{28,24},{1,5},{5... | collective-permute-start | bytes 786440 | tf_op jit(solution)/shard_map/ppermute | solution.py:65
  211.0 5.4 %slice-start = ((f32[512,512]{1,0:T(8,128)}), f32[256,512]{1,0:T(8,128)S(1)}, s32[]{:S(2)}) async-start(f32[512,512]{1,0:T(8,128)} %copy-done.3), calls=%async_computation | async-start | bytes 1048576 | tf_op jit(solution)/shard_map/slice | solution.py:208
  211.0 5.4 %slice-start.1 = ((f32[512,512]{1,0:T(8,128)}), f32[256,512]{1,0:T(8,128)S(1)}, s32[]{:S(2)}) async-start(f32[512,512]{1,0:T(8,128)} %copy-done.4), calls=%async_computation.1 | async-start | bytes 1048576 | tf_op jit(solution)/shard_map/slice | solution.py:208
  (3 other events, 3.8 us)

commit v2 on v1

--- a/solution.py
+++ b/solution.py
@@ -3,6 +3,8 @@
 import jax
 import jax.numpy as jnp
 from jax import lax
+from jax.experimental import pallas as pl
+from jax.experimental.pallas import tpu as pltpu
 from jax.sharding import PartitionSpec as P
 
 
@@ -26,25 +28,147 @@
     )
 
 
-def attend(qkv, labels):
-    length = qkv.shape[1]
-    head_count = qkv.shape[2] // HEAD
-    queries = qkv[0].reshape(length, head_count, HEAD)
-    key_rows = qkv[1].reshape(length, head_count, HEAD)
-    value_rows = qkv[2].reshape(length, head_count, HEAD)
-    scores = jnp.einsum("qhd,khd->hqk", queries, key_rows, preferred_element_type=jnp.float32) * (
-        1.0 / math.sqrt(HEAD)
+def attend_kernel(place_ref, qkv_ref, labels_ref, weight_ref, *refs):
+    outs, (context, rolled) = refs[:-2], refs[-2:]
+    length, width = context.shape
+    share = length // len(outs)
+
+    @pl.when(pl.program_id(0) == 0)
+    def _():
+        row = jnp.broadcast_to(labels_ref[...].astype(f32), (length, length))
+        first = lax.broadcasted_iota(jnp.int32, (length, length), 0) // ROWS_DEV
+        second = lax.broadcasted_iota(jnp.int32, (length, length), 1) // ROWS_DEV
+        same = (row == row.T) & (first == second)
+        for h in range(width // HEAD):
+            cols = slice(h * HEAD, (h + 1) * HEAD)
+            scores = lax.dot_general(
+                qkv_ref[0, :, cols],
+                qkv_ref[1, :, cols],
+                (((1,), (1,)), ((), ())),
+                preferred_element_type=f32,
+            ) * (1.0 / math.sqrt(HEAD))
+            masked = jnp.where(same, scores, -1e30)
+            top = jnp.max(masked, axis=1, keepdims=True)
+            exponent = jnp.where(same, jnp.exp(masked - top), 0.0)
+            weights = (exponent / jnp.sum(exponent, axis=1, keepdims=True)).astype(bf16)
+            context[:, cols] = jnp.dot(
+                weights, qkv_ref[2, :, cols], preferred_element_type=f32
+            ).astype(bf16)
+        for k in range(len(outs)):
+            start = pl.multiple_of(lax.rem(place_ref[0] + k, len(outs)) * share, share)
+            rolled[k * share : (k + 1) * share, :] = context[pl.ds(start, share), :]
+
+    partial = lax.dot_general(
+        rolled[...], weight_ref[...], (((1,), (1,)), ((), ())), preferred_element_type=f32
     )
-    pack_of = jnp.arange(length, dtype=jnp.int32) // ROWS_DEV
-    same_image = ((labels[:, None] == labels[None, :]) & (pack_of[:, None] == pack_of[None, :]))[
-        None
-    ]
-    masked = jnp.where(same_image, scores, -1e30)
-    row_top = jnp.max(masked, axis=2, keepdims=True)
-    exponent = jnp.where(same_image, jnp.exp(masked - row_top), 0.0)
-    weights = (exponent / jnp.sum(exponent, axis=2, keepdims=True)).astype(jnp.bfloat16)
-    context = jnp.einsum("hqk,khd->qhd", weights, value_rows, preferred_element_type=jnp.float32)
-    return context.reshape(length, head_count * HEAD).astype(jnp.bfloat16)
+    for k, out in enumerate(outs):
+        out[...] = partial[k * share : (k + 1) * share].astype(bf16)
+
+
+def attend(qkv, labels, out_weight, place, members):
+    length, width = qkv.shape[1:]
+    d_model = out_weight.shape[0]
+    block = min(512, d_model)
+    share = length // members
+    grid_spec = pltpu.PrefetchScalarGridSpec(
+        num_scalar_prefetch=1,
+        grid=(d_model // block,),
+        in_specs=[
+            pl.BlockSpec(qkv.shape, lambda j, p: (0, 0, 0)),
+            pl.BlockSpec((1, length), lambda j, p: (0, 0)),
+            pl.BlockSpec((block, width), lambda j, p: (j, 0)),
+        ],
+        out_specs=[pl.BlockSpec((share, block), lambda j, p: (0, j))] * members,
+        scratch_shapes=[pltpu.VMEM((length, width), bf16)] * 2,
+    )
+    return pl.pallas_call(
+        attend_kernel,
+        grid_spec=grid_spec,
+        out_shape=[jax.ShapeDtypeStruct((share, d_model), bf16)] * members,
+        cost_estimate=pl.CostEstimate(
+            flops=2 * length * width * (d_model + 2 * length),
+            transcendentals=length * length * width // HEAD,
+            bytes_accessed=2 * (qkv.size + out_weight.size + length * d_model),
+        ),
+        name="attend",
+    )(place.reshape(1), qkv, labels.reshape(1, length), out_weight)
+
+
+def merge_weight(index, products, others):
+    rows, width = others[0].shape
+    streams = len(others)
+    steps = max(1, rows // 128)
+    step = rows // steps
+
+    def kernel(index_ref, *refs):
+        out = refs[-1]
+        for q in range(streams):
+            mine = refs[q][...]
+            theirs = refs[streams + q][...].astype(f32)
+            low = slice(q * width, (q + 1) * width)
+            high = slice((streams + q) * width, (streams + q + 1) * width)
+
+            @pl.when(index_ref[0] == 0)
+            def _():
+                out[:, low] = mine
+                out[:, high] = theirs
+
+            @pl.when(index_ref[0] != 0)
+            def _():
+                out[:, low] = theirs
+                out[:, high] = mine
+
+    return pl.pallas_call(
+        kernel,
+        grid_spec=pltpu.PrefetchScalarGridSpec(
+            num_scalar_prefetch=1,
+            grid=(steps,),
+            in_specs=[pl.BlockSpec((step, width), lambda i, n: (n[0] * steps + i, 0))] * streams
+            + [pl.BlockSpec((step, width), lambda i, n: (i, 0))] * streams,
+            out_specs=pl.BlockSpec((step, 2 * streams * width), lambda i, n: (i, 0)),
+        ),
+        out_shape=jax.ShapeDtypeStruct((rows, 2 * streams * width), f32),
+        name="merge_weight",
+    )(index, *products, *others)
+
+
+def merge_act(index, own, others, slope):
+    rows, width = others[0].shape
+    streams = len(others)
+    steps = max(1, rows // 128)
+    step = rows // steps
+
+    def kernel(index_ref, *refs):
+        factor, out = refs[-2], refs[-1]
+        for q in range(streams):
+            mine = refs[q][...]
+            theirs = refs[streams + q][...].astype(f32)
+            low = slice(q * width, (q + 1) * width)
+            high = slice((streams + q) * width, (streams + q + 1) * width)
+
+            @pl.when(index_ref[0] == 0)
+            def _():
+                out[:, low] = mine * factor[:, low]
+                out[:, high] = theirs * factor[:, high]
+
+            @pl.when(index_ref[0] != 0)
+            def _():
+                out[:, low] = theirs * factor[:, low]
+                out[:, high] = mine * factor[:, high]
+
+    block = pl.BlockSpec((step, width), lambda i, n: (i, 0))
+    wide = pl.BlockSpec((step, 2 * streams * width), lambda i, n: (i, 0))
+    return pl.pallas_call(
+        kernel,
+        grid_spec=pltpu.PrefetchScalarGridSpec(
+            num_scalar_prefetch=1,
+            grid=(steps,),
+            in_specs=[block] * (2 * streams) + [wide],
+            out_specs=wide,
+        ),
+        out_shape=jax.ShapeDtypeStruct(slope.shape, f32),
+        name="merge_act",
+    )(index, *own, *others, slope)
 
 
 STREAMS = 2
@@ -87,6 +211,9 @@
         d_line = d_model // line
         d_side = d_line // 2
         half = hidden // 2
+
+        def first_then(first, then):
+            return lax.optimization_barrier((then, first))[0]
 
         def weight_grad_of(grads, act, ups, downs):
             product = None
@@ -105,11 +232,7 @@
                     preferred_element_type=f32,
                 )
                 product = term if product is None else product + term
-            product = product * (1.0 / n_dp)
-            own = lax.dynamic_slice(product, (side * d_side, 0), (d_side, width))
-            other = lax.dynamic_slice(product, ((1 - side) * d_side, 0), (d_side, width))
-            other = other.astype(bf16)
-            return own, across_side(other)
+            return product * (1.0 / n_dp)
 
         groups = [sorted({1, line - 1}), [*range(2, line - 1), 0]]
         shifted = []
@@ -147,13 +270,9 @@
             (gelu_exact(preact).astype(bf16), gelu_slope(preact))
         )
         width = half // STREAMS
-        acts = []
-        for q in range(STREAMS):
-            keep = lax.dynamic_slice(activation, (0, side * half + q * width), (tokens, width))
-            give = lax.dynamic_slice(
-                activation, (0, (1 - side) * half + q * width), (tokens, width)
-            )
-            acts.append(jnp.concatenate([keep, across_side(give)], axis=0))
+        keep = lax.dynamic_slice(activation, (0, side * half), (tokens, half))
+        give = lax.dynamic_slice(activation, (0, (1 - side) * half), (tokens, half))
+        act = jnp.concatenate([keep, across_side(give)], axis=0)
 
         stored_rows = down_weight.shape[0]
         pieces = lax.optimization_barrier(
@@ -185,51 +304,58 @@
             g, i = block_of[k]
             return products[g, q][i]
 
-        moving = [(acts[q], acts[q]) for q in range(STREAMS)]
+        def slot(right, left):
+            right = along_line(right, 1, lambda p: p < line - 1)
+            left = along_line(left, -1, lambda p: p > 0)
+            return right, left
+
+        def of_stream(value, q):
+            return value[:, q * width : (q + 1) * width]
+
+        got = slot(act, act)
+        moving = [tuple(of_stream(v, q) for v in got) for q in range(STREAMS)]
         ups, downs = [[] for _ in moving], [[] for _ in moving]
-        outs, own_h, other_h = [], [], []
-        for s in range(1, line + 1):
+        index = side.reshape(1)
+        full, others = [], []
+        for s in range(2, line + 1):
             for q in range(STREAMS):
                 right, left = moving[q]
-                if s > 1:
-                    ups[q].append(right)
-                    downs[q].append(left)
-                    right = right.astype(f32) + jnp.where(z < s - 1, part(s - 1, q), 0.0)
-                    left = left.astype(f32) + jnp.where(z > line - s, part(line - s + 1, q), 0.0)
-                    right, left = right.astype(bf16), left.astype(bf16)
+                ups[q].append(right)
+                downs[q].append(left)
+                to_right, to_left = part(s - 1, q), part(line - s + 1, q)
+                if s == 2 and q:
+                    to_right, to_left = first_then(joined, (to_right, to_left))
+                right = right.astype(f32) + jnp.where(z < s - 1, to_right, 0.0)
+                left = left.astype(f32) + jnp.where(z > line - s, to_left, 0.0)
+                joined = right, left = right.astype(bf16), left.astype(bf16)
                 if s == line:
-                    outs.append(weight_grad_of(grads, acts[q], ups[q], downs[q]))
-                right = along_line(right, 1, lambda p: p < line - 1)
-                left = along_line(left, -1, lambda p: p > 0)
-                moving[q] = right, left
+                    own_act = of_stream(act, q)
+                    if q:
+                        own_act, ups[q][0], downs[q][0] = first_then(
+                            other, (own_act, ups[q][0], downs[q][0])
+                        )
+                    product = weight_grad_of(grads, own_act, ups[q], downs[q])
+                    other = lax.dynamic_slice(
+                        product, ((1 - side) * d_side, 0), (d_side, width)
+                    ).astype(bf16)
+                    others.append(across_side(other))
+                    full.append(product)
+                moving[q] = slot(right, left)
+        own, gives = [], []
         for q in range(STREAMS):
             right, left = moving[q]
-            total = part(0, q) + right.astype(f32) + left.astype(f32)
-            own_h.append(total[:tokens])
-            give = total[tokens:].astype(bf16)
-            other_h.append(across_side(give).astype(f32))
-        act_grad = (
-            place(jnp.concatenate(own_h, axis=1), jnp.concatenate(other_h, axis=1), side, 1)
-            * slope
-        )
-        own = jnp.concatenate([o[0] for o in outs], axis=1)
-        other = jnp.concatenate([o[1].astype(f32) for o in outs], axis=1)
-        weight_grad = place(own, other, side, 1)
-
-        qkv, _ = lax.optimization_barrier((qkv, products[0, 0]))
-        context = attend(qkv, segment_ids[0].reshape(-1))
-        partial = lax.dot_general(
-            context, out_weight, (((1,), (1,)), ((), ())), preferred_element_type=f32
-        ).astype(bf16)
-        share = partial.shape[0] // n_tensor
-        total = lax.dynamic_slice(partial, (t * share, 0), (share, d_model)).astype(f32)
+            total_h = part(0, q) + right.astype(f32) + left.astype(f32)
+            own.append(total_h[:tokens])
+            give = total_h[tokens:].astype(bf16)
+            gives.append(across_side(give))
+        weight_grad = merge_weight(index, full, others)
+        act_grad = merge_act(index, own, gives, slope)
+
+        shares = list(attend(qkv, segment_ids[0], out_weight, t, n_tensor))
         for k in range(1, n_tensor):
-            rows = lax.dynamic_slice(
-                partial, (((t + k) % n_tensor) * share, 0), (share, d_model)
-            )
             pairs = [(i, (i + k) % n_tensor) for i in range(n_tensor)]
-            total = total + lax.ppermute(rows, "tensor", pairs).astype(f32)
-        attention_out = total + out_bias.astype(f32)
+            shares[k] = lax.ppermute(shares[k], "tensor", pairs)
+        attention_out = sum(share.astype(f32) for share in shares) + out_bias.astype(f32)
         return (attention_out, act_grad, weight_grad)
 
     return body

time: 221 us -> 214 us (0.968)
  waiting for transfers between devices: 74.2 us -> 107 us
  Pallas kernels: 0 us -> 18.2 us
  starting transfers between devices: 70.3 us -> 52.6 us
  other arithmetic: 29.9 us -> 13.3 us
  matrix products: 23.8 us -> 10.1 us
  local copies, waits for them, and re-layouts: 19.5 us -> 11.1 us
    ppermute x19 -> x17, waiting for transfers between devices: 26.9 us -> 57.2 us  [along_line(): return lax.ppermute(value, 'dp', pairs)]
    pallas_call x0 -> x3, Pallas kernels: none -> 18.2 us  [the longest x1 10.6 us: attend(): pl.pallas_call(attend_kernel, grid_spec=grid_spec, out_shape=[jax.ShapeDt...]
    ppermute x19 -> x17, starting transfers between devices: 53.4 us -> 42.5 us  [along_line(): return lax.ppermute(value, 'dp', pairs)]
    dot_general x2 -> x0, matrix products: 7.72 us -> none  [the longest x1 5.81 us: body(): lax.dot_general(context, out_weight, (((1,), (1,)), ((), ())), preferred_...]
    ppermute x2, waiting for transfers between devices: 11.6 us -> 4 us  [along_cross(): lax.ppermute(value, 'tensor', [(t, (t + 2 * shift) % n_tensor) for t in r...]
    ppermute x10 -> x9, waiting for transfers between devices: 35.6 us -> 41.8 us  [across_side(): return lax.ppermute(value, 'dp', [(i, i ^ 1) for i in range(n_dp)])]
    unnamed x57 -> x26, local copies, waits for them, and re-layouts: 6.86 us -> 2 us
    select_n x4 -> x2, other arithmetic: 5.15 us -> 1.25 us  [place(): first = jnp.where(index == 0, own, other)]
  transfers between devices with their start and end apart: 36 -> 33, of which waited for: 13 -> 21; matrix products, arithmetic and copies ran while one was open for 31% -> 14% of each run, Pallas kernels for 0% -> 7%
where the time goes in v2:
time: 214 us; the launch traced here: 213 us
  waiting for transfers between devices  107 us (50%)
  starting transfers between devices  52.6 us (25%)
  Pallas kernels  18.2 us (9%)
  other arithmetic  13.3 us (6%)
  local copies, waits for them, and re-layouts  11.1 us (5%)
  matrix products  10.1 us (5%)
    ppermute x17, waiting for transfers between devices, along_line(): return lax.ppermute(value, 'dp', pairs)  57.2 us
    ppermute x17, starting transfers between devices, along_line(): return lax.ppermute(value, 'dp', pairs)  42.5 us
    ppermute x9, waiting for transfers between devices, across_side(): return lax.ppermute(value, 'dp', [(i, i ^ 1) for i in range(n_dp)])  41.8 us
    pallas_call x1, Pallas kernels, attend(): pl.pallas_call(attend_kernel, grid_spec=grid_spec, out_shape=[jax.ShapeDt...  10.6 us
    ppermute x9, starting transfers between devices, across_side(): return lax.ppermute(value, 'dp', [(i, i ^ 1) for i in range(n_dp)])  7.83 us
    dot_general x4, matrix products, weight_grad_of(): lax.dot_general(grads[g].reshape(-1, d_line), chunk, (((0,), (0,)), ((),...  5.18 us
    dot_general x4, matrix products, multiply(): lax.dot_general(grads[g], weights[q], (((2,), (0,)), ((), ())), preferred...  4.96 us
    pallas_call x1, Pallas kernels, merge_weight(): pl.pallas_call(kernel, grid_spec=pltpu.PrefetchScalarGridSpec(num_scalar_...  4.47 us
  transfers between devices with their start and end apart: 33, of which 21 were waited for; matrix products, arithmetic and copies ran while one was open for 14% of the time, Pallas kernels for 7%

profile of v2, /device:TPU:0, one launch (start us, length us, event | category | flops | bytes accessed | tf_op | source)
XLA Modules:
  0.0 213.2 jit_solution(4217943173791282388)
XLA Ops:
  0.7 1.8 constant_dynamic-slice_fusion.1
  2.5 4.1 %collective-permute-start.3 = (bf16[64,1024]{1,0:T(8,128)(2,1)S(1)}, bf16[64,1024]{1,0:T(8,128)(2,1)S(1)}, u32[]{:S(2)}, u32[]{:S(2)}) collective-permute-start(bf16[64,1024]{1,0:T(8,128)(2,1)S(1)} %get-tuple-element.73), channel_id=1, source_target_pairs={{0,16},{4,20},{8,24},{12,28},{16,0},{20,4},{24,8},{28,12},{1,17},{... | collective-permute-start | bytes 393224 | tf_op jit(solution)/shard_map/ppermute | solution.py:186
  6.6 6.3 %collective-permute-done.3 = bf16[64,1024]{1,0:T(8,128)(2,1)S(1)} collective-permute-done((bf16[64,1024]{1,0:T(8,128)(2,1)S(1)}, bf16[64,1024]{1,0:T(8,128)(2,1)S(1)}, u32[]{:S(2)}, u32[]{:S(2)}) %collective-permute-start.3) | collective-permute-done | bytes 131104 | tf_op jit(solution)/shard_map/ppermute | solution.py:186
  12.9 1.6 collective-permute-start.4
  14.6 1.3 reshape_squeeze.3.labels_ref
  15.9 10.6 %attend.1 = (bf16[64,4096]{1,0:T(8,128)(2,1)}, bf16[64,4096]{1,0:T(8,128)(2,1)}, bf16[64,4096]{1,0:T(8,128)(2,1)}, bf16[64,4096]{1,0:T(8,128)(2,1)}) custom-call(s32[1]{0:T(128)} %bitcast.place_ref, bf16[3,256,1024]{2,1,0:T(8,128)(2,1)} %qkv_ref.1, s32[1,256]{1,0:T(1,128)} %reshape_squeeze.3.labels_ref, bf16[4096,1024]{1,0:T(8,128)(2,1)} %weight_ref.1), custom_call_target="tpu_custom_call" | custom-call | flops 2415919104 | bytes 12058624 | tf_op jit(solution)/shard_map/attend/pallas_call | solution.py:84
  26.5 4.3 %collective-permute-start.11 = (bf16[64,1024]{1,0:T(8,128)(2,1)}, bf16[64,1024]{1,0:T(8,128)(2,1)S(1)}, u32[]{:S(2)}, u32[]{:S(2)}) collective-permute-start(bf16[64,1024]{1,0:T(8,128)(2,1)} %get-tuple-element.74), channel_id=1, source_target_pairs={{0,24},{4,28},{8,0},{12,4},{16,8},{20,12},{24,16},{28,20},{1,25},{... | collective-permute-start | bytes 393224 | tf_op jit(solution)/shard_map/ppermute | solution.py:186
  30.8 0.9 fusion.50
  31.7 0.7 collective-permute-start.5
  32.4 2.0 fusion.6
  34.4 0.9 constant_dynamic-slice_fusion.3
  35.8 1.8 collective-permute-done.10
  38.2 2.9 %constant_dynamic-slice_fusion.4 = (bf16[512,512]{1,0:T(8,128)(2,1)}, bf16[512,512]{1,0:T(8,128)(2,1)}, bf16[512,512]{1,0:T(8,128)(2,1)}, bf16[512,512]{1,0:T(8,128)(2,1)}) fusion(bf16[512,2048]{1,0:T(8,128)(2,1)} %param.13, s32[]{:T(128)S(6)} %select_n.344, s32[]{:T(128)S(6)} %select_n.342, s32[]{:T(128)S(6)} %select_n.341, s32[]{:T(128)S(6)} %select_n.343), kind=kLoop, calls=%fused_computation.117 | loop fusion | bytes 4194320 | tf_op jit(solution)/shard_map/dynamic_slice | solution.py:280
  41.1 1.5 collective-permute-start.7
  42.6 4.0 %collective-permute-done.5 = bf16[2,2,64,1024]{3,2,1,0:T(8,128)(2,1)S(1)} collective-permute-done((bf16[2,2,64,1024]{3,2,1,0:T(8,128)(2,1)}, bf16[2,2,64,1024]{3,2,1,0:T(8,128)(2,1)S(1)}, u32[]{:S(2)}, u32[]{:S(2)}) %collective-permute-start.5) | collective-permute-done | bytes 524320 | tf_op jit(solution)/shard_map/ppermute | solution.py:195
  47.2 8.7 %collective-permute-done.12 = bf16[2,64,1024]{2,1,0:T(8,128)(2,1)S(1)} collective-permute-done((bf16[2,64,1024]{2,1,0:T(8,128)(2,1)S(1)}, bf16[2,64,1024]{2,1,0:T(8,128)(2,1)S(1)}, u32[]{:S(2)}, u32[]{:S(2)}) %collective-permute-start.12) | collective-permute-done | bytes 262176 | tf_op jit(solution)/shard_map/ppermute | solution.py:189
  56.0 1.4 collective-permute-start.13
  57.4 1.2 pad_maximum_fusion.2
  58.6 1.2 fusion.38
  59.7 7.5 %collective-permute-done.7 = bf16[512,512]{1,0:T(8,128)(2,1)} collective-permute-done((bf16[512,512]{1,0:T(8,128)(2,1)}, bf16[512,512]{1,0:T(8,128)(2,1)}, u32[]{:S(2)}, u32[]{:S(2)}) %collective-permute-start.7) | collective-permute-done | bytes 524320 | tf_op jit(solution)/shard_map/ppermute | solution.py:189
  67.3 1.3 collective-permute-start.9
  68.6 1.1 broadcast_select_fusion.9
  69.8 7.6 %collective-permute-done.22 = bf16[512,512]{1,0:T(8,128)(2,1)S(1)} collective-permute-done((bf16[512,512]{1,0:T(8,128)(2,1)}, bf16[512,512]{1,0:T(8,128)(2,1)S(1)}, u32[]{:S(2)}, u32[]{:S(2)}) %collective-permute-start.22) | collective-permute-done | bytes 524320 | tf_op jit(solution)/shard_map/ppermute | solution.py:189
  77.3 1.3 collective-permute-start.18
  79.8 1.2 fusion.36
  82.2 1.2 fusion.35
  83.4 5.9 %collective-permute-done.9 = bf16[512,1024]{1,0:T(8,128)(2,1)S(1)} collective-permute-done((bf16[512,1024]{1,0:T(8,128)(2,1)S(1)}, bf16[512,1024]{1,0:T(8,128)(2,1)S(1)}, u32[]{:S(2)}, u32[]{:S(2)}) %collective-permute-start.9) | collective-permute-done | bytes 1048608 | tf_op jit(solution)/shard_map/ppermute | solution.py:186
  89.3 13.9 %collective-permute-done.18 = bf16[512,1024]{1,0:T(8,128)(2,1)S(1)} collective-permute-done((bf16[512,1024]{1,0:T(8,128)(2,1)S(1)}, bf16[512,1024]{1,0:T(8,128)(2,1)S(1)}, u32[]{:S(2)}, u32[]{:S(2)}) %collective-permute-start.18) | collective-permute-done | bytes 1048608 | tf_op jit(solution)/shard_map/ppermute | solution.py:186
  103.7 1.5 collective-permute-start.15
  105.2 1.3 collective-permute-start.19
  106.5 1.2 fusion.33
  108.1 5.0 %collective-permute-start.23 = (bf16[512,512]{1,0:T(8,128)(2,1)S(1)}, bf16[512,512]{1,0:T(8,128)(2,1)S(1)}, u32[]{:S(2)}, u32[]{:S(2)}) collective-permute-start(bf16[512,512]{1,0:T(8,128)(2,1)S(1)} %add_convert_fusion.3), channel_id=1, source_target_pairs={{0,8},{4,12},{8,16},{12,20},{16,24},{20,28},{1,9},{5,13},{9,17},{1... | collective-permute-start | bytes 1572872 | tf_op jit(solution)/shard_map/ppermute | solution.py:186
  113.4 1.3 collective-permute-start.26
  114.7 1.2 fusion.34
  115.9 1.5 collective-permute-done.15
  117.5 4.9 %collective-permute-done.19 = bf16[512,512]{1,0:T(8,128)(2,1)S(1)} collective-permute-done((bf16[512,512]{1,0:T(8,128)(2,1)S(1)}, bf16[512,512]{1,0:T(8,128)(2,1)S(1)}, u32[]{:S(2)}, u32[]{:S(2)}) %collective-permute-start.19) | collective-permute-done | bytes 524320 | tf_op jit(solution)/shard_map/ppermute | solution.py:186
  122.6 4.0 %collective-permute-start.16 = (bf16[512,512]{1,0:T(8,128)(2,1)S(1)}, bf16[512,512]{1,0:T(8,128)(2,1)S(1)}, u32[]{:S(2)}, u32[]{:S(2)}) collective-permute-start(bf16[512,512]{1,0:T(8,128)(2,1)S(1)} %get-tuple-element.41), channel_id=1, source_target_pairs={{0,8},{4,12},{8,16},{12,20},{16,24},{20,28},{1,9},{5,13},{9,17},{1... | collective-permute-start | bytes 1572872 | tf_op jit(solution)/shard_map/ppermute | solution.py:186
  126.6 1.5 collective-permute-start.20
  128.7 4.9 %collective-permute-done.26 = bf16[512,512]{1,0:T(8,128)(2,1)S(1)} collective-permute-done((bf16[512,512]{1,0:T(8,128)(2,1)S(1)}, bf16[512,512]{1,0:T(8,128)(2,1)S(1)}, u32[]{:S(2)}, u32[]{:S(2)}) %collective-permute-start.26) | collective-permute-done | bytes 524320 | tf_op jit(solution)/shard_map/ppermute | solution.py:186
  133.9 4.0 %collective-permute-start.24 = (bf16[512,512]{1,0:T(8,128)(2,1)S(1)}, bf16[512,512]{1,0:T(8,128)(2,1)S(1)}, u32[]{:S(2)}, u32[]{:S(2)}) collective-permute-start(bf16[512,512]{1,0:T(8,128)(2,1)S(1)} %get-tuple-element.35), channel_id=1, source_target_pairs={{0,8},{4,12},{8,16},{12,20},{16,24},{20,28},{1,9},{5,13},{9,17},{1... | collective-permute-start | bytes 1572872 | tf_op jit(solution)/shard_map/ppermute | solution.py:186
  137.8 1.3 collective-permute-start.27
  139.2 1.3 fusion.14
  140.6 4.2 %collective-permute-done.20 = bf16[512,512]{1,0:T(8,128)(2,1)S(1)} collective-permute-done((bf16[512,512]{1,0:T(8,128)(2,1)S(1)}, bf16[512,512]{1,0:T(8,128)(2,1)S(1)}, u32[]{:S(2)}, u32[]{:S(2)}) %collective-permute-start.20) | collective-permute-done | bytes 524320 | tf_op jit(solution)/shard_map/ppermute | solution.py:186
  145.2 1.3 collective-permute-start.21
  146.5 4.6 %collective-permute-start.17 = (bf16[512,512]{1,0:T(8,128)(2,1)S(1)}, bf16[512,512]{1,0:T(8,128)(2,1)S(1)}, u32[]{:S(2)}, u32[]{:S(2)}) collective-permute-start(bf16[512,512]{1,0:T(8,128)(2,1)S(1)} %get-tuple-element.39), channel_id=1, source_target_pairs={{0,8},{4,12},{8,16},{12,20},{16,24},{20,28},{1,9},{5,13},{9,17},{1... | collective-permute-start | bytes 1572872 | tf_op jit(solution)/shard_map/ppermute | solution.py:186
  151.2 4.9 %collective-permute-done.27 = bf16[512,512]{1,0:T(8,128)(2,1)S(1)} collective-permute-done((bf16[512,512]{1,0:T(8,128)(2,1)S(1)}, bf16[512,512]{1,0:T(8,128)(2,1)S(1)}, u32[]{:S(2)}, u32[]{:S(2)}) %collective-permute-start.27) | collective-permute-done | bytes 524320 | tf_op jit(solution)/shard_map/ppermute | solution.py:186
  156.4 1.3 collective-permute-start.28
  157.7 4.6 %collective-permute-start.25 = (bf16[512,512]{1,0:T(8,128)(2,1)S(1)}, bf16[512,512]{1,0:T(8,128)(2,1)S(1)}, u32[]{:S(2)}, u32[]{:S(2)}) collective-permute-start(bf16[512,512]{1,0:T(8,128)(2,1)S(1)} %get-tuple-element.33), channel_id=1, source_target_pairs={{0,8},{4,12},{8,16},{12,20},{16,24},{20,28},{1,9},{5,13},{9,17},{1... | collective-permute-start | bytes 1572872 | tf_op jit(solution)/shard_map/ppermute | solution.py:186
  162.5 1.3 add_multiply_fusion.1.refs_0_
  163.9 1.3 fusion.21
  165.4 1.3 add_multiply_fusion.refs_1_
  168.1 7.6 %collective-permute-done.28 = bf16[512,512]{1,0:T(8,128)(2,1)S(1)} collective-permute-done((bf16[512,512]{1,0:T(8,128)(2,1)S(1)}, bf16[512,512]{1,0:T(8,128)(2,1)S(1)}, u32[]{:S(2)}, u32[]{:S(2)}) %collective-permute-start.28) | collective-permute-done | bytes 524320 | tf_op jit(solution)/shard_map/ppermute | solution.py:186
  176.2 1.5 collective-permute-start.32
  178.6 3.0 %collective-permute-done.1 = bf16[64,4096]{1,0:T(8,128)(2,1)S(1)} collective-permute-done((bf16[64,4096]{1,0:T(8,128)(2,1)S(1)}, bf16[64,4096]{1,0:T(8,128)(2,1)S(1)}, u32[]{:S(2)}, u32[]{:S(2)}) %collective-permute-start.1) | collective-permute-done | bytes 524320 | tf_op jit(solution)/shard_map/ppermute | solution.py:357
  182.1 2.3 %add_add_fusion = f32[64,4096]{1,0:T(8,128)} fusion(bf16[64,4096]{1,0:T(8,128)(2,1)} %collective-permute-done.2, bf16[64,4096]{1,0:T(8,128)(2,1)S(1)} %collective-permute-done.1, bf16[64,4096]{1,0:T(8,128)(2,1)S(1)} %collective-permute-done, bf16[64,4096]{1,0:T(8,128)(2,1)S(1)} %copy-done.7, f32[4096]{0:T(1024)S(1)} %convert_element_type.117), kind=kLoop, calls=%fused_computation.69 | loop fusion | flops 2097152 | bytes 3162112 | tf_op jit(solution)/shard_map/add | solution.py:358
  184.4 0.9 slice.118.refs_0_
  185.2 0.8 slice.125.refs_1_
  186.1 4.5 %collective-permute-done.31.refs_2_ = bf16[512,512]{1,0:T(8,128)(2,1)S(1)} collective-permute-done((bf16[512,512]{1,0:T(8,128)(2,1)S(1)}, bf16[512,512]{1,0:T(8,128)(2,1)S(1)}, u32[]{:S(2)}, u32[]{:S(2)}) %collective-permute-start.31) | collective-permute-done | bytes 524320 | tf_op jit(solution)/shard_map/ppermute | solution.py:189
  190.5 11.2 %collective-permute-done.32.refs_3_ = bf16[512,512]{1,0:T(8,128)(2,1)S(1)} collective-permute-done((bf16[512,512]{1,0:T(8,128)(2,1)S(1)}, bf16[512,512]{1,0:T(8,128)(2,1)S(1)}, u32[]{:S(2)}, u32[]{:S(2)}) %collective-permute-start.32) | collective-permute-done | bytes 524320 | tf_op jit(solution)/shard_map/ppermute | solution.py:189
  201.7 0.8 copy-done.6
  202.6 4.5 %merge_weight.1 = f32[512,2048]{1,0:T(8,128)} custom-call(s32[1]{0:T(128)} %bitcast.1.index_ref, f32[1024,512]{1,0:T(8,128)} %copy-done, f32[1024,512]{1,0:T(8,128)} %copy-done.1, bf16[512,512]{1,0:T(8,128)(2,1)} %copy-done.5, bf16[512,512]{1,0:T(8,128)(2,1)} %copy-done.6), custom_call_target="tpu_custom_call" | custom-call | tf_op jit(solution)/shard_map/merge_weight/pallas_call | solution.py:121
  207.0 2.3 %collective-permute-done.30.refs_3_ = bf16[256,512]{1,0:T(8,128)(2,1)S(1)} collective-permute-done((bf16[256,512]{1,0:T(8,128)(2,1)S(1)}, bf16[256,512]{1,0:T(8,128)(2,1)S(1)}, u32[]{:S(2)}, u32[]{:S(2)}) %collective-permute-start.30) | collective-permute-done | bytes 262176 | tf_op jit(solution)/shard_map/ppermute | solution.py:189
  209.3 0.7 copy-done.9
  210.0 3.2 %merge_act.1 = f32[256,2048]{1,0:T(8,128)} custom-call(s32[1]{0:T(128)} %bitcast.1.index_ref, f32[256,512]{1,0:T(8,128)} %slice.118.refs_0_, f32[256,512]{1,0:T(8,128)} %slice.125.refs_1_, bf16[256,512]{1,0:T(8,128)(2,1)} %copy-done.8, bf16[256,512]{1,0:T(8,128)(2,1)} %copy-done.9, f32[256,2048]{1,0:T(8,128)} %get-tuple-element.29.refs_4_), custom_call_target="tpu_custom_call" | custom-call | tf_op jit(solution)/shard_map/merge_act/pallas_call | solution.py:161
  (85 shorter events, 11.0 us)
Async XLA Ops:
  2.5 10.4 %collective-permute-start.3 = (bf16[64,1024]{1,0:T(8,128)(2,1)S(1)}, bf16[64,1024]{1,0:T(8,128)(2,1)S(1)}, u32[]{:S(2)}, u32[]{:S(2)}) collective-permute-start(bf16[64,1024]{1,0:T(8,128)(2,1)S(1)} %get-tuple-element.73), channel_id=1, source_target_pairs={{0,16},{4,20},{8,24},{12,28},{16,0},{20,4},{24,8},{28,12},{1,17},{... | collective-permute-start | bytes 393224 | tf_op jit(solution)/shard_map/ppermute | solution.py:186
  12.9 17.9 %collective-permute-start.4 = (bf16[2,64,1024]{2,1,0:T(8,128)(2,1)S(1)}, bf16[2,64,1024]{2,1,0:T(8,128)(2,1)S(1)}, u32[]{:S(2)}, u32[]{:S(2)}) collective-permute-start(bf16[2,64,1024]{2,1,0:T(8,128)(2,1)S(1)} %get-tuple-element.80), channel_id=1, source_target_pairs={{0,4},{4,0},{8,12},{12,8},{16,20},{20,16},{24,28},{28,24},{1,5},{5... | collective-permute-start | bytes 786440 | tf_op jit(solution)/shard_map/ppermute | solution.py:189
  26.5 6.0 %copy-start.4 = (bf16[256,2048]{1,0:T(8,128)(2,1)S(1)}, bf16[256,2048]{1,0:T(8,128)(2,1)}, u32[]{:S(2)}) copy-start(bf16[256,2048]{1,0:T(8,128)(2,1)} %param.12) | copy-start | bytes 3145732
  26.5 151.6 %collective-permute-start.2 = (bf16[64,4096]{1,0:T(8,128)(2,1)}, bf16[64,4096]{1,0:T(8,128)(2,1)}, u32[]{:S(2)}, u32[]{:S(2)}) collective-permute-start(bf16[64,4096]{1,0:T(8,128)(2,1)} %get-tuple-element.21), channel_id=1, source_target_pairs={{0,3},{1,0},{2,1},{3,2},{4,7},{5,4},{6,5},{7,6},{8,11},{9,8},{10,9... | collective-permute-start | bytes 1572872 | tf_op jit(solution)/shard_map/ppermute | solution.py:357
  26.5 9.3 %collective-permute-start.11 = (bf16[64,1024]{1,0:T(8,128)(2,1)}, bf16[64,1024]{1,0:T(8,128)(2,1)S(1)}, u32[]{:S(2)}, u32[]{:S(2)}) collective-permute-start(bf16[64,1024]{1,0:T(8,128)(2,1)} %get-tuple-element.74), channel_id=1, source_target_pairs={{0,24},{4,28},{8,0},{12,4},{16,8},{20,12},{24,16},{28,20},{1,25},{... | collective-permute-start | bytes 393224 | tf_op jit(solution)/shard_map/ppermute | solution.py:186
  30.8 6.8 %collective-permute-start.10 = (bf16[64,1024]{1,0:T(8,128)(2,1)S(1)}, bf16[64,1024]{1,0:T(8,128)(2,1)S(1)}, u32[]{:S(2)}, u32[]{:S(2)}) collective-permute-start(bf16[64,1024]{1,0:T(8,128)(2,1)S(1)} %get-tuple-element.71), channel_id=1, source_target_pairs={{0,8},{4,12},{8,16},{12,20},{16,24},{20,28},{24,0},{28,4},{1,9},{5... | collective-permute-start | bytes 393224 | tf_op jit(solution)/shard_map/ppermute | solution.py:186
  31.7 14.9 %collective-permute-start.5 = (bf16[2,2,64,1024]{3,2,1,0:T(8,128)(2,1)}, bf16[2,2,64,1024]{3,2,1,0:T(8,128)(2,1)S(1)}, u32[]{:S(2)}, u32[]{:S(2)}) collective-permute-start(bf16[2,2,64,1024]{3,2,1,0:T(8,128)(2,1)} %get-tuple-element.76), channel_id=1, source_target_pairs={{0,2},{1,3},{2,0},{3,1},{4,6},{5,7},{6,4},{7,5},{8,10},{9,11},{10,... | collective-permute-start | bytes 1572872 | tf_op jit(solution)/shard_map/ppermute | solution.py:195
  35.3 20.7 %collective-permute-start.8 = (bf16[256,1024]{1,0:T(8,128)(2,1)}, bf16[256,1024]{1,0:T(8,128)(2,1)}, u32[]{:S(2)}, u32[]{:S(2)}) collective-permute-start(bf16[256,1024]{1,0:T(8,128)(2,1)} %get-tuple-element.64), channel_id=1, source_target_pairs={{0,4},{4,0},{8,12},{12,8},{16,20},{20,16},{24,28},{28,24},{1,5},{5... | collective-permute-start | bytes 1572872 | tf_op jit(solution)/shard_map/ppermute | solution.py:189
  37.6 5.0 %copy-start.10 = (bf16[4096]{0:T(1024)(128)(2,1)S(1)}, bf16[4096]{0:T(1024)(128)(2,1)}, u32[]{:S(2)}) copy-start(bf16[4096]{0:T(1024)(128)(2,1)} %param.10) | copy-start | bytes 24580
  37.7 18.3 %collective-permute-start.12 = (bf16[2,64,1024]{2,1,0:T(8,128)(2,1)S(1)}, bf16[2,64,1024]{2,1,0:T(8,128)(2,1)S(1)}, u32[]{:S(2)}, u32[]{:S(2)}) collective-permute-start(bf16[2,64,1024]{2,1,0:T(8,128)(2,1)S(1)} %get-tuple-element.78), channel_id=1, source_target_pairs={{0,4},{4,0},{8,12},{12,8},{16,20},{20,16},{24,28},{28,24},{1,5},{5... | collective-permute-start | bytes 786440 | tf_op jit(solution)/shard_map/ppermute | solution.py:189
  41.1 26.2 %collective-permute-start.7 = (bf16[512,512]{1,0:T(8,128)(2,1)}, bf16[512,512]{1,0:T(8,128)(2,1)}, u32[]{:S(2)}, u32[]{:S(2)}) collective-permute-start(bf16[512,512]{1,0:T(8,128)(2,1)} %get-tuple-element.23), channel_id=1, source_target_pairs={{0,4},{4,0},{8,12},{12,8},{16,20},{20,16},{24,28},{28,24},{1,5},{5... | collective-permute-start | bytes 1572872 | tf_op jit(solution)/shard_map/ppermute | solution.py:189
  46.6 30.7 %collective-permute-start.22 = (bf16[512,512]{1,0:T(8,128)(2,1)}, bf16[512,512]{1,0:T(8,128)(2,1)S(1)}, u32[]{:S(2)}, u32[]{:S(2)}) collective-permute-start(bf16[512,512]{1,0:T(8,128)(2,1)} %get-tuple-element.26), channel_id=1, source_target_pairs={{0,4},{4,0},{8,12},{12,8},{16,20},{20,16},{24,28},{28,24},{1,5},{5... | collective-permute-start | bytes 1572872 | tf_op jit(solution)/shard_map/ppermute | solution.py:189
  55.9 23.0 %collective-permute-start.6 = (bf16[2,2,2,64,1024]{4,3,2,1,0:T(8,128)(2,1)S(1)}, bf16[2,2,2,64,1024]{4,3,2,1,0:T(8,128)(2,1)S(1)}, u32[]{:S(2)}, u32[]{:S(2)}) collective-permute-start(bf16[2,2,2,64,1024]{4,3,2,1,0:T(8,128)(2,1)S(1)} %pad_maximum_fusion.3), channel_id=1, source_target_pairs={{0,1},{1,0},{2,3},{3,2},{4,5},{5,4},{6,7},{7,6},{8,9},{9,8},{10,11... | collective-permute-start | bytes 3145736 | tf_op jit(solution)/shard_map/ppermute | solution.py:192
  56.0 22.7 %collective-permute-start.13 = (bf16[2,2,64,1024]{3,2,1,0:T(8,128)(2,1)S(1)}, bf16[2,2,64,1024]{3,2,1,0:T(8,128)(2,1)S(1)}, u32[]{:S(2)}, u32[]{:S(2)}) collective-permute-start(bf16[2,2,64,1024]{3,2,1,0:T(8,128)(2,1)S(1)} %get-tuple-element.70), channel_id=1, source_target_pairs={{0,2},{1,3},{2,0},{3,1},{4,6},{5,7},{6,4},{7,5},{8,10},{9,11},{10,... | collective-permute-start | bytes 1572872 | tf_op jit(solution)/shard_map/ppermute | solution.py:195
  57.4 11.2 %copy-start.3 = (bf16[512,512]{1,0:T(8,128)(2,1)S(1)}, bf16[512,512]{1,0:T(8,128)(2,1)}, u32[]{:S(2)}) copy-start(bf16[512,512]{1,0:T(8,128)(2,1)} %get-tuple-element.22) | copy-start | bytes 1572868
  58.6 20.0 %copy-start.2 = (bf16[512,512]{1,0:T(8,128)(2,1)S(1)}, bf16[512,512]{1,0:T(8,128)(2,1)}, u32[]{:S(2)}) copy-start(bf16[512,512]{1,0:T(8,128)(2,1)} %get-tuple-element.25) | copy-start | bytes 1572868
  67.3 22.1 %collective-permute-start.9 = (bf16[512,1024]{1,0:T(8,128)(2,1)S(1)}, bf16[512,1024]{1,0:T(8,128)(2,1)S(1)}, u32[]{:S(2)}, u32[]{:S(2)}) collective-permute-start(bf16[512,1024]{1,0:T(8,128)(2,1)S(1)} %pad_maximum_fusion.2), channel_id=1, source_target_pairs={{0,8},{4,12},{8,16},{12,20},{16,24},{20,28},{1,9},{5,13},{9,17},{1... | collective-permute-start | bytes 3145736 | tf_op jit(solution)/shard_map/ppermute | solution.py:186
  77.3 26.0 %collective-permute-start.18 = (bf16[512,1024]{1,0:T(8,128)(2,1)S(1)}, bf16[512,1024]{1,0:T(8,128)(2,1)S(1)}, u32[]{:S(2)}, u32[]{:S(2)}) collective-permute-start(bf16[512,1024]{1,0:T(8,128)(2,1)S(1)} %pad_maximum_fusion.2), channel_id=1, source_target_pairs={{8,0},{12,4},{16,8},{20,12},{24,16},{28,20},{9,1},{13,5},{17,9},{2... | collective-permute-start | bytes 3145736 | tf_op jit(solution)/shard_map/ppermute | solution.py:186
  78.9 2.7 %collective-permute-start.14 = (bf16[2,2,2,64,1024]{4,3,2,1,0:T(8,128)(2,1)S(1)}, bf16[2,2,2,64,1024]{4,3,2,1,0:T(8,128)(2,1)S(1)}, u32[]{:S(2)}, u32[]{:S(2)}) collective-permute-start(bf16[2,2,2,64,1024]{4,3,2,1,0:T(8,128)(2,1)S(1)} %pad_maximum_fusion.4), channel_id=1, source_target_pairs={{0,1},{1,0},{2,3},{3,2},{4,5},{5,4},{6,7},{7,6},{8,9},{9,8},{10,11... | collective-permute-start | bytes 3145736 | tf_op jit(solution)/shard_map/ppermute | solution.py:192
  103.7 13.8 %collective-permute-start.15 = (bf16[512,512]{1,0:T(8,128)(2,1)S(1)}, bf16[512,512]{1,0:T(8,128)(2,1)S(1)}, u32[]{:S(2)}, u32[]{:S(2)}) collective-permute-start(bf16[512,512]{1,0:T(8,128)(2,1)S(1)} %get-tuple-element.43), channel_id=1, source_target_pairs={{0,8},{4,12},{8,16},{12,20},{16,24},{20,28},{1,9},{5,13},{9,17},{1... | collective-permute-start | bytes 1572872 | tf_op jit(solution)/shard_map/ppermute | solution.py:186
  105.2 17.1 %collective-permute-start.19 = (bf16[512,512]{1,0:T(8,128)(2,1)S(1)}, bf16[512,512]{1,0:T(8,128)(2,1)S(1)}, u32[]{:S(2)}, u32[]{:S(2)}) collective-permute-start(bf16[512,512]{1,0:T(8,128)(2,1)S(1)} %get-tuple-element.44), channel_id=1, source_target_pairs={{8,0},{12,4},{16,8},{20,12},{24,16},{28,20},{9,1},{13,5},{17,9},{2... | collective-permute-start | bytes 1572872 | tf_op jit(solution)/shard_map/ppermute | solution.py:186
  108.1 20.6 %collective-permute-start.23 = (bf16[512,512]{1,0:T(8,128)(2,1)S(1)}, bf16[512,512]{1,0:T(8,128)(2,1)S(1)}, u32[]{:S(2)}, u32[]{:S(2)}) collective-permute-start(bf16[512,512]{1,0:T(8,128)(2,1)S(1)} %add_convert_fusion.3), channel_id=1, source_target_pairs={{0,8},{4,12},{8,16},{12,20},{16,24},{20,28},{1,9},{5,13},{9,17},{1... | collective-permute-start | bytes 1572872 | tf_op jit(solution)/shard_map/ppermute | solution.py:186
  113.4 20.2 %collective-permute-start.26 = (bf16[512,512]{1,0:T(8,128)(2,1)S(1)}, bf16[512,512]{1,0:T(8,128)(2,1)S(1)}, u32[]{:S(2)}, u32[]{:S(2)}) collective-permute-start(bf16[512,512]{1,0:T(8,128)(2,1)S(1)} %add_convert_fusion.1), channel_id=1, source_target_pairs={{8,0},{12,4},{16,8},{20,12},{24,16},{28,20},{9,1},{13,5},{17,9},{2... | collective-permute-start | bytes 1572872 | tf_op jit(solution)/shard_map/ppermute | solution.py:186
  122.6 17.9 %collective-permute-start.16 = (bf16[512,512]{1,0:T(8,128)(2,1)S(1)}, bf16[512,512]{1,0:T(8,128)(2,1)S(1)}, u32[]{:S(2)}, u32[]{:S(2)}) collective-permute-start(bf16[512,512]{1,0:T(8,128)(2,1)S(1)} %get-tuple-element.41), channel_id=1, source_target_pairs={{0,8},{4,12},{8,16},{12,20},{16,24},{20,28},{1,9},{5,13},{9,17},{1... | collective-permute-start | bytes 1572872 | tf_op jit(solution)/shard_map/ppermute | solution.py:186
  126.6 18.2 %collective-permute-start.20 = (bf16[512,512]{1,0:T(8,128)(2,1)S(1)}, bf16[512,512]{1,0:T(8,128)(2,1)S(1)}, u32[]{:S(2)}, u32[]{:S(2)}) collective-permute-start(bf16[512,512]{1,0:T(8,128)(2,1)S(1)} %get-tuple-element.42), channel_id=1, source_target_pairs={{8,0},{12,4},{16,8},{20,12},{24,16},{28,20},{9,1},{13,5},{17,9},{2... | collective-permute-start | bytes 1572872 | tf_op jit(solution)/shard_map/ppermute | solution.py:186
  133.9 17.3 %collective-permute-start.24 = (bf16[512,512]{1,0:T(8,128)(2,1)S(1)}, bf16[512,512]{1,0:T(8,128)(2,1)S(1)}, u32[]{:S(2)}, u32[]{:S(2)}) collective-permute-start(bf16[512,512]{1,0:T(8,128)(2,1)S(1)} %get-tuple-element.35), channel_id=1, source_target_pairs={{0,8},{4,12},{8,16},{12,20},{16,24},{20,28},{1,9},{5,13},{9,17},{1... | collective-permute-start | bytes 1572872 | tf_op jit(solution)/shard_map/ppermute | solution.py:186
  137.8 18.2 %collective-permute-start.27 = (bf16[512,512]{1,0:T(8,128)(2,1)S(1)}, bf16[512,512]{1,0:T(8,128)(2,1)S(1)}, u32[]{:S(2)}, u32[]{:S(2)}) collective-permute-start(bf16[512,512]{1,0:T(8,128)(2,1)S(1)} %get-tuple-element.36), channel_id=1, source_target_pairs={{8,0},{12,4},{16,8},{20,12},{24,16},{28,20},{9,1},{13,5},{17,9},{2... | collective-permute-start | bytes 1572872 | tf_op jit(solution)/shard_map/ppermute | solution.py:186
  145.2 22.0 %collective-permute-start.21 = (bf16[512,512]{1,0:T(8,128)(2,1)S(1)}, bf16[512,512]{1,0:T(8,128)(2,1)S(1)}, u32[]{:S(2)}, u32[]{:S(2)}) collective-permute-start(bf16[512,512]{1,0:T(8,128)(2,1)S(1)} %get-tuple-element.40), channel_id=1, source_target_pairs={{8,0},{12,4},{16,8},{20,12},{24,16},{28,20},{9,1},{13,5},{17,9},{2... | collective-permute-start | bytes 1572872 | tf_op jit(solution)/shard_map/ppermute | solution.py:186
  146.5 20.7 %collective-permute-start.17 = (bf16[512,512]{1,0:T(8,128)(2,1)S(1)}, bf16[512,512]{1,0:T(8,128)(2,1)S(1)}, u32[]{:S(2)}, u32[]{:S(2)}) collective-permute-start(bf16[512,512]{1,0:T(8,128)(2,1)S(1)} %get-tuple-element.39), channel_id=1, source_target_pairs={{0,8},{4,12},{8,16},{12,20},{16,24},{20,28},{1,9},{5,13},{9,17},{1... | collective-permute-start | bytes 1572872 | tf_op jit(solution)/shard_map/ppermute | solution.py:186
  156.4 19.3 %collective-permute-start.28 = (bf16[512,512]{1,0:T(8,128)(2,1)S(1)}, bf16[512,512]{1,0:T(8,128)(2,1)S(1)}, u32[]{:S(2)}, u32[]{:S(2)}) collective-permute-start(bf16[512,512]{1,0:T(8,128)(2,1)S(1)} %get-tuple-element.34), channel_id=1, source_target_pairs={{8,0},{12,4},{16,8},{20,12},{24,16},{28,20},{9,1},{13,5},{17,9},{2... | collective-permute-start | bytes 1572872 | tf_op jit(solution)/shard_map/ppermute | solution.py:186
  157.7 18.5 %collective-permute-start.25 = (bf16[512,512]{1,0:T(8,128)(2,1)S(1)}, bf16[512,512]{1,0:T(8,128)(2,1)S(1)}, u32[]{:S(2)}, u32[]{:S(2)}) collective-permute-start(bf16[512,512]{1,0:T(8,128)(2,1)S(1)} %get-tuple-element.33), channel_id=1, source_target_pairs={{0,8},{4,12},{8,16},{12,20},{16,24},{20,28},{1,9},{5,13},{9,17},{1... | collective-permute-start | bytes 1572872 | tf_op jit(solution)/shard_map/ppermute | solution.py:186
  163.8 1.4 copy-start
  165.4 1.9 copy-start.12
  165.4 1.9 copy-start.11
  166.7 1.4 copy-start.1
  167.3 14.3 %collective-permute-start.1 = (bf16[64,4096]{1,0:T(8,128)(2,1)S(1)}, bf16[64,4096]{1,0:T(8,128)(2,1)S(1)}, u32[]{:S(2)}, u32[]{:S(2)}) collective-permute-start(bf16[64,4096]{1,0:T(8,128)(2,1)S(1)} %copy-done.12), channel_id=1, source_target_pairs={{0,2},{1,3},{2,0},{3,1},{4,6},{5,7},{6,4},{7,5},{8,10},{9,11},{10,... | collective-permute-start | bytes 1572872 | tf_op jit(solution)/shard_map/ppermute | solution.py:357
  167.3 14.8 %collective-permute-start = (bf16[64,4096]{1,0:T(8,128)(2,1)S(1)}, bf16[64,4096]{1,0:T(8,128)(2,1)S(1)}, u32[]{:S(2)}, u32[]{:S(2)}) collective-permute-start(bf16[64,4096]{1,0:T(8,128)(2,1)S(1)} %copy-done.11), channel_id=1, source_target_pairs={{0,1},{1,2},{2,3},{3,0},{4,5},{5,6},{6,7},{7,4},{8,9},{9,10},{10,1... | collective-permute-start | bytes 1572872 | tf_op jit(solution)/shard_map/ppermute | solution.py:357
  168.0 14.0 %copy-start.7 = (bf16[64,4096]{1,0:T(8,128)(2,1)S(1)}, bf16[64,4096]{1,0:T(8,128)(2,1)}, u32[]{:S(2)}) copy-start(bf16[64,4096]{1,0:T(8,128)(2,1)} %get-tuple-element.18) | copy-start | bytes 1572868
  175.7 14.8 %collective-permute-start.31 = (bf16[512,512]{1,0:T(8,128)(2,1)S(1)}, bf16[512,512]{1,0:T(8,128)(2,1)S(1)}, u32[]{:S(2)}, u32[]{:S(2)}) collective-permute-start(bf16[512,512]{1,0:T(8,128)(2,1)S(1)} %dynamic-slice_convert_fusion.1), channel_id=1, source_target_pairs={{0,4},{4,0},{8,12},{12,8},{16,20},{20,16},{24,28},{28,24},{1,5},{5... | collective-permute-start | bytes 1572872 | tf_op jit(solution)/shard_map/ppermute | solution.py:189
  176.2 25.5 %collective-permute-start.32 = (bf16[512,512]{1,0:T(8,128)(2,1)S(1)}, bf16[512,512]{1,0:T(8,128)(2,1)S(1)}, u32[]{:S(2)}, u32[]{:S(2)}) collective-permute-start(bf16[512,512]{1,0:T(8,128)(2,1)S(1)} %dynamic-slice_convert_fusion), channel_id=1, source_target_pairs={{0,4},{4,0},{8,12},{12,8},{16,20},{20,16},{24,28},{28,24},{1,5},{5... | collective-permute-start | bytes 1572872 | tf_op jit(solution)/shard_map/ppermute | solution.py:189
  178.0 29.0 %collective-permute-start.29 = (bf16[256,512]{1,0:T(8,128)(2,1)S(1)}, bf16[256,512]{1,0:T(8,128)(2,1)S(1)}, u32[]{:S(2)}, u32[]{:S(2)}) collective-permute-start(bf16[256,512]{1,0:T(8,128)(2,1)S(1)} %slice.229), channel_id=1, source_target_pairs={{0,4},{4,0},{8,12},{12,8},{16,20},{20,16},{24,28},{28,24},{1,5},{5... | collective-permute-start | bytes 786440 | tf_op jit(solution)/shard_map/ppermute | solution.py:189
  181.6 27.8 %collective-permute-start.30 = (bf16[256,512]{1,0:T(8,128)(2,1)S(1)}, bf16[256,512]{1,0:T(8,128)(2,1)S(1)}, u32[]{:S(2)}, u32[]{:S(2)}) collective-permute-start(bf16[256,512]{1,0:T(8,128)(2,1)S(1)} %slice.228), channel_id=1, source_target_pairs={{0,4},{4,0},{8,12},{12,8},{16,20},{20,16},{24,28},{28,24},{1,5},{5... | collective-permute-start | bytes 786440 | tf_op jit(solution)/shard_map/ppermute | solution.py:189
  190.5 11.2 %copy-start.5 = (bf16[512,512]{1,0:T(8,128)(2,1)}, bf16[512,512]{1,0:T(8,128)(2,1)S(1)}, u32[]{:S(2)}) copy-start(bf16[512,512]{1,0:T(8,128)(2,1)S(1)} %collective-permute-done.31.refs_2_) | copy-start | bytes 1572868
  201.7 0.8 copy-start.6
  207.0 2.3 %copy-start.8 = (bf16[256,512]{1,0:T(8,128)(2,1)}, bf16[256,512]{1,0:T(8,128)(2,1)S(1)}, u32[]{:S(2)}) copy-start(bf16[256,512]{1,0:T(8,128)(2,1)S(1)} %collective-permute-done.29.refs_2_) | copy-start | bytes 786436
  209.3 0.7 copy-start.9

commit v3 on v2

--- a/solution.py
+++ b/solution.py
@@ -246,7 +246,8 @@
         def gather_grad(g):
             blocks = shifted[: len(groups[0])] if g == 0 else shifted[len(groups[0]) :]
             grad = jnp.stack(blocks)
-            grad = jnp.stack([grad, across_side(grad)], axis=1)
+            got = across_side(grad)
+            grad = jnp.stack([grad, got], axis=1)
             got = [along_cross(grad, k) for k in range(1, cross)]
             rolled = jnp.stack([grad] + got)
             swapped = across_core(rolled)
@@ -272,7 +273,8 @@
         width = half // STREAMS
         keep = lax.dynamic_slice(activation, (0, side * half), (tokens, half))
         give = lax.dynamic_slice(activation, (0, (1 - side) * half), (tokens, half))
-        act = jnp.concatenate([keep, across_side(give)], axis=0)
+        got = across_side(give)
+        act = jnp.concatenate([keep, got], axis=0)
 
         stored_rows = down_weight.shape[0]
         pieces = lax.optimization_barrier(
@@ -343,11 +345,13 @@
                 moving[q] = slot(right, left)
         own, gives = [], []
         for q in range(STREAMS):
-            right, left = moving[q]
-            total_h = part(0, q) + right.astype(f32) + left.astype(f32)
-            own.append(total_h[:tokens])
-            give = total_h[tokens:].astype(bf16)
+            def rows_of(low, high):
+                terms = [part(0, q), *moving[q]]
+                return sum(term[low:high].astype(f32) for term in terms)
+
+            give = rows_of(tokens, 2 * tokens).astype(bf16)
             gives.append(across_side(give))
+            own.append(rows_of(0, tokens))
         weight_grad = merge_weight(index, full, others)
         act_grad = merge_act(index, own, gives, slope)
 

time: 214 us -> 214 us (level)
  local copies, waits for them, and re-layouts: 11.1 us -> 8.94 us
  transfers between devices with their start and end apart: 33 -> 33, of which waited for: 21 -> 22; matrix products, arithmetic and copies ran while one was open for 14% -> 14% of each run, Pallas kernels for 7% -> 7%
where the time goes in v3:
time: 214 us; the launch traced here: 213 us
  waiting for transfers between devices  107 us (50%)
  starting transfers between devices  52.5 us (25%)
  Pallas kernels  18.2 us (9%)
  other arithmetic  15 us (7%)
  matrix products  10.1 us (5%)
  local copies, waits for them, and re-layouts  8.94 us (4%)
    ppermute x17, waiting for transfers between devices, along_line(): return lax.ppermute(value, 'dp', pairs)  56.8 us
    ppermute x9, waiting for transfers between devices, across_side(): return lax.ppermute(value, 'dp', [(i, i ^ 1) for i in range(n_dp)])  43.5 us
    ppermute x17, starting transfers between devices, along_line(): return lax.ppermute(value, 'dp', pairs)  42.5 us
    pallas_call x1, Pallas kernels, attend(): pl.pallas_call(attend_kernel, grid_spec=grid_spec, out_shape=[jax.ShapeDt...  10.6 us
    ppermute x9, starting transfers between devices, across_side(): return lax.ppermute(value, 'dp', [(i, i ^ 1) for i in range(n_dp)])  7.8 us
    dot_general x4, matrix products, weight_grad_of(): lax.dot_general(grads[g].reshape(-1, d_line), chunk, (((0,), (0,)), ((),...  5.16 us
    dot_general x4, matrix products, multiply(): lax.dot_general(grads[g], weights[q], (((2,), (0,)), ((), ())), preferred...  4.98 us
    pallas_call x1, Pallas kernels, merge_weight(): pl.pallas_call(kernel, grid_spec=pltpu.PrefetchScalarGridSpec(num_scalar_...  4.47 us
  transfers between devices with their start and end apart: 33, of which 22 were waited for; matrix products, arithmetic and copies ran while one was open for 14% of the time, Pallas kernels for 7%

profile of v3, /device:TPU:0, one launch (start us, length us, event | category | flops | bytes accessed | tf_op | source)
XLA Modules:
  0.0 213.2 jit_solution(11244678905800866715)
XLA Ops:
  0.7 1.8 constant_dynamic-slice_fusion.1
  2.5 4.1 %collective-permute-start.3 = (bf16[64,1024]{1,0:T(8,128)(2,1)S(1)}, bf16[64,1024]{1,0:T(8,128)(2,1)S(1)}, u32[]{:S(2)}, u32[]{:S(2)}) collective-permute-start(bf16[64,1024]{1,0:T(8,128)(2,1)S(1)} %get-tuple-element.77), channel_id=1, source_target_pairs={{0,16},{4,20},{8,24},{12,28},{16,0},{20,4},{24,8},{28,12},{1,17},{... | collective-permute-start | bytes 393224 | tf_op jit(solution)/shard_map/ppermute | solution.py:186
  6.6 6.3 %collective-permute-done.3 = bf16[64,1024]{1,0:T(8,128)(2,1)S(1)} collective-permute-done((bf16[64,1024]{1,0:T(8,128)(2,1)S(1)}, bf16[64,1024]{1,0:T(8,128)(2,1)S(1)}, u32[]{:S(2)}, u32[]{:S(2)}) %collective-permute-start.3) | collective-permute-done | bytes 131104 | tf_op jit(solution)/shard_map/ppermute | solution.py:186
  12.9 1.6 collective-permute-start.4
  14.6 1.3 reshape_squeeze.3.labels_ref
  15.9 10.6 %attend.1 = (bf16[64,4096]{1,0:T(8,128)(2,1)}, bf16[64,4096]{1,0:T(8,128)(2,1)}, bf16[64,4096]{1,0:T(8,128)(2,1)}, bf16[64,4096]{1,0:T(8,128)(2,1)}) custom-call(s32[1]{0:T(128)} %bitcast.place_ref, bf16[3,256,1024]{2,1,0:T(8,128)(2,1)} %qkv_ref.1, s32[1,256]{1,0:T(1,128)} %reshape_squeeze.3.labels_ref, bf16[4096,1024]{1,0:T(8,128)(2,1)} %weight_ref.1), custom_call_target="tpu_custom_call" | custom-call | flops 2415919104 | bytes 12058624 | tf_op jit(solution)/shard_map/attend/pallas_call | solution.py:84
  26.5 4.3 %collective-permute-start.11 = (bf16[64,1024]{1,0:T(8,128)(2,1)}, bf16[64,1024]{1,0:T(8,128)(2,1)S(1)}, u32[]{:S(2)}, u32[]{:S(2)}) collective-permute-start(bf16[64,1024]{1,0:T(8,128)(2,1)} %get-tuple-element.78), channel_id=1, source_target_pairs={{0,24},{4,28},{8,0},{12,4},{16,8},{20,12},{24,16},{28,20},{1,25},{... | collective-permute-start | bytes 393224 | tf_op jit(solution)/shard_map/ppermute | solution.py:186
  30.8 0.9 fusion.56
  31.7 0.7 collective-permute-start.5
  32.4 2.0 fusion.6
  34.4 0.9 constant_dynamic-slice_fusion.3
  35.8 1.8 collective-permute-done.10
  38.2 2.9 %constant_dynamic-slice_fusion.4 = (bf16[512,512]{1,0:T(8,128)(2,1)}, bf16[512,512]{1,0:T(8,128)(2,1)}, bf16[512,512]{1,0:T(8,128)(2,1)}, bf16[512,512]{1,0:T(8,128)(2,1)}) fusion(bf16[512,2048]{1,0:T(8,128)(2,1)} %param.13, s32[]{:T(128)S(6)} %select_n.344, s32[]{:T(128)S(6)} %select_n.342, s32[]{:T(128)S(6)} %select_n.341, s32[]{:T(128)S(6)} %select_n.343), kind=kLoop, calls=%fused_computation.123 | loop fusion | bytes 4194320 | tf_op jit(solution)/shard_map/dynamic_slice | solution.py:282
  41.1 1.5 collective-permute-start.7
  42.6 4.0 %collective-permute-done.5 = bf16[2,2,64,1024]{3,2,1,0:T(8,128)(2,1)S(1)} collective-permute-done((bf16[2,2,64,1024]{3,2,1,0:T(8,128)(2,1)}, bf16[2,2,64,1024]{3,2,1,0:T(8,128)(2,1)S(1)}, u32[]{:S(2)}, u32[]{:S(2)}) %collective-permute-start.5) | collective-permute-done | bytes 524320 | tf_op jit(solution)/shard_map/ppermute | solution.py:195
  47.2 8.7 %collective-permute-done.12 = bf16[2,64,1024]{2,1,0:T(8,128)(2,1)S(1)} collective-permute-done((bf16[2,64,1024]{2,1,0:T(8,128)(2,1)S(1)}, bf16[2,64,1024]{2,1,0:T(8,128)(2,1)S(1)}, u32[]{:S(2)}, u32[]{:S(2)}) %collective-permute-start.12) | collective-permute-done | bytes 262176 | tf_op jit(solution)/shard_map/ppermute | solution.py:189
  56.0 1.4 collective-permute-start.13
  57.4 1.2 pad_maximum_fusion.2
  58.6 1.2 fusion.34
  59.7 7.5 %collective-permute-done.7 = bf16[512,512]{1,0:T(8,128)(2,1)} collective-permute-done((bf16[512,512]{1,0:T(8,128)(2,1)}, bf16[512,512]{1,0:T(8,128)(2,1)}, u32[]{:S(2)}, u32[]{:S(2)}) %collective-permute-start.7) | collective-permute-done | bytes 524320 | tf_op jit(solution)/shard_map/ppermute | solution.py:189
  67.3 1.3 collective-permute-start.9
  68.6 1.1 broadcast_select_fusion.9
  69.8 7.6 %collective-permute-done.22 = bf16[512,512]{1,0:T(8,128)(2,1)S(1)} collective-permute-done((bf16[512,512]{1,0:T(8,128)(2,1)}, bf16[512,512]{1,0:T(8,128)(2,1)S(1)}, u32[]{:S(2)}, u32[]{:S(2)}) %collective-permute-start.22) | collective-permute-done | bytes 524320 | tf_op jit(solution)/shard_map/ppermute | solution.py:189
  77.3 1.3 collective-permute-start.18
  79.7 1.2 fusion.32
  82.1 1.3 fusion.31
  83.4 6.0 %collective-permute-done.9 = bf16[512,1024]{1,0:T(8,128)(2,1)S(1)} collective-permute-done((bf16[512,1024]{1,0:T(8,128)(2,1)S(1)}, bf16[512,1024]{1,0:T(8,128)(2,1)S(1)}, u32[]{:S(2)}, u32[]{:S(2)}) %collective-permute-start.9) | collective-permute-done | bytes 1048608 | tf_op jit(solution)/shard_map/ppermute | solution.py:186
  89.3 13.9 %collective-permute-done.18 = bf16[512,1024]{1,0:T(8,128)(2,1)S(1)} collective-permute-done((bf16[512,1024]{1,0:T(8,128)(2,1)S(1)}, bf16[512,1024]{1,0:T(8,128)(2,1)S(1)}, u32[]{:S(2)}, u32[]{:S(2)}) %collective-permute-start.18) | collective-permute-done | bytes 1048608 | tf_op jit(solution)/shard_map/ppermute | solution.py:186
  103.7 1.5 collective-permute-start.15
  105.2 1.3 collective-permute-start.19
  106.5 1.2 fusion.29
  108.1 5.0 %collective-permute-start.23 = (bf16[512,512]{1,0:T(8,128)(2,1)S(1)}, bf16[512,512]{1,0:T(8,128)(2,1)S(1)}, u32[]{:S(2)}, u32[]{:S(2)}) collective-permute-start(bf16[512,512]{1,0:T(8,128)(2,1)S(1)} %add_convert_fusion.3), channel_id=1, source_target_pairs={{0,8},{4,12},{8,16},{12,20},{16,24},{20,28},{1,9},{5,13},{9,17},{1... | collective-permute-start | bytes 1572872 | tf_op jit(solution)/shard_map/ppermute | solution.py:186
  113.4 1.3 collective-permute-start.26
  114.7 1.2 fusion.30
  115.9 1.5 collective-permute-done.15
  117.5 4.9 %collective-permute-done.19 = bf16[512,512]{1,0:T(8,128)(2,1)S(1)} collective-permute-done((bf16[512,512]{1,0:T(8,128)(2,1)S(1)}, bf16[512,512]{1,0:T(8,128)(2,1)S(1)}, u32[]{:S(2)}, u32[]{:S(2)}) %collective-permute-start.19) | collective-permute-done | bytes 524320 | tf_op jit(solution)/shard_map/ppermute | solution.py:186
  122.6 4.0 %collective-permute-start.16 = (bf16[512,512]{1,0:T(8,128)(2,1)S(1)}, bf16[512,512]{1,0:T(8,128)(2,1)S(1)}, u32[]{:S(2)}, u32[]{:S(2)}) collective-permute-start(bf16[512,512]{1,0:T(8,128)(2,1)S(1)} %get-tuple-element.45), channel_id=1, source_target_pairs={{0,8},{4,12},{8,16},{12,20},{16,24},{20,28},{1,9},{5,13},{9,17},{1... | collective-permute-start | bytes 1572872 | tf_op jit(solution)/shard_map/ppermute | solution.py:186
  126.6 1.5 collective-permute-start.20
  128.7 4.9 %collective-permute-done.26 = bf16[512,512]{1,0:T(8,128)(2,1)S(1)} collective-permute-done((bf16[512,512]{1,0:T(8,128)(2,1)S(1)}, bf16[512,512]{1,0:T(8,128)(2,1)S(1)}, u32[]{:S(2)}, u32[]{:S(2)}) %collective-permute-start.26) | collective-permute-done | bytes 524320 | tf_op jit(solution)/shard_map/ppermute | solution.py:186
  133.9 4.0 %collective-permute-start.24 = (bf16[512,512]{1,0:T(8,128)(2,1)S(1)}, bf16[512,512]{1,0:T(8,128)(2,1)S(1)}, u32[]{:S(2)}, u32[]{:S(2)}) collective-permute-start(bf16[512,512]{1,0:T(8,128)(2,1)S(1)} %get-tuple-element.39), channel_id=1, source_target_pairs={{0,8},{4,12},{8,16},{12,20},{16,24},{20,28},{1,9},{5,13},{9,17},{1... | collective-permute-start | bytes 1572872 | tf_op jit(solution)/shard_map/ppermute | solution.py:186
  137.8 1.3 collective-permute-start.27
  139.2 1.3 fusion.10
  140.6 4.2 %collective-permute-done.20 = bf16[512,512]{1,0:T(8,128)(2,1)S(1)} collective-permute-done((bf16[512,512]{1,0:T(8,128)(2,1)S(1)}, bf16[512,512]{1,0:T(8,128)(2,1)S(1)}, u32[]{:S(2)}, u32[]{:S(2)}) %collective-permute-start.20) | collective-permute-done | bytes 524320 | tf_op jit(solution)/shard_map/ppermute | solution.py:186
  145.2 1.3 collective-permute-start.21
  146.5 4.6 %collective-permute-start.17 = (bf16[512,512]{1,0:T(8,128)(2,1)S(1)}, bf16[512,512]{1,0:T(8,128)(2,1)S(1)}, u32[]{:S(2)}, u32[]{:S(2)}) collective-permute-start(bf16[512,512]{1,0:T(8,128)(2,1)S(1)} %get-tuple-element.43), channel_id=1, source_target_pairs={{0,8},{4,12},{8,16},{12,20},{16,24},{20,28},{1,9},{5,13},{9,17},{1... | collective-permute-start | bytes 1572872 | tf_op jit(solution)/shard_map/ppermute | solution.py:186
  151.2 4.9 %collective-permute-done.27 = bf16[512,512]{1,0:T(8,128)(2,1)S(1)} collective-permute-done((bf16[512,512]{1,0:T(8,128)(2,1)S(1)}, bf16[512,512]{1,0:T(8,128)(2,1)S(1)}, u32[]{:S(2)}, u32[]{:S(2)}) %collective-permute-start.27) | collective-permute-done | bytes 524320 | tf_op jit(solution)/shard_map/ppermute | solution.py:186
  156.4 1.3 collective-permute-start.28
  157.7 4.6 %collective-permute-start.25 = (bf16[512,512]{1,0:T(8,128)(2,1)S(1)}, bf16[512,512]{1,0:T(8,128)(2,1)S(1)}, u32[]{:S(2)}, u32[]{:S(2)}) collective-permute-start(bf16[512,512]{1,0:T(8,128)(2,1)S(1)} %get-tuple-element.37), channel_id=1, source_target_pairs={{0,8},{4,12},{8,16},{12,20},{16,24},{20,28},{1,9},{5,13},{9,17},{1... | collective-permute-start | bytes 1572872 | tf_op jit(solution)/shard_map/ppermute | solution.py:186
  162.6 1.3 add_multiply_fusion.1.refs_0_
  164.0 1.3 fusion.17
  165.4 1.3 add_multiply_fusion.refs_1_
  167.3 1.0 fusion.40
  168.4 7.3 %collective-permute-done.28 = bf16[512,512]{1,0:T(8,128)(2,1)S(1)} collective-permute-done((bf16[512,512]{1,0:T(8,128)(2,1)S(1)}, bf16[512,512]{1,0:T(8,128)(2,1)S(1)}, u32[]{:S(2)}, u32[]{:S(2)}) %collective-permute-start.28) | collective-permute-done | bytes 524320 | tf_op jit(solution)/shard_map/ppermute | solution.py:186
  176.2 1.5 collective-permute-start.32
  177.7 1.1 fusion.37
  179.3 2.2 %collective-permute-done.1 = bf16[64,4096]{1,0:T(8,128)(2,1)S(1)} collective-permute-done((bf16[64,4096]{1,0:T(8,128)(2,1)S(1)}, bf16[64,4096]{1,0:T(8,128)(2,1)S(1)}, u32[]{:S(2)}, u32[]{:S(2)}) %collective-permute-start.1) | collective-permute-done | bytes 524320 | tf_op jit(solution)/shard_map/ppermute | solution.py:361
  182.1 2.3 %add_add_fusion = f32[64,4096]{1,0:T(8,128)} fusion(bf16[64,4096]{1,0:T(8,128)(2,1)} %collective-permute-done.2, bf16[64,4096]{1,0:T(8,128)(2,1)S(1)} %collective-permute-done.1, bf16[64,4096]{1,0:T(8,128)(2,1)S(1)} %collective-permute-done, bf16[64,4096]{1,0:T(8,128)(2,1)S(1)} %copy-done.7, f32[4096]{0:T(1024)S(1)} %convert_element_type.133), kind=kLoop, calls=%fused_computation.63 | loop fusion | flops 2097152 | bytes 3162112 | tf_op jit(solution)/shard_map/add | solution.py:362
  184.4 6.1 %collective-permute-done.31.refs_2_ = bf16[512,512]{1,0:T(8,128)(2,1)S(1)} collective-permute-done((bf16[512,512]{1,0:T(8,128)(2,1)S(1)}, bf16[512,512]{1,0:T(8,128)(2,1)S(1)}, u32[]{:S(2)}, u32[]{:S(2)}) %collective-permute-start.31) | collective-permute-done | bytes 524320 | tf_op jit(solution)/shard_map/ppermute | solution.py:189
  190.5 11.2 %collective-permute-done.32.refs_3_ = bf16[512,512]{1,0:T(8,128)(2,1)S(1)} collective-permute-done((bf16[512,512]{1,0:T(8,128)(2,1)S(1)}, bf16[512,512]{1,0:T(8,128)(2,1)S(1)}, u32[]{:S(2)}, u32[]{:S(2)}) %collective-permute-start.32) | collective-permute-done | bytes 524320 | tf_op jit(solution)/shard_map/ppermute | solution.py:189
  201.7 0.8 copy-done.6
  202.5 4.5 %merge_weight.1 = f32[512,2048]{1,0:T(8,128)} custom-call(s32[1]{0:T(128)} %bitcast.1.index_ref, f32[1024,512]{1,0:T(8,128)} %copy-done, f32[1024,512]{1,0:T(8,128)} %copy-done.1, bf16[512,512]{1,0:T(8,128)(2,1)} %copy-done.5, bf16[512,512]{1,0:T(8,128)(2,1)} %copy-done.6), custom_call_target="tpu_custom_call" | custom-call | tf_op jit(solution)/shard_map/merge_weight/pallas_call | solution.py:121
  207.0 2.3 %collective-permute-done.30.refs_3_ = bf16[256,512]{1,0:T(8,128)(2,1)S(1)} collective-permute-done((bf16[256,512]{1,0:T(8,128)(2,1)}, bf16[256,512]{1,0:T(8,128)(2,1)S(1)}, u32[]{:S(2)}, u32[]{:S(2)}) %collective-permute-start.30) | collective-permute-done | bytes 262176 | tf_op jit(solution)/shard_map/ppermute | solution.py:189
  209.3 0.7 copy-done.9
  210.0 3.2 %merge_act.1 = f32[256,2048]{1,0:T(8,128)} custom-call(s32[1]{0:T(128)} %bitcast.1.index_ref, f32[256,512]{1,0:T(8,128)} %get-tuple-element.36.refs_0_, f32[256,512]{1,0:T(8,128)} %get-tuple-element.34.refs_1_, bf16[256,512]{1,0:T(8,128)(2,1)} %copy-done.8, bf16[256,512]{1,0:T(8,128)(2,1)} %copy-done.9, f32[256,2048]{1,0:T(8,128)} %get-tuple-element.29.refs_4_), custom_call_target="tpu_custom_call" | custom-call | tf_op jit(solution)/shard_map/merge_act/pallas_call | solution.py:161
  (81 shorter events, 10.0 us)
Async XLA Ops:
  2.5 10.4 %collective-permute-start.3 = (bf16[64,1024]{1,0:T(8,128)(2,1)S(1)}, bf16[64,1024]{1,0:T(8,128)(2,1)S(1)}, u32[]{:S(2)}, u32[]{:S(2)}) collective-permute-start(bf16[64,1024]{1,0:T(8,128)(2,1)S(1)} %get-tuple-element.77), channel_id=1, source_target_pairs={{0,16},{4,20},{8,24},{12,28},{16,0},{20,4},{24,8},{28,12},{1,17},{... | collective-permute-start | bytes 393224 | tf_op jit(solution)/shard_map/ppermute | solution.py:186
  12.9 17.9 %collective-permute-start.4 = (bf16[2,64,1024]{2,1,0:T(8,128)(2,1)S(1)}, bf16[2,64,1024]{2,1,0:T(8,128)(2,1)S(1)}, u32[]{:S(2)}, u32[]{:S(2)}) collective-permute-start(bf16[2,64,1024]{2,1,0:T(8,128)(2,1)S(1)} %get-tuple-element.84), channel_id=1, source_target_pairs={{0,4},{4,0},{8,12},{12,8},{16,20},{20,16},{24,28},{28,24},{1,5},{5... | collective-permute-start | bytes 786440 | tf_op jit(solution)/shard_map/ppermute | solution.py:189
  26.5 5.9 %copy-start.4 = (bf16[256,2048]{1,0:T(8,128)(2,1)S(1)}, bf16[256,2048]{1,0:T(8,128)(2,1)}, u32[]{:S(2)}) copy-start(bf16[256,2048]{1,0:T(8,128)(2,1)} %param.12) | copy-start | bytes 3145732
  26.5 152.3 %collective-permute-start.2 = (bf16[64,4096]{1,0:T(8,128)(2,1)}, bf16[64,4096]{1,0:T(8,128)(2,1)}, u32[]{:S(2)}, u32[]{:S(2)}) collective-permute-start(bf16[64,4096]{1,0:T(8,128)(2,1)} %get-tuple-element.21), channel_id=1, source_target_pairs={{0,3},{1,0},{2,1},{3,2},{4,7},{5,4},{6,5},{7,6},{8,11},{9,8},{10,9... | collective-permute-start | bytes 1572872 | tf_op jit(solution)/shard_map/ppermute | solution.py:361
  26.5 9.3 %collective-permute-start.11 = (bf16[64,1024]{1,0:T(8,128)(2,1)}, bf16[64,1024]{1,0:T(8,128)(2,1)S(1)}, u32[]{:S(2)}, u32[]{:S(2)}) collective-permute-start(bf16[64,1024]{1,0:T(8,128)(2,1)} %get-tuple-element.78), channel_id=1, source_target_pairs={{0,24},{4,28},{8,0},{12,4},{16,8},{20,12},{24,16},{28,20},{1,25},{... | collective-permute-start | bytes 393224 | tf_op jit(solution)/shard_map/ppermute | solution.py:186
  30.8 6.8 %collective-permute-start.10 = (bf16[64,1024]{1,0:T(8,128)(2,1)S(1)}, bf16[64,1024]{1,0:T(8,128)(2,1)S(1)}, u32[]{:S(2)}, u32[]{:S(2)}) collective-permute-start(bf16[64,1024]{1,0:T(8,128)(2,1)S(1)} %get-tuple-element.75), channel_id=1, source_target_pairs={{0,8},{4,12},{8,16},{12,20},{16,24},{20,28},{24,0},{28,4},{1,9},{5... | collective-permute-start | bytes 393224 | tf_op jit(solution)/shard_map/ppermute | solution.py:186
  31.7 14.9 %collective-permute-start.5 = (bf16[2,2,64,1024]{3,2,1,0:T(8,128)(2,1)}, bf16[2,2,64,1024]{3,2,1,0:T(8,128)(2,1)S(1)}, u32[]{:S(2)}, u32[]{:S(2)}) collective-permute-start(bf16[2,2,64,1024]{3,2,1,0:T(8,128)(2,1)} %get-tuple-element.80), channel_id=1, source_target_pairs={{0,2},{1,3},{2,0},{3,1},{4,6},{5,7},{6,4},{7,5},{8,10},{9,11},{10,... | collective-permute-start | bytes 1572872 | tf_op jit(solution)/shard_map/ppermute | solution.py:195
  35.3 20.7 %collective-permute-start.8 = (bf16[256,1024]{1,0:T(8,128)(2,1)}, bf16[256,1024]{1,0:T(8,128)(2,1)}, u32[]{:S(2)}, u32[]{:S(2)}) collective-permute-start(bf16[256,1024]{1,0:T(8,128)(2,1)} %get-tuple-element.68), channel_id=1, source_target_pairs={{0,4},{4,0},{8,12},{12,8},{16,20},{20,16},{24,28},{28,24},{1,5},{5... | collective-permute-start | bytes 1572872 | tf_op jit(solution)/shard_map/ppermute | solution.py:189
  37.6 5.0 %copy-start.10 = (bf16[4096]{0:T(1024)(128)(2,1)S(1)}, bf16[4096]{0:T(1024)(128)(2,1)}, u32[]{:S(2)}) copy-start(bf16[4096]{0:T(1024)(128)(2,1)} %param.10) | copy-start | bytes 24580
  37.6 18.3 %collective-permute-start.12 = (bf16[2,64,1024]{2,1,0:T(8,128)(2,1)S(1)}, bf16[2,64,1024]{2,1,0:T(8,128)(2,1)S(1)}, u32[]{:S(2)}, u32[]{:S(2)}) collective-permute-start(bf16[2,64,1024]{2,1,0:T(8,128)(2,1)S(1)} %get-tuple-element.82), channel_id=1, source_target_pairs={{0,4},{4,0},{8,12},{12,8},{16,20},{20,16},{24,28},{28,24},{1,5},{5... | collective-permute-start | bytes 786440 | tf_op jit(solution)/shard_map/ppermute | solution.py:189
  41.1 26.2 %collective-permute-start.7 = (bf16[512,512]{1,0:T(8,128)(2,1)}, bf16[512,512]{1,0:T(8,128)(2,1)}, u32[]{:S(2)}, u32[]{:S(2)}) collective-permute-start(bf16[512,512]{1,0:T(8,128)(2,1)} %get-tuple-element.23), channel_id=1, source_target_pairs={{0,4},{4,0},{8,12},{12,8},{16,20},{20,16},{24,28},{28,24},{1,5},{5... | collective-permute-start | bytes 1572872 | tf_op jit(solution)/shard_map/ppermute | solution.py:189
  46.6 30.7 %collective-permute-start.22 = (bf16[512,512]{1,0:T(8,128)(2,1)}, bf16[512,512]{1,0:T(8,128)(2,1)S(1)}, u32[]{:S(2)}, u32[]{:S(2)}) collective-permute-start(bf16[512,512]{1,0:T(8,128)(2,1)} %get-tuple-element.26), channel_id=1, source_target_pairs={{0,4},{4,0},{8,12},{12,8},{16,20},{20,16},{24,28},{28,24},{1,5},{5... | collective-permute-start | bytes 1572872 | tf_op jit(solution)/shard_map/ppermute | solution.py:189
  55.9 23.0 %collective-permute-start.6 = (bf16[2,2,2,64,1024]{4,3,2,1,0:T(8,128)(2,1)S(1)}, bf16[2,2,2,64,1024]{4,3,2,1,0:T(8,128)(2,1)S(1)}, u32[]{:S(2)}, u32[]{:S(2)}) collective-permute-start(bf16[2,2,2,64,1024]{4,3,2,1,0:T(8,128)(2,1)S(1)} %pad_maximum_fusion.3), channel_id=1, source_target_pairs={{0,1},{1,0},{2,3},{3,2},{4,5},{5,4},{6,7},{7,6},{8,9},{9,8},{10,11... | collective-permute-start | bytes 3145736 | tf_op jit(solution)/shard_map/ppermute | solution.py:192
  56.0 22.7 %collective-permute-start.13 = (bf16[2,2,64,1024]{3,2,1,0:T(8,128)(2,1)S(1)}, bf16[2,2,64,1024]{3,2,1,0:T(8,128)(2,1)S(1)}, u32[]{:S(2)}, u32[]{:S(2)}) collective-permute-start(bf16[2,2,64,1024]{3,2,1,0:T(8,128)(2,1)S(1)} %get-tuple-element.74), channel_id=1, source_target_pairs={{0,2},{1,3},{2,0},{3,1},{4,6},{5,7},{6,4},{7,5},{8,10},{9,11},{10,... | collective-permute-start | bytes 1572872 | tf_op jit(solution)/shard_map/ppermute | solution.py:195
  57.4 11.2 %copy-start.3 = (bf16[512,512]{1,0:T(8,128)(2,1)S(1)}, bf16[512,512]{1,0:T(8,128)(2,1)}, u32[]{:S(2)}) copy-start(bf16[512,512]{1,0:T(8,128)(2,1)} %get-tuple-element.22) | copy-start | bytes 1572868
  58.6 20.0 %copy-start.2 = (bf16[512,512]{1,0:T(8,128)(2,1)S(1)}, bf16[512,512]{1,0:T(8,128)(2,1)}, u32[]{:S(2)}) copy-start(bf16[512,512]{1,0:T(8,128)(2,1)} %get-tuple-element.25) | copy-start | bytes 1572868
  67.3 22.1 %collective-permute-start.9 = (bf16[512,1024]{1,0:T(8,128)(2,1)S(1)}, bf16[512,1024]{1,0:T(8,128)(2,1)S(1)}, u32[]{:S(2)}, u32[]{:S(2)}) collective-permute-start(bf16[512,1024]{1,0:T(8,128)(2,1)S(1)} %pad_maximum_fusion.2), channel_id=1, source_target_pairs={{0,8},{4,12},{8,16},{12,20},{16,24},{20,28},{1,9},{5,13},{9,17},{1... | collective-permute-start | bytes 3145736 | tf_op jit(solution)/shard_map/ppermute | solution.py:186
  77.3 26.0 %collective-permute-start.18 = (bf16[512,1024]{1,0:T(8,128)(2,1)S(1)}, bf16[512,1024]{1,0:T(8,128)(2,1)S(1)}, u32[]{:S(2)}, u32[]{:S(2)}) collective-permute-start(bf16[512,1024]{1,0:T(8,128)(2,1)S(1)} %pad_maximum_fusion.2), channel_id=1, source_target_pairs={{8,0},{12,4},{16,8},{20,12},{24,16},{28,20},{9,1},{13,5},{17,9},{2... | collective-permute-start | bytes 3145736 | tf_op jit(solution)/shard_map/ppermute | solution.py:186
  78.8 2.7 %collective-permute-start.14 = (bf16[2,2,2,64,1024]{4,3,2,1,0:T(8,128)(2,1)S(1)}, bf16[2,2,2,64,1024]{4,3,2,1,0:T(8,128)(2,1)S(1)}, u32[]{:S(2)}, u32[]{:S(2)}) collective-permute-start(bf16[2,2,2,64,1024]{4,3,2,1,0:T(8,128)(2,1)S(1)} %pad_maximum_fusion.4), channel_id=1, source_target_pairs={{0,1},{1,0},{2,3},{3,2},{4,5},{5,4},{6,7},{7,6},{8,9},{9,8},{10,11... | collective-permute-start | bytes 3145736 | tf_op jit(solution)/shard_map/ppermute | solution.py:192
  103.7 13.8 %collective-permute-start.15 = (bf16[512,512]{1,0:T(8,128)(2,1)S(1)}, bf16[512,512]{1,0:T(8,128)(2,1)S(1)}, u32[]{:S(2)}, u32[]{:S(2)}) collective-permute-start(bf16[512,512]{1,0:T(8,128)(2,1)S(1)} %get-tuple-element.47), channel_id=1, source_target_pairs={{0,8},{4,12},{8,16},{12,20},{16,24},{20,28},{1,9},{5,13},{9,17},{1... | collective-permute-start | bytes 1572872 | tf_op jit(solution)/shard_map/ppermute | solution.py:186
  105.2 17.1 %collective-permute-start.19 = (bf16[512,512]{1,0:T(8,128)(2,1)S(1)}, bf16[512,512]{1,0:T(8,128)(2,1)S(1)}, u32[]{:S(2)}, u32[]{:S(2)}) collective-permute-start(bf16[512,512]{1,0:T(8,128)(2,1)S(1)} %get-tuple-element.48), channel_id=1, source_target_pairs={{8,0},{12,4},{16,8},{20,12},{24,16},{28,20},{9,1},{13,5},{17,9},{2... | collective-permute-start | bytes 1572872 | tf_op jit(solution)/shard_map/ppermute | solution.py:186
  108.1 20.6 %collective-permute-start.23 = (bf16[512,512]{1,0:T(8,128)(2,1)S(1)}, bf16[512,512]{1,0:T(8,128)(2,1)S(1)}, u32[]{:S(2)}, u32[]{:S(2)}) collective-permute-start(bf16[512,512]{1,0:T(8,128)(2,1)S(1)} %add_convert_fusion.3), channel_id=1, source_target_pairs={{0,8},{4,12},{8,16},{12,20},{16,24},{20,28},{1,9},{5,13},{9,17},{1... | collective-permute-start | bytes 1572872 | tf_op jit(solution)/shard_map/ppermute | solution.py:186
  113.4 20.2 %collective-permute-start.26 = (bf16[512,512]{1,0:T(8,128)(2,1)S(1)}, bf16[512,512]{1,0:T(8,128)(2,1)S(1)}, u32[]{:S(2)}, u32[]{:S(2)}) collective-permute-start(bf16[512,512]{1,0:T(8,128)(2,1)S(1)} %add_convert_fusion.1), channel_id=1, source_target_pairs={{8,0},{12,4},{16,8},{20,12},{24,16},{28,20},{9,1},{13,5},{17,9},{2... | collective-permute-start | bytes 1572872 | tf_op jit(solution)/shard_map/ppermute | solution.py:186
  122.6 18.0 %collective-permute-start.16 = (bf16[512,512]{1,0:T(8,128)(2,1)S(1)}, bf16[512,512]{1,0:T(8,128)(2,1)S(1)}, u32[]{:S(2)}, u32[]{:S(2)}) collective-permute-start(bf16[512,512]{1,0:T(8,128)(2,1)S(1)} %get-tuple-element.45), channel_id=1, source_target_pairs={{0,8},{4,12},{8,16},{12,20},{16,24},{20,28},{1,9},{5,13},{9,17},{1... | collective-permute-start | bytes 1572872 | tf_op jit(solution)/shard_map/ppermute | solution.py:186
  126.6 18.2 %collective-permute-start.20 = (bf16[512,512]{1,0:T(8,128)(2,1)S(1)}, bf16[512,512]{1,0:T(8,128)(2,1)S(1)}, u32[]{:S(2)}, u32[]{:S(2)}) collective-permute-start(bf16[512,512]{1,0:T(8,128)(2,1)S(1)} %get-tuple-element.46), channel_id=1, source_target_pairs={{8,0},{12,4},{16,8},{20,12},{24,16},{28,20},{9,1},{13,5},{17,9},{2... | collective-permute-start | bytes 1572872 | tf_op jit(solution)/shard_map/ppermute | solution.py:186
  133.9 17.3 %collective-permute-start.24 = (bf16[512,512]{1,0:T(8,128)(2,1)S(1)}, bf16[512,512]{1,0:T(8,128)(2,1)S(1)}, u32[]{:S(2)}, u32[]{:S(2)}) collective-permute-start(bf16[512,512]{1,0:T(8,128)(2,1)S(1)} %get-tuple-element.39), channel_id=1, source_target_pairs={{0,8},{4,12},{8,16},{12,20},{16,24},{20,28},{1,9},{5,13},{9,17},{1... | collective-permute-start | bytes 1572872 | tf_op jit(solution)/shard_map/ppermute | solution.py:186
  137.8 18.2 %collective-permute-start.27 = (bf16[512,512]{1,0:T(8,128)(2,1)S(1)}, bf16[512,512]{1,0:T(8,128)(2,1)S(1)}, u32[]{:S(2)}, u32[]{:S(2)}) collective-permute-start(bf16[512,512]{1,0:T(8,128)(2,1)S(1)} %get-tuple-element.40), channel_id=1, source_target_pairs={{8,0},{12,4},{16,8},{20,12},{24,16},{28,20},{9,1},{13,5},{17,9},{2... | collective-permute-start | bytes 1572872 | tf_op jit(solution)/shard_map/ppermute | solution.py:186
  145.2 22.1 %collective-permute-start.21 = (bf16[512,512]{1,0:T(8,128)(2,1)S(1)}, bf16[512,512]{1,0:T(8,128)(2,1)S(1)}, u32[]{:S(2)}, u32[]{:S(2)}) collective-permute-start(bf16[512,512]{1,0:T(8,128)(2,1)S(1)} %get-tuple-element.44), channel_id=1, source_target_pairs={{8,0},{12,4},{16,8},{20,12},{24,16},{28,20},{9,1},{13,5},{17,9},{2... | collective-permute-start | bytes 1572872 | tf_op jit(solution)/shard_map/ppermute | solution.py:186
  146.5 20.8 %collective-permute-start.17 = (bf16[512,512]{1,0:T(8,128)(2,1)S(1)}, bf16[512,512]{1,0:T(8,128)(2,1)S(1)}, u32[]{:S(2)}, u32[]{:S(2)}) collective-permute-start(bf16[512,512]{1,0:T(8,128)(2,1)S(1)} %get-tuple-element.43), channel_id=1, source_target_pairs={{0,8},{4,12},{8,16},{12,20},{16,24},{20,28},{1,9},{5,13},{9,17},{1... | collective-permute-start | bytes 1572872 | tf_op jit(solution)/shard_map/ppermute | solution.py:186
  156.4 19.3 %collective-permute-start.28 = (bf16[512,512]{1,0:T(8,128)(2,1)S(1)}, bf16[512,512]{1,0:T(8,128)(2,1)S(1)}, u32[]{:S(2)}, u32[]{:S(2)}) collective-permute-start(bf16[512,512]{1,0:T(8,128)(2,1)S(1)} %get-tuple-element.38), channel_id=1, source_target_pairs={{8,0},{12,4},{16,8},{20,12},{24,16},{28,20},{9,1},{13,5},{17,9},{2... | collective-permute-start | bytes 1572872 | tf_op jit(solution)/shard_map/ppermute | solution.py:186
  157.7 18.5 %collective-permute-start.25 = (bf16[512,512]{1,0:T(8,128)(2,1)S(1)}, bf16[512,512]{1,0:T(8,128)(2,1)S(1)}, u32[]{:S(2)}, u32[]{:S(2)}) collective-permute-start(bf16[512,512]{1,0:T(8,128)(2,1)S(1)} %get-tuple-element.37), channel_id=1, source_target_pairs={{0,8},{4,12},{8,16},{12,20},{16,24},{20,28},{1,9},{5,13},{9,17},{1... | collective-permute-start | bytes 1572872 | tf_op jit(solution)/shard_map/ppermute | solution.py:186
  163.9 1.4 copy-start
  165.4 1.9 copy-start.12
  165.4 1.9 copy-start.11
  166.7 12.1 %copy-start.1 = (f32[1024,512]{1,0:T(8,128)}, f32[1024,512]{1,0:T(8,128)S(1)}, u32[]{:S(2)}) copy-start(f32[1024,512]{1,0:T(8,128)S(1)} %add_multiply_fusion.refs_1_) | copy-start | bytes 6291460
  167.3 14.3 %collective-permute-start.1 = (bf16[64,4096]{1,0:T(8,128)(2,1)S(1)}, bf16[64,4096]{1,0:T(8,128)(2,1)S(1)}, u32[]{:S(2)}, u32[]{:S(2)}) collective-permute-start(bf16[64,4096]{1,0:T(8,128)(2,1)S(1)} %copy-done.12), channel_id=1, source_target_pairs={{0,2},{1,3},{2,0},{3,1},{4,6},{5,7},{6,4},{7,5},{8,10},{9,11},{10,... | collective-permute-start | bytes 1572872 | tf_op jit(solution)/shard_map/ppermute | solution.py:361
  167.3 14.8 %collective-permute-start = (bf16[64,4096]{1,0:T(8,128)(2,1)S(1)}, bf16[64,4096]{1,0:T(8,128)(2,1)S(1)}, u32[]{:S(2)}, u32[]{:S(2)}) collective-permute-start(bf16[64,4096]{1,0:T(8,128)(2,1)S(1)} %copy-done.11), channel_id=1, source_target_pairs={{0,1},{1,2},{2,3},{3,0},{4,5},{5,6},{6,7},{7,4},{8,9},{9,10},{10,1... | collective-permute-start | bytes 1572872 | tf_op jit(solution)/shard_map/ppermute | solution.py:361
  168.4 13.7 %copy-start.7 = (bf16[64,4096]{1,0:T(8,128)(2,1)S(1)}, bf16[64,4096]{1,0:T(8,128)(2,1)}, u32[]{:S(2)}) copy-start(bf16[64,4096]{1,0:T(8,128)(2,1)} %get-tuple-element.18) | copy-start | bytes 1572868
  175.7 14.8 %collective-permute-start.31 = (bf16[512,512]{1,0:T(8,128)(2,1)S(1)}, bf16[512,512]{1,0:T(8,128)(2,1)S(1)}, u32[]{:S(2)}, u32[]{:S(2)}) collective-permute-start(bf16[512,512]{1,0:T(8,128)(2,1)S(1)} %dynamic-slice_convert_fusion.1), channel_id=1, source_target_pairs={{0,4},{4,0},{8,12},{12,8},{16,20},{20,16},{24,28},{28,24},{1,5},{5... | collective-permute-start | bytes 1572872 | tf_op jit(solution)/shard_map/ppermute | solution.py:189
  176.2 25.5 %collective-permute-start.32 = (bf16[512,512]{1,0:T(8,128)(2,1)S(1)}, bf16[512,512]{1,0:T(8,128)(2,1)S(1)}, u32[]{:S(2)}, u32[]{:S(2)}) collective-permute-start(bf16[512,512]{1,0:T(8,128)(2,1)S(1)} %dynamic-slice_convert_fusion), channel_id=1, source_target_pairs={{0,4},{4,0},{8,12},{12,8},{16,20},{20,16},{24,28},{28,24},{1,5},{5... | collective-permute-start | bytes 1572872 | tf_op jit(solution)/shard_map/ppermute | solution.py:189
  178.8 28.2 %collective-permute-start.29 = (bf16[256,512]{1,0:T(8,128)(2,1)S(1)}, bf16[256,512]{1,0:T(8,128)(2,1)S(1)}, u32[]{:S(2)}, u32[]{:S(2)}) collective-permute-start(bf16[256,512]{1,0:T(8,128)(2,1)S(1)} %get-tuple-element.35), channel_id=1, source_target_pairs={{0,4},{4,0},{8,12},{12,8},{16,20},{20,16},{24,28},{28,24},{1,5},{5... | collective-permute-start | bytes 786440 | tf_op jit(solution)/shard_map/ppermute | solution.py:189
  181.6 27.8 %collective-permute-start.30 = (bf16[256,512]{1,0:T(8,128)(2,1)}, bf16[256,512]{1,0:T(8,128)(2,1)S(1)}, u32[]{:S(2)}, u32[]{:S(2)}) collective-permute-start(bf16[256,512]{1,0:T(8,128)(2,1)} %get-tuple-element.33), channel_id=1, source_target_pairs={{0,4},{4,0},{8,12},{12,8},{16,20},{20,16},{24,28},{28,24},{1,5},{5... | collective-permute-start | bytes 786440 | tf_op jit(solution)/shard_map/ppermute | solution.py:189
  190.5 11.2 %copy-start.5 = (bf16[512,512]{1,0:T(8,128)(2,1)}, bf16[512,512]{1,0:T(8,128)(2,1)S(1)}, u32[]{:S(2)}) copy-start(bf16[512,512]{1,0:T(8,128)(2,1)S(1)} %collective-permute-done.31.refs_2_) | copy-start | bytes 1572868
  201.7 0.8 copy-start.6
  207.0 2.3 %copy-start.8 = (bf16[256,512]{1,0:T(8,128)(2,1)}, bf16[256,512]{1,0:T(8,128)(2,1)S(1)}, u32[]{:S(2)}) copy-start(bf16[256,512]{1,0:T(8,128)(2,1)S(1)} %collective-permute-done.29.refs_2_) | copy-start | bytes 786436
  209.3 0.7 copy-start.9

commit v4 on v3

--- a/solution.py
+++ b/solution.py
@@ -49,8 +49,9 @@
             ) * (1.0 / math.sqrt(HEAD))
             masked = jnp.where(same, scores, -1e30)
             top = jnp.max(masked, axis=1, keepdims=True)
-            exponent = jnp.where(same, jnp.exp(masked - top), 0.0)
-            weights = (exponent / jnp.sum(exponent, axis=1, keepdims=True)).astype(bf16)
+            exponent = jnp.exp(masked - top)
+            inverse = 1.0 / jnp.sum(exponent, axis=1, keepdims=True)
+            weights = (exponent * inverse).astype(bf16)
             context[:, cols] = jnp.dot(
                 weights, qkv_ref[2, :, cols], preferred_element_type=f32
             ).astype(bf16)
@@ -68,7 +69,7 @@
 def attend(qkv, labels, out_weight, place, members):
     length, width = qkv.shape[1:]
     d_model = out_weight.shape[0]
-    block = min(512, d_model)
+    block = min(1024, d_model)
     share = length // members
     grid_spec = pltpu.PrefetchScalarGridSpec(
         num_scalar_prefetch=1,
@@ -266,13 +267,12 @@
             grad = jnp.stack(placed, axis=2)
             return grad.reshape(len(blocks), 2 * tokens, d_line)
 
+        width = half // STREAMS
+        given = lax.dynamic_slice(pre_act, (0, (1 - side) * half), (tokens, half)).astype(f32)
+        give = lax.optimization_barrier(gelu_exact(given).astype(bf16))
         preact = pre_act.astype(f32)
-        activation, slope = lax.optimization_barrier(
-            (gelu_exact(preact).astype(bf16), gelu_slope(preact))
-        )
-        width = half // STREAMS
-        keep = lax.dynamic_slice(activation, (0, side * half), (tokens, half))
-        give = lax.dynamic_slice(activation, (0, (1 - side) * half), (tokens, half))
+        kept = lax.dynamic_slice(preact, (0, side * half), (tokens, half))
+        keep, slope = lax.optimization_barrier((gelu_exact(kept).astype(bf16), gelu_slope(preact)))
         got = across_side(give)
         act = jnp.concatenate([keep, got], axis=0)
 

time: 214 us -> 202 us (0.944)
  waiting for transfers between devices: 107 us -> 92.3 us
  starting transfers between devices: 52.5 us -> 60.6 us
    ppermute x17, waiting for transfers between devices: 56.8 us -> 44.4 us  [along_line(): return lax.ppermute(value, 'dp', pairs)]
    ppermute x9, starting transfers between devices: 7.8 us -> 11.8 us  [across_side(): return lax.ppermute(value, 'dp', [(i, i ^ 1) for i in range(n_dp)])]
    ppermute x2, waiting for transfers between devices: 3.99 us -> 0.14 us  [along_cross(): lax.ppermute(value, 'tensor', [(t, (t + 2 * shift) % n_tensor) for t in r...]
    ppermute x3, starting transfers between devices: 0.09 us -> 3.81 us  [body(): shares[k] = lax.ppermute(shares[k], 'tensor', pairs)]
    concatenate x2 -> x0, other arithmetic: 2.33 us -> none  [body(): act = jnp.concatenate([keep, got], axis=0)]
where the time goes in v4:
time: 202 us; the launch traced here: 201 us
  waiting for transfers between devices  92.3 us (46%)
  starting transfers between devices  60.6 us (30%)
  Pallas kernels  16.4 us (8%)
  other arithmetic  13.1 us (6%)
  matrix products  10.1 us (5%)
  local copies, waits for them, and re-layouts  7.28 us (4%)
    ppermute x17, waiting for transfers between devices, along_line(): return lax.ppermute(value, 'dp', pairs)  44.4 us
    ppermute x9, waiting for transfers between devices, across_side(): return lax.ppermute(value, 'dp', [(i, i ^ 1) for i in range(n_dp)])  44 us
    ppermute x17, starting transfers between devices, along_line(): return lax.ppermute(value, 'dp', pairs)  42.4 us
    ppermute x9, starting transfers between devices, across_side(): return lax.ppermute(value, 'dp', [(i, i ^ 1) for i in range(n_dp)])  11.8 us
    pallas_call x1, Pallas kernels, attend(): pl.pallas_call(attend_kernel, grid_spec=grid_spec, out_shape=[jax.ShapeDt...  8.77 us
    dot_general x4, matrix products, weight_grad_of(): lax.dot_general(grads[g].reshape(-1, d_line), chunk, (((0,), (0,)), ((),...  5.15 us
    dot_general x4, matrix products, multiply(): lax.dot_general(grads[g], weights[q], (((2,), (0,)), ((), ())), preferred...  4.96 us
    pallas_call x1, Pallas kernels, merge_weight(): pl.pallas_call(kernel, grid_spec=pltpu.PrefetchScalarGridSpec(num_scalar_...  4.47 us
  transfers between devices with their start and end apart: 33, of which 22 were waited for; matrix products, arithmetic and copies ran while one was open for 14% of the time, Pallas kernels for 7%

profile of v4, /device:TPU:0, one launch (start us, length us, event | category | flops | bytes accessed | tf_op | source)
XLA Modules:
  0.0 201.2 jit_solution(4563220009554241665)
XLA Ops:
  0.7 1.1 constant_dynamic-slice_fusion.1
  1.9 4.1 %collective-permute-start.3 = (bf16[64,1024]{1,0:T(8,128)(2,1)S(1)}, bf16[64,1024]{1,0:T(8,128)(2,1)S(1)}, u32[]{:S(2)}, u32[]{:S(2)}) collective-permute-start(bf16[64,1024]{1,0:T(8,128)(2,1)S(1)} %get-tuple-element.73), channel_id=1, source_target_pairs={{0,16},{4,20},{8,24},{12,28},{16,0},{20,4},{24,8},{28,12},{1,17},{... | collective-permute-start | bytes 393224 | tf_op jit(solution)/shard_map/ppermute | solution.py:187
  6.0 1.3 reshape_squeeze.3.labels_ref
  7.3 8.8 %attend.1 = (bf16[64,4096]{1,0:T(8,128)(2,1)}, bf16[64,4096]{1,0:T(8,128)(2,1)}, bf16[64,4096]{1,0:T(8,128)(2,1)}, bf16[64,4096]{1,0:T(8,128)(2,1)}) custom-call(s32[1]{0:T(128)} %bitcast.place_ref, bf16[3,256,1024]{2,1,0:T(8,128)(2,1)} %qkv_ref.1, s32[1,256]{1,0:T(1,128)} %reshape_squeeze.3.labels_ref, bf16[4096,1024]{1,0:T(8,128)(2,1)} %weight_ref.1), custom_call_target="tpu_custom_call" | custom-call | flops 2415919104 | bytes 12058624 | tf_op jit(solution)/shard_map/attend/pallas_call | solution.py:85
  16.8 1.4 collective-permute-start.11
  18.8 1.6 collective-permute-start.4
  20.4 1.4 constant_dynamic-slice_fusion.2
  22.3 1.0 fusion.5
  23.3 1.5 collective-permute-start.8
  25.0 1.6 collective-permute-start.12
  26.6 1.5 collective-permute-done.4
  28.9 0.9 collective-permute-start.5
  29.8 2.1 %fusion.3.refs_4_ = f32[256,2048]{1,0:T(8,128)} fusion(bf16[256,2048]{1,0:T(8,128)(2,1)S(1)} %copy-done), kind=kLoop, calls=%fused_computation.4 | loop fusion | flops 4718592 | bytes 3145728 | tf_op jit(solution)/shard_map/add | solution.py:26
  32.7 21.8 %collective-permute-done.12 = bf16[2,64,1024]{2,1,0:T(8,128)(2,1)S(1)} collective-permute-done((bf16[2,64,1024]{2,1,0:T(8,128)(2,1)S(1)}, bf16[2,64,1024]{2,1,0:T(8,128)(2,1)S(1)}, u32[]{:S(2)}, u32[]{:S(2)}) %collective-permute-start.12) | collective-permute-done | bytes 262176 | tf_op jit(solution)/shard_map/ppermute | solution.py:190
  54.5 1.5 collective-permute-start.22
  56.1 1.6 collective-permute-start.13
  57.8 1.1 constant_dynamic-update-slice_fusion
  58.9 3.7 %collective-permute-start.9 = (bf16[512,1024]{1,0:T(8,128)(2,1)S(1)}, bf16[512,1024]{1,0:T(8,128)(2,1)S(1)}, u32[]{:S(2)}, u32[]{:S(2)}) collective-permute-start(bf16[512,1024]{1,0:T(8,128)(2,1)S(1)} %constant_dynamic-update-slice_fusion), channel_id=1, source_target_pairs={{0,8},{4,12},{8,16},{12,20},{16,24},{20,28},{1,9},{5,13},{9,17},{1... | collective-permute-start | bytes 3145736 | tf_op jit(solution)/shard_map/ppermute | solution.py:187
  62.8 4.2 %collective-permute-done.22 = bf16[512,512]{1,0:T(8,128)(2,1)S(1)} collective-permute-done((bf16[512,512]{1,0:T(8,128)(2,1)}, bf16[512,512]{1,0:T(8,128)(2,1)S(1)}, u32[]{:S(2)}, u32[]{:S(2)}) %collective-permute-start.22) | collective-permute-done | bytes 524320 | tf_op jit(solution)/shard_map/ppermute | solution.py:190
  67.0 1.3 collective-permute-start.18
  69.5 1.2 fusion.33
  71.9 1.2 fusion.32
  73.2 12.5 %collective-permute-done.9 = bf16[512,1024]{1,0:T(8,128)(2,1)S(1)} collective-permute-done((bf16[512,1024]{1,0:T(8,128)(2,1)S(1)}, bf16[512,1024]{1,0:T(8,128)(2,1)S(1)}, u32[]{:S(2)}, u32[]{:S(2)}) %collective-permute-start.9) | collective-permute-done | bytes 1048608 | tf_op jit(solution)/shard_map/ppermute | solution.py:187
  85.6 5.9 %collective-permute-done.18 = bf16[512,1024]{1,0:T(8,128)(2,1)S(1)} collective-permute-done((bf16[512,1024]{1,0:T(8,128)(2,1)S(1)}, bf16[512,1024]{1,0:T(8,128)(2,1)S(1)}, u32[]{:S(2)}, u32[]{:S(2)}) %collective-permute-start.18) | collective-permute-done | bytes 1048608 | tf_op jit(solution)/shard_map/ppermute | solution.py:187
  91.9 3.5 %collective-permute-start.15 = (bf16[512,512]{1,0:T(8,128)(2,1)S(1)}, bf16[512,512]{1,0:T(8,128)(2,1)S(1)}, u32[]{:S(2)}, u32[]{:S(2)}) collective-permute-start(bf16[512,512]{1,0:T(8,128)(2,1)S(1)} %get-tuple-element.47), channel_id=1, source_target_pairs={{0,8},{4,12},{8,16},{12,20},{16,24},{20,28},{1,9},{5,13},{9,17},{1... | collective-permute-start | bytes 1572872 | tf_op jit(solution)/shard_map/ppermute | solution.py:187
  95.4 1.3 collective-permute-start.19
  96.7 1.2 fusion.30
  98.4 4.6 %collective-permute-start.23 = (bf16[512,512]{1,0:T(8,128)(2,1)S(1)}, bf16[512,512]{1,0:T(8,128)(2,1)S(1)}, u32[]{:S(2)}, u32[]{:S(2)}) collective-permute-start(bf16[512,512]{1,0:T(8,128)(2,1)S(1)} %add_convert_fusion.3), channel_id=1, source_target_pairs={{0,8},{4,12},{8,16},{12,20},{16,24},{20,28},{1,9},{5,13},{9,17},{1... | collective-permute-start | bytes 1572872 | tf_op jit(solution)/shard_map/ppermute | solution.py:187
  103.2 1.5 collective-permute-start.26
  104.7 1.2 fusion.31
  105.9 1.8 collective-permute-done.15
  107.7 4.0 %collective-permute-done.19 = bf16[512,512]{1,0:T(8,128)(2,1)S(1)} collective-permute-done((bf16[512,512]{1,0:T(8,128)(2,1)S(1)}, bf16[512,512]{1,0:T(8,128)(2,1)S(1)}, u32[]{:S(2)}, u32[]{:S(2)}) %collective-permute-start.19) | collective-permute-done | bytes 524320 | tf_op jit(solution)/shard_map/ppermute | solution.py:187
  112.0 3.1 %collective-permute-start.16 = (bf16[512,512]{1,0:T(8,128)(2,1)S(1)}, bf16[512,512]{1,0:T(8,128)(2,1)S(1)}, u32[]{:S(2)}, u32[]{:S(2)}) collective-permute-start(bf16[512,512]{1,0:T(8,128)(2,1)S(1)} %get-tuple-element.45), channel_id=1, source_target_pairs={{0,8},{4,12},{8,16},{12,20},{16,24},{20,28},{1,9},{5,13},{9,17},{1... | collective-permute-start | bytes 1572872 | tf_op jit(solution)/shard_map/ppermute | solution.py:187
  115.0 1.3 collective-permute-start.20
  116.3 2.6 %collective-permute-done.23 = bf16[512,512]{1,0:T(8,128)(2,1)S(1)} collective-permute-done((bf16[512,512]{1,0:T(8,128)(2,1)S(1)}, bf16[512,512]{1,0:T(8,128)(2,1)S(1)}, u32[]{:S(2)}, u32[]{:S(2)}) %collective-permute-start.23) | collective-permute-done | bytes 524320 | tf_op jit(solution)/shard_map/ppermute | solution.py:187
  118.9 4.0 %collective-permute-done.26 = bf16[512,512]{1,0:T(8,128)(2,1)S(1)} collective-permute-done((bf16[512,512]{1,0:T(8,128)(2,1)S(1)}, bf16[512,512]{1,0:T(8,128)(2,1)S(1)}, u32[]{:S(2)}, u32[]{:S(2)}) %collective-permute-start.26) | collective-permute-done | bytes 524320 | tf_op jit(solution)/shard_map/ppermute | solution.py:187
  123.2 3.1 %collective-permute-start.24 = (bf16[512,512]{1,0:T(8,128)(2,1)S(1)}, bf16[512,512]{1,0:T(8,128)(2,1)S(1)}, u32[]{:S(2)}, u32[]{:S(2)}) collective-permute-start(bf16[512,512]{1,0:T(8,128)(2,1)S(1)} %get-tuple-element.39), channel_id=1, source_target_pairs={{0,8},{4,12},{8,16},{12,20},{16,24},{20,28},{1,9},{5,13},{9,17},{1... | collective-permute-start | bytes 1572872 | tf_op jit(solution)/shard_map/ppermute | solution.py:187
  126.3 1.3 collective-permute-start.27
  127.6 1.3 fusion.11
  129.0 1.2 collective-permute-done.16
  130.2 4.0 %collective-permute-done.20 = bf16[512,512]{1,0:T(8,128)(2,1)S(1)} collective-permute-done((bf16[512,512]{1,0:T(8,128)(2,1)S(1)}, bf16[512,512]{1,0:T(8,128)(2,1)S(1)}, u32[]{:S(2)}, u32[]{:S(2)}) %collective-permute-start.20) | collective-permute-done | bytes 524320 | tf_op jit(solution)/shard_map/ppermute | solution.py:187
  134.5 1.3 collective-permute-start.21
  135.8 4.6 %collective-permute-start.17 = (bf16[512,512]{1,0:T(8,128)(2,1)S(1)}, bf16[512,512]{1,0:T(8,128)(2,1)S(1)}, u32[]{:S(2)}, u32[]{:S(2)}) collective-permute-start(bf16[512,512]{1,0:T(8,128)(2,1)S(1)} %get-tuple-element.43), channel_id=1, source_target_pairs={{0,8},{4,12},{8,16},{12,20},{16,24},{20,28},{1,9},{5,13},{9,17},{1... | collective-permute-start | bytes 1572872 | tf_op jit(solution)/shard_map/ppermute | solution.py:187
  140.4 1.0 collective-permute-done.24
  141.4 4.0 %collective-permute-done.27 = bf16[512,512]{1,0:T(8,128)(2,1)S(1)} collective-permute-done((bf16[512,512]{1,0:T(8,128)(2,1)S(1)}, bf16[512,512]{1,0:T(8,128)(2,1)S(1)}, u32[]{:S(2)}, u32[]{:S(2)}) %collective-permute-start.27) | collective-permute-done | bytes 524320 | tf_op jit(solution)/shard_map/ppermute | solution.py:187
  145.8 1.3 collective-permute-start.28
  147.1 4.6 %collective-permute-start.25 = (bf16[512,512]{1,0:T(8,128)(2,1)S(1)}, bf16[512,512]{1,0:T(8,128)(2,1)S(1)}, u32[]{:S(2)}, u32[]{:S(2)}) collective-permute-start(bf16[512,512]{1,0:T(8,128)(2,1)S(1)} %get-tuple-element.37), channel_id=1, source_target_pairs={{0,8},{4,12},{8,16},{12,20},{16,24},{20,28},{1,9},{5,13},{9,17},{1... | collective-permute-start | bytes 1572872 | tf_op jit(solution)/shard_map/ppermute | solution.py:187
  151.9 1.3 add_multiply_fusion.1.refs_0_
  153.3 1.3 fusion.18
  154.8 1.3 add_multiply_fusion.refs_1_
  156.6 3.2 %collective-permute-start.1 = (bf16[64,4096]{1,0:T(8,128)(2,1)S(1)}, bf16[64,4096]{1,0:T(8,128)(2,1)S(1)}, u32[]{:S(2)}, u32[]{:S(2)}) collective-permute-start(bf16[64,4096]{1,0:T(8,128)(2,1)S(1)} %copy-done.13), channel_id=1, source_target_pairs={{0,2},{1,3},{2,0},{3,1},{4,6},{5,7},{6,4},{7,5},{8,10},{9,11},{10,... | collective-permute-start | bytes 1572872 | tf_op jit(solution)/shard_map/ppermute | solution.py:361
  159.8 1.0 fusion.39
  160.8 3.0 %collective-permute-done.28 = bf16[512,512]{1,0:T(8,128)(2,1)S(1)} collective-permute-done((bf16[512,512]{1,0:T(8,128)(2,1)S(1)}, bf16[512,512]{1,0:T(8,128)(2,1)S(1)}, u32[]{:S(2)}, u32[]{:S(2)}) %collective-permute-start.28) | collective-permute-done | bytes 524320 | tf_op jit(solution)/shard_map/ppermute | solution.py:187
  163.8 1.5 collective-permute-start.31
  165.8 1.1 fusion.36
  166.9 1.5 collective-permute-start.29
  168.4 3.1 %collective-permute-done.1 = bf16[64,4096]{1,0:T(8,128)(2,1)S(1)} collective-permute-done((bf16[64,4096]{1,0:T(8,128)(2,1)S(1)}, bf16[64,4096]{1,0:T(8,128)(2,1)S(1)}, u32[]{:S(2)}, u32[]{:S(2)}) %collective-permute-start.1) | collective-permute-done | bytes 524320 | tf_op jit(solution)/shard_map/ppermute | solution.py:361
  171.6 1.5 collective-permute-start.30
  173.1 2.3 %add_add_fusion = f32[64,4096]{1,0:T(8,128)} fusion(bf16[64,4096]{1,0:T(8,128)(2,1)} %collective-permute-done.2, bf16[64,4096]{1,0:T(8,128)(2,1)S(1)} %collective-permute-done.1, bf16[64,4096]{1,0:T(8,128)(2,1)S(1)} %collective-permute-done, bf16[64,4096]{1,0:T(8,128)(2,1)S(1)} %copy-done.8, f32[4096]{0:T(1024)S(1)} %convert_element_type.139), kind=kLoop, calls=%fused_computation.58 | loop fusion | flops 2097152 | bytes 3162112 | tf_op jit(solution)/shard_map/add | solution.py:362
  175.4 3.2 %collective-permute-done.31.refs_2_ = bf16[512,512]{1,0:T(8,128)(2,1)S(1)} collective-permute-done((bf16[512,512]{1,0:T(8,128)(2,1)S(1)}, bf16[512,512]{1,0:T(8,128)(2,1)S(1)}, u32[]{:S(2)}, u32[]{:S(2)}) %collective-permute-start.31) | collective-permute-done | bytes 524320 | tf_op jit(solution)/shard_map/ppermute | solution.py:190
  178.6 11.2 %collective-permute-done.32.refs_3_ = bf16[512,512]{1,0:T(8,128)(2,1)S(1)} collective-permute-done((bf16[512,512]{1,0:T(8,128)(2,1)S(1)}, bf16[512,512]{1,0:T(8,128)(2,1)S(1)}, u32[]{:S(2)}, u32[]{:S(2)}) %collective-permute-start.32) | collective-permute-done | bytes 524320 | tf_op jit(solution)/shard_map/ppermute | solution.py:190
  190.6 4.5 %merge_weight.1 = f32[512,2048]{1,0:T(8,128)} custom-call(s32[1]{0:T(128)} %bitcast.1.index_ref, f32[1024,512]{1,0:T(8,128)} %copy-done.1, f32[1024,512]{1,0:T(8,128)} %copy-done.2, bf16[512,512]{1,0:T(8,128)(2,1)} %copy-done.6, bf16[512,512]{1,0:T(8,128)(2,1)} %copy-done.7), custom_call_target="tpu_custom_call" | custom-call | tf_op jit(solution)/shard_map/merge_weight/pallas_call | solution.py:122
  195.1 2.2 %collective-permute-done.30.refs_3_ = bf16[256,512]{1,0:T(8,128)(2,1)S(1)} collective-permute-done((bf16[256,512]{1,0:T(8,128)(2,1)S(1)}, bf16[256,512]{1,0:T(8,128)(2,1)S(1)}, u32[]{:S(2)}, u32[]{:S(2)}) %collective-permute-start.30) | collective-permute-done | bytes 262176 | tf_op jit(solution)/shard_map/ppermute | solution.py:190
  198.0 3.2 %merge_act.1 = f32[256,2048]{1,0:T(8,128)} custom-call(s32[1]{0:T(128)} %bitcast.1.index_ref, f32[256,512]{1,0:T(8,128)} %get-tuple-element.36.refs_0_, f32[256,512]{1,0:T(8,128)} %get-tuple-element.34.refs_1_, bf16[256,512]{1,0:T(8,128)(2,1)} %copy-done.9, bf16[256,512]{1,0:T(8,128)(2,1)} %copy-done.10, f32[256,2048]{1,0:T(8,128)} %fusion.3.refs_4_), custom_call_target="tpu_custom_call" | custom-call | tf_op jit(solution)/shard_map/merge_act/pallas_call | solution.py:162
  (86 shorter events, 11.7 us)
Async XLA Ops:
  1.9 16.9 %collective-permute-start.3 = (bf16[64,1024]{1,0:T(8,128)(2,1)S(1)}, bf16[64,1024]{1,0:T(8,128)(2,1)S(1)}, u32[]{:S(2)}, u32[]{:S(2)}) collective-permute-start(bf16[64,1024]{1,0:T(8,128)(2,1)S(1)} %get-tuple-element.73), channel_id=1, source_target_pairs={{0,16},{4,20},{8,24},{12,28},{16,0},{20,4},{24,8},{28,12},{1,17},{... | collective-permute-start | bytes 393224 | tf_op jit(solution)/shard_map/ppermute | solution.py:187
  7.3 13.1 %copy-start.3 = (bf16[512,2048]{1,0:T(8,128)(2,1)S(1)}, bf16[512,2048]{1,0:T(8,128)(2,1)}, u32[]{:S(2)}) copy-start(bf16[512,2048]{1,0:T(8,128)(2,1)} %param.13) | copy-start | bytes 6291460
  16.1 150.8 %collective-permute-start.2 = (bf16[64,4096]{1,0:T(8,128)(2,1)}, bf16[64,4096]{1,0:T(8,128)(2,1)}, u32[]{:S(2)}, u32[]{:S(2)}) collective-permute-start(bf16[64,4096]{1,0:T(8,128)(2,1)} %get-tuple-element.21), channel_id=1, source_target_pairs={{0,3},{1,0},{2,1},{3,2},{4,7},{5,4},{6,5},{7,6},{8,11},{9,8},{10,9... | collective-permute-start | bytes 1572872 | tf_op jit(solution)/shard_map/ppermute | solution.py:361
  16.8 6.6 %collective-permute-start.11 = (bf16[64,1024]{1,0:T(8,128)(2,1)S(1)}, bf16[64,1024]{1,0:T(8,128)(2,1)S(1)}, u32[]{:S(2)}, u32[]{:S(2)}) collective-permute-start(bf16[64,1024]{1,0:T(8,128)(2,1)S(1)} %get-tuple-element.74), channel_id=1, source_target_pairs={{0,24},{4,28},{8,0},{12,4},{16,8},{20,12},{24,16},{28,20},{1,25},{... | collective-permute-start | bytes 393224 | tf_op jit(solution)/shard_map/ppermute | solution.py:187
  18.1 6.9 %collective-permute-start.10 = (bf16[64,1024]{1,0:T(8,128)(2,1)S(1)}, bf16[64,1024]{1,0:T(8,128)(2,1)S(1)}, u32[]{:S(2)}, u32[]{:S(2)}) collective-permute-start(bf16[64,1024]{1,0:T(8,128)(2,1)S(1)} %get-tuple-element.71), channel_id=1, source_target_pairs={{0,8},{4,12},{8,16},{12,20},{16,24},{20,28},{24,0},{28,4},{1,9},{5... | collective-permute-start | bytes 393224 | tf_op jit(solution)/shard_map/ppermute | solution.py:187
  18.8 3.5 %copy-start = (bf16[256,2048]{1,0:T(8,128)(2,1)S(1)}, bf16[256,2048]{1,0:T(8,128)(2,1)}, u32[]{:S(2)}) copy-start(bf16[256,2048]{1,0:T(8,128)(2,1)} %param.12) | copy-start | bytes 3145732
  18.8 9.2 %collective-permute-start.4 = (bf16[2,64,1024]{2,1,0:T(8,128)(2,1)S(1)}, bf16[2,64,1024]{2,1,0:T(8,128)(2,1)S(1)}, u32[]{:S(2)}, u32[]{:S(2)}) collective-permute-start(bf16[2,64,1024]{2,1,0:T(8,128)(2,1)S(1)} %get-tuple-element.80), channel_id=1, source_target_pairs={{0,4},{4,0},{8,12},{12,8},{16,20},{20,16},{24,28},{28,24},{1,5},{5... | collective-permute-start | bytes 786440 | tf_op jit(solution)/shard_map/ppermute | solution.py:190
  21.8 37.1 %collective-permute-start.7 = (bf16[512,512]{1,0:T(8,128)(2,1)}, bf16[512,512]{1,0:T(8,128)(2,1)S(1)}, u32[]{:S(2)}, u32[]{:S(2)}) collective-permute-start(bf16[512,512]{1,0:T(8,128)(2,1)} %get-tuple-element.23), channel_id=1, source_target_pairs={{0,4},{4,0},{8,12},{12,8},{16,20},{20,16},{24,28},{28,24},{1,5},{5... | collective-permute-start | bytes 1572872 | tf_op jit(solution)/shard_map/ppermute | solution.py:190
  23.3 34.4 %collective-permute-start.8 = (bf16[256,1024]{1,0:T(8,128)(2,1)}, bf16[256,1024]{1,0:T(8,128)(2,1)}, u32[]{:S(2)}, u32[]{:S(2)}) collective-permute-start(bf16[256,1024]{1,0:T(8,128)(2,1)} %fusion.5), channel_id=1, source_target_pairs={{0,4},{4,0},{8,12},{12,8},{16,20},{20,16},{24,28},{28,24},{1,5},{5... | collective-permute-start | bytes 1572872 | tf_op jit(solution)/shard_map/ppermute | solution.py:190
  25.0 29.5 %collective-permute-start.12 = (bf16[2,64,1024]{2,1,0:T(8,128)(2,1)S(1)}, bf16[2,64,1024]{2,1,0:T(8,128)(2,1)S(1)}, u32[]{:S(2)}, u32[]{:S(2)}) collective-permute-start(bf16[2,64,1024]{2,1,0:T(8,128)(2,1)S(1)} %get-tuple-element.78), channel_id=1, source_target_pairs={{0,4},{4,0},{8,12},{12,8},{16,20},{20,16},{24,28},{28,24},{1,5},{5... | collective-permute-start | bytes 786440 | tf_op jit(solution)/shard_map/ppermute | solution.py:190
  28.9 27.1 %collective-permute-start.5 = (bf16[2,2,64,1024]{3,2,1,0:T(8,128)(2,1)}, bf16[2,2,64,1024]{3,2,1,0:T(8,128)(2,1)S(1)}, u32[]{:S(2)}, u32[]{:S(2)}) collective-permute-start(bf16[2,2,64,1024]{3,2,1,0:T(8,128)(2,1)} %get-tuple-element.76), channel_id=1, source_target_pairs={{0,2},{1,3},{2,0},{3,1},{4,6},{5,7},{6,4},{7,5},{8,10},{9,11},{10,... | collective-permute-start | bytes 1572872 | tf_op jit(solution)/shard_map/ppermute | solution.py:196
  32.0 0.7 copy-start.11
  54.5 12.5 %collective-permute-start.22 = (bf16[512,512]{1,0:T(8,128)(2,1)}, bf16[512,512]{1,0:T(8,128)(2,1)S(1)}, u32[]{:S(2)}, u32[]{:S(2)}) collective-permute-start(bf16[512,512]{1,0:T(8,128)(2,1)} %get-tuple-element.26), channel_id=1, source_target_pairs={{0,4},{4,0},{8,12},{12,8},{16,20},{20,16},{24,28},{28,24},{1,5},{5... | collective-permute-start | bytes 1572872 | tf_op jit(solution)/shard_map/ppermute | solution.py:190
  56.0 6.6 %copy-start.5 = (bf16[512,512]{1,0:T(8,128)(2,1)S(1)}, bf16[512,512]{1,0:T(8,128)(2,1)}, u32[]{:S(2)}) copy-start(bf16[512,512]{1,0:T(8,128)(2,1)} %get-tuple-element.22) | copy-start | bytes 1572868
  56.1 12.4 %collective-permute-start.13 = (bf16[2,2,64,1024]{3,2,1,0:T(8,128)(2,1)S(1)}, bf16[2,2,64,1024]{3,2,1,0:T(8,128)(2,1)S(1)}, u32[]{:S(2)}, u32[]{:S(2)}) collective-permute-start(bf16[2,2,64,1024]{3,2,1,0:T(8,128)(2,1)S(1)} %get-tuple-element.70), channel_id=1, source_target_pairs={{0,2},{1,3},{2,0},{3,1},{4,6},{5,7},{6,4},{7,5},{8,10},{9,11},{10,... | collective-permute-start | bytes 1572872 | tf_op jit(solution)/shard_map/ppermute | solution.py:196
  57.8 10.9 %collective-permute-start.6 = (bf16[2,2,2,64,1024]{4,3,2,1,0:T(8,128)(2,1)S(1)}, bf16[2,2,2,64,1024]{4,3,2,1,0:T(8,128)(2,1)S(1)}, u32[]{:S(2)}, u32[]{:S(2)}) collective-permute-start(bf16[2,2,2,64,1024]{4,3,2,1,0:T(8,128)(2,1)S(1)} %pad_maximum_fusion.2), channel_id=1, source_target_pairs={{0,1},{1,0},{2,3},{3,2},{4,5},{5,4},{6,7},{7,6},{8,9},{9,8},{10,11... | collective-permute-start | bytes 3145736 | tf_op jit(solution)/shard_map/ppermute | solution.py:193
  58.9 9.3 %copy-start.4 = (bf16[512,512]{1,0:T(8,128)(2,1)S(1)}, bf16[512,512]{1,0:T(8,128)(2,1)}, u32[]{:S(2)}) copy-start(bf16[512,512]{1,0:T(8,128)(2,1)} %get-tuple-element.25) | copy-start | bytes 1572868
  58.9 26.7 %collective-permute-start.9 = (bf16[512,1024]{1,0:T(8,128)(2,1)S(1)}, bf16[512,1024]{1,0:T(8,128)(2,1)S(1)}, u32[]{:S(2)}, u32[]{:S(2)}) collective-permute-start(bf16[512,1024]{1,0:T(8,128)(2,1)S(1)} %constant_dynamic-update-slice_fusion), channel_id=1, source_target_pairs={{0,8},{4,12},{8,16},{12,20},{16,24},{20,28},{1,9},{5,13},{9,17},{1... | collective-permute-start | bytes 3145736 | tf_op jit(solution)/shard_map/ppermute | solution.py:187
  67.0 24.5 %collective-permute-start.18 = (bf16[512,1024]{1,0:T(8,128)(2,1)S(1)}, bf16[512,1024]{1,0:T(8,128)(2,1)S(1)}, u32[]{:S(2)}, u32[]{:S(2)}) collective-permute-start(bf16[512,1024]{1,0:T(8,128)(2,1)S(1)} %constant_dynamic-update-slice_fusion), channel_id=1, source_target_pairs={{8,0},{12,4},{16,8},{20,12},{24,16},{28,20},{9,1},{13,5},{17,9},{2... | collective-permute-start | bytes 3145736 | tf_op jit(solution)/shard_map/ppermute | solution.py:187
  68.6 2.7 %collective-permute-start.14 = (bf16[2,2,2,64,1024]{4,3,2,1,0:T(8,128)(2,1)S(1)}, bf16[2,2,2,64,1024]{4,3,2,1,0:T(8,128)(2,1)S(1)}, u32[]{:S(2)}, u32[]{:S(2)}) collective-permute-start(bf16[2,2,2,64,1024]{4,3,2,1,0:T(8,128)(2,1)S(1)} %pad_maximum_fusion.3), channel_id=1, source_target_pairs={{0,1},{1,0},{2,3},{3,2},{4,5},{5,4},{6,7},{7,6},{8,9},{9,8},{10,11... | collective-permute-start | bytes 3145736 | tf_op jit(solution)/shard_map/ppermute | solution.py:193
  91.9 15.8 %collective-permute-start.15 = (bf16[512,512]{1,0:T(8,128)(2,1)S(1)}, bf16[512,512]{1,0:T(8,128)(2,1)S(1)}, u32[]{:S(2)}, u32[]{:S(2)}) collective-permute-start(bf16[512,512]{1,0:T(8,128)(2,1)S(1)} %get-tuple-element.47), channel_id=1, source_target_pairs={{0,8},{4,12},{8,16},{12,20},{16,24},{20,28},{1,9},{5,13},{9,17},{1... | collective-permute-start | bytes 1572872 | tf_op jit(solution)/shard_map/ppermute | solution.py:187
  95.4 16.2 %collective-permute-start.19 = (bf16[512,512]{1,0:T(8,128)(2,1)S(1)}, bf16[512,512]{1,0:T(8,128)(2,1)S(1)}, u32[]{:S(2)}, u32[]{:S(2)}) collective-permute-start(bf16[512,512]{1,0:T(8,128)(2,1)S(1)} %get-tuple-element.48), channel_id=1, source_target_pairs={{8,0},{12,4},{16,8},{20,12},{24,16},{28,20},{9,1},{13,5},{17,9},{2... | collective-permute-start | bytes 1572872 | tf_op jit(solution)/shard_map/ppermute | solution.py:187
  98.4 20.6 %collective-permute-start.23 = (bf16[512,512]{1,0:T(8,128)(2,1)S(1)}, bf16[512,512]{1,0:T(8,128)(2,1)S(1)}, u32[]{:S(2)}, u32[]{:S(2)}) collective-permute-start(bf16[512,512]{1,0:T(8,128)(2,1)S(1)} %add_convert_fusion.3), channel_id=1, source_target_pairs={{0,8},{4,12},{8,16},{12,20},{16,24},{20,28},{1,9},{5,13},{9,17},{1... | collective-permute-start | bytes 1572872 | tf_op jit(solution)/shard_map/ppermute | solution.py:187
  103.2 19.7 %collective-permute-start.26 = (bf16[512,512]{1,0:T(8,128)(2,1)S(1)}, bf16[512,512]{1,0:T(8,128)(2,1)S(1)}, u32[]{:S(2)}, u32[]{:S(2)}) collective-permute-start(bf16[512,512]{1,0:T(8,128)(2,1)S(1)} %add_convert_fusion.1), channel_id=1, source_target_pairs={{8,0},{12,4},{16,8},{20,12},{24,16},{28,20},{9,1},{13,5},{17,9},{2... | collective-permute-start | bytes 1572872 | tf_op jit(solution)/shard_map/ppermute | solution.py:187
  112.0 18.2 %collective-permute-start.16 = (bf16[512,512]{1,0:T(8,128)(2,1)S(1)}, bf16[512,512]{1,0:T(8,128)(2,1)S(1)}, u32[]{:S(2)}, u32[]{:S(2)}) collective-permute-start(bf16[512,512]{1,0:T(8,128)(2,1)S(1)} %get-tuple-element.45), channel_id=1, source_target_pairs={{0,8},{4,12},{8,16},{12,20},{16,24},{20,28},{1,9},{5,13},{9,17},{1... | collective-permute-start | bytes 1572872 | tf_op jit(solution)/shard_map/ppermute | solution.py:187
  115.0 19.1 %collective-permute-start.20 = (bf16[512,512]{1,0:T(8,128)(2,1)S(1)}, bf16[512,512]{1,0:T(8,128)(2,1)S(1)}, u32[]{:S(2)}, u32[]{:S(2)}) collective-permute-start(bf16[512,512]{1,0:T(8,128)(2,1)S(1)} %get-tuple-element.46), channel_id=1, source_target_pairs={{8,0},{12,4},{16,8},{20,12},{24,16},{28,20},{9,1},{13,5},{17,9},{2... | collective-permute-start | bytes 1572872 | tf_op jit(solution)/shard_map/ppermute | solution.py:187
  123.2 18.2 %collective-permute-start.24 = (bf16[512,512]{1,0:T(8,128)(2,1)S(1)}, bf16[512,512]{1,0:T(8,128)(2,1)S(1)}, u32[]{:S(2)}, u32[]{:S(2)}) collective-permute-start(bf16[512,512]{1,0:T(8,128)(2,1)S(1)} %get-tuple-element.39), channel_id=1, source_target_pairs={{0,8},{4,12},{8,16},{12,20},{16,24},{20,28},{1,9},{5,13},{9,17},{1... | collective-permute-start | bytes 1572872 | tf_op jit(solution)/shard_map/ppermute | solution.py:187
  126.3 19.1 %collective-permute-start.27 = (bf16[512,512]{1,0:T(8,128)(2,1)S(1)}, bf16[512,512]{1,0:T(8,128)(2,1)S(1)}, u32[]{:S(2)}, u32[]{:S(2)}) collective-permute-start(bf16[512,512]{1,0:T(8,128)(2,1)S(1)} %get-tuple-element.40), channel_id=1, source_target_pairs={{8,0},{12,4},{16,8},{20,12},{24,16},{28,20},{9,1},{13,5},{17,9},{2... | collective-permute-start | bytes 1572872 | tf_op jit(solution)/shard_map/ppermute | solution.py:187
  134.5 22.1 %collective-permute-start.21 = (bf16[512,512]{1,0:T(8,128)(2,1)S(1)}, bf16[512,512]{1,0:T(8,128)(2,1)S(1)}, u32[]{:S(2)}, u32[]{:S(2)}) collective-permute-start(bf16[512,512]{1,0:T(8,128)(2,1)S(1)} %get-tuple-element.44), channel_id=1, source_target_pairs={{8,0},{12,4},{16,8},{20,12},{24,16},{28,20},{9,1},{13,5},{17,9},{2... | collective-permute-start | bytes 1572872 | tf_op jit(solution)/shard_map/ppermute | solution.py:187
  135.8 24.0 %collective-permute-start.17 = (bf16[512,512]{1,0:T(8,128)(2,1)S(1)}, bf16[512,512]{1,0:T(8,128)(2,1)S(1)}, u32[]{:S(2)}, u32[]{:S(2)}) collective-permute-start(bf16[512,512]{1,0:T(8,128)(2,1)S(1)} %get-tuple-element.43), channel_id=1, source_target_pairs={{0,8},{4,12},{8,16},{12,20},{16,24},{20,28},{1,9},{5,13},{9,17},{1... | collective-permute-start | bytes 1572872 | tf_op jit(solution)/shard_map/ppermute | solution.py:187
  145.8 18.0 %collective-permute-start.28 = (bf16[512,512]{1,0:T(8,128)(2,1)S(1)}, bf16[512,512]{1,0:T(8,128)(2,1)S(1)}, u32[]{:S(2)}, u32[]{:S(2)}) collective-permute-start(bf16[512,512]{1,0:T(8,128)(2,1)S(1)} %get-tuple-element.38), channel_id=1, source_target_pairs={{8,0},{12,4},{16,8},{20,12},{24,16},{28,20},{9,1},{13,5},{17,9},{2... | collective-permute-start | bytes 1572872 | tf_op jit(solution)/shard_map/ppermute | solution.py:187
  147.1 18.2 %collective-permute-start.25 = (bf16[512,512]{1,0:T(8,128)(2,1)S(1)}, bf16[512,512]{1,0:T(8,128)(2,1)S(1)}, u32[]{:S(2)}, u32[]{:S(2)}) collective-permute-start(bf16[512,512]{1,0:T(8,128)(2,1)S(1)} %get-tuple-element.37), channel_id=1, source_target_pairs={{0,8},{4,12},{8,16},{12,20},{16,24},{20,28},{1,9},{5,13},{9,17},{1... | collective-permute-start | bytes 1572872 | tf_op jit(solution)/shard_map/ppermute | solution.py:187
  153.2 1.4 copy-start.1
  154.7 1.9 copy-start.13
  154.7 5.0 %copy-start.12 = (bf16[64,4096]{1,0:T(8,128)(2,1)S(1)}, bf16[64,4096]{1,0:T(8,128)(2,1)}, u32[]{:S(2)}) copy-start(bf16[64,4096]{1,0:T(8,128)(2,1)} %get-tuple-element.19) | copy-start | bytes 1572868
  156.1 10.8 %copy-start.2 = (f32[1024,512]{1,0:T(8,128)}, f32[1024,512]{1,0:T(8,128)S(1)}, u32[]{:S(2)}) copy-start(f32[1024,512]{1,0:T(8,128)S(1)} %add_multiply_fusion.refs_1_) | copy-start | bytes 6291460
  156.6 15.0 %collective-permute-start.1 = (bf16[64,4096]{1,0:T(8,128)(2,1)S(1)}, bf16[64,4096]{1,0:T(8,128)(2,1)S(1)}, u32[]{:S(2)}, u32[]{:S(2)}) collective-permute-start(bf16[64,4096]{1,0:T(8,128)(2,1)S(1)} %copy-done.13), channel_id=1, source_target_pairs={{0,2},{1,3},{2,0},{3,1},{4,6},{5,7},{6,4},{7,5},{8,10},{9,11},{10,... | collective-permute-start | bytes 1572872 | tf_op jit(solution)/shard_map/ppermute | solution.py:361
  159.8 13.3 %collective-permute-start = (bf16[64,4096]{1,0:T(8,128)(2,1)S(1)}, bf16[64,4096]{1,0:T(8,128)(2,1)S(1)}, u32[]{:S(2)}, u32[]{:S(2)}) collective-permute-start(bf16[64,4096]{1,0:T(8,128)(2,1)S(1)} %copy-done.12), channel_id=1, source_target_pairs={{0,1},{1,2},{2,3},{3,0},{4,5},{5,6},{6,7},{7,4},{8,9},{9,10},{10,1... | collective-permute-start | bytes 1572872 | tf_op jit(solution)/shard_map/ppermute | solution.py:361
  160.8 12.3 %copy-start.8 = (bf16[64,4096]{1,0:T(8,128)(2,1)S(1)}, bf16[64,4096]{1,0:T(8,128)(2,1)}, u32[]{:S(2)}) copy-start(bf16[64,4096]{1,0:T(8,128)(2,1)} %get-tuple-element.18) | copy-start | bytes 1572868
  163.8 14.8 %collective-permute-start.31 = (bf16[512,512]{1,0:T(8,128)(2,1)S(1)}, bf16[512,512]{1,0:T(8,128)(2,1)S(1)}, u32[]{:S(2)}, u32[]{:S(2)}) collective-permute-start(bf16[512,512]{1,0:T(8,128)(2,1)S(1)} %dynamic-slice_convert_fusion.1), channel_id=1, source_target_pairs={{0,4},{4,0},{8,12},{12,8},{16,20},{20,16},{24,28},{28,24},{1,5},{5... | collective-permute-start | bytes 1572872 | tf_op jit(solution)/shard_map/ppermute | solution.py:190
  165.3 24.5 %collective-permute-start.32 = (bf16[512,512]{1,0:T(8,128)(2,1)S(1)}, bf16[512,512]{1,0:T(8,128)(2,1)S(1)}, u32[]{:S(2)}, u32[]{:S(2)}) collective-permute-start(bf16[512,512]{1,0:T(8,128)(2,1)S(1)} %dynamic-slice_convert_fusion), channel_id=1, source_target_pairs={{0,4},{4,0},{8,12},{12,8},{16,20},{20,16},{24,28},{28,24},{1,5},{5... | collective-permute-start | bytes 1572872 | tf_op jit(solution)/shard_map/ppermute | solution.py:190
  166.9 28.2 %collective-permute-start.29 = (bf16[256,512]{1,0:T(8,128)(2,1)S(1)}, bf16[256,512]{1,0:T(8,128)(2,1)S(1)}, u32[]{:S(2)}, u32[]{:S(2)}) collective-permute-start(bf16[256,512]{1,0:T(8,128)(2,1)S(1)} %get-tuple-element.35), channel_id=1, source_target_pairs={{0,4},{4,0},{8,12},{12,8},{16,20},{20,16},{24,28},{28,24},{1,5},{5... | collective-permute-start | bytes 786440 | tf_op jit(solution)/shard_map/ppermute | solution.py:190
  171.6 25.7 %collective-permute-start.30 = (bf16[256,512]{1,0:T(8,128)(2,1)S(1)}, bf16[256,512]{1,0:T(8,128)(2,1)S(1)}, u32[]{:S(2)}, u32[]{:S(2)}) collective-permute-start(bf16[256,512]{1,0:T(8,128)(2,1)S(1)} %get-tuple-element.33), channel_id=1, source_target_pairs={{0,4},{4,0},{8,12},{12,8},{16,20},{20,16},{24,28},{28,24},{1,5},{5... | collective-permute-start | bytes 786440 | tf_op jit(solution)/shard_map/ppermute | solution.py:190
  178.6 11.2 %copy-start.6 = (bf16[512,512]{1,0:T(8,128)(2,1)}, bf16[512,512]{1,0:T(8,128)(2,1)S(1)}, u32[]{:S(2)}) copy-start(bf16[512,512]{1,0:T(8,128)(2,1)S(1)} %collective-permute-done.31.refs_2_) | copy-start | bytes 1572868
  189.8 0.8 copy-start.7
  195.1 2.2 %copy-start.9 = (bf16[256,512]{1,0:T(8,128)(2,1)}, bf16[256,512]{1,0:T(8,128)(2,1)S(1)}, u32[]{:S(2)}) copy-start(bf16[256,512]{1,0:T(8,128)(2,1)S(1)} %collective-permute-done.29.refs_2_) | copy-start | bytes 786436
  197.3 0.7 copy-start.10

commit v5 on v4

--- a/solution.py
+++ b/solution.py
@@ -69,7 +69,7 @@
 def attend(qkv, labels, out_weight, place, members):
     length, width = qkv.shape[1:]
     d_model = out_weight.shape[0]
-    block = min(1024, d_model)
+    block = min(2048, d_model)
     share = length // members
     grid_spec = pltpu.PrefetchScalarGridSpec(
         num_scalar_prefetch=1,
@@ -98,7 +98,7 @@
 def merge_weight(index, products, others):
     rows, width = others[0].shape
     streams = len(others)
-    steps = max(1, rows // 128)
+    steps = max(1, rows // 256)
     step = rows // steps
 
     def kernel(index_ref, *refs):
@@ -133,43 +133,43 @@
     )(index, *products, *others)
 
 
-def merge_act(index, own, others, slope):
-    rows, width = others[0].shape
-    streams = len(others)
-    steps = max(1, rows // 128)
-    step = rows // steps
+def merge_act(index, sources, slope, buffer):
+    rows, width = sources[0][0].shape
+    streams = slope.shape[1] // (2 * width)
+    count = len(sources)
+
+    def column(j, n):
+        block = 0
+        for m, (_, sent, q) in enumerate(sources):
+            half = 1 - n[0] if sent else n[0]
+            block = jnp.where(j == m, half * streams + q, block)
+        return block
 
     def kernel(index_ref, *refs):
-        factor, out = refs[-2], refs[-1]
-        for q in range(streams):
-            mine = refs[q][...]
-            theirs = refs[streams + q][...].astype(f32)
-            low = slice(q * width, (q + 1) * width)
-            high = slice((streams + q) * width, (streams + q + 1) * width)
-
-            @pl.when(index_ref[0] == 0)
+        factor, out = refs[count], refs[-1]
+        for m in range(count):
+
+            @pl.when(pl.program_id(0) == m)
             def _():
-                out[:, low] = mine * factor[:, low]
-                out[:, high] = theirs * factor[:, high]
-
-            @pl.when(index_ref[0] != 0)
-            def _():
-                out[:, low] = theirs * factor[:, low]
-                out[:, high] = mine * factor[:, high]
-
-    block = pl.BlockSpec((step, width), lambda i, n: (i, 0))
-    wide = pl.BlockSpec((step, 2 * streams * width), lambda i, n: (i, 0))
+                out[...] = refs[m][...].astype(f32) * factor[...]
+
+    target = pl.BlockSpec((rows, width), lambda j, n: (0, column(j, n)))
+    operands = [index] + [array for array, _, _ in sources] + [slope]
+    in_specs = [pl.BlockSpec((rows, width), lambda j, n: (0, 0))] * count + [target]
+    aliases = {}
+    if buffer is not None:
+        aliases = {len(operands): 0}
+        operands.append(buffer)
+        in_specs.append(pl.BlockSpec(memory_space=pl.ANY))
     return pl.pallas_call(
         kernel,
         grid_spec=pltpu.PrefetchScalarGridSpec(
-            num_scalar_prefetch=1,
-            grid=(steps,),
-            in_specs=[block] * (2 * streams) + [wide],
-            out_specs=wide,
+            num_scalar_prefetch=1, grid=(count,), in_specs=in_specs, out_specs=target
         ),
         out_shape=jax.ShapeDtypeStruct(slope.shape, f32),
+        input_output_aliases=aliases,
         name="merge_act",
-    )(index, *own, *others, slope)
+    )(*operands)
 
 
 STREAMS = 2
@@ -345,15 +345,16 @@
                 moving[q] = slot(right, left)
         own, gives = [], []
         for q in range(STREAMS):
-            def rows_of(low, high):
-                terms = [part(0, q), *moving[q]]
-                return sum(term[low:high].astype(f32) for term in terms)
-
-            give = rows_of(tokens, 2 * tokens).astype(bf16)
+            terms = [part(0, q), *moving[q]]
+            give = sum(term[tokens:].astype(f32) for term in terms).astype(bf16)
             gives.append(across_side(give))
-            own.append(rows_of(0, tokens))
+            terms = first_then(give, terms)
+            own.append(sum(term[:tokens].astype(f32) for term in terms))
         weight_grad = merge_weight(index, full, others)
-        act_grad = merge_act(index, own, gives, slope)
+        early = [(h, False, q) for q, h in enumerate(own)]
+        early += [(h, True, q) for q, h in enumerate(gives[:-1])]
+        act_grad = merge_act(index, early, slope, None)
+        act_grad = merge_act(index, [(gives[-1], True, STREAMS - 1)], slope, act_grad)
 
         shares = list(attend(qkv, segment_ids[0], out_weight, t, n_tensor))
         for k in range(1, n_tensor):

time: 202 us -> 186 us (0.921)
  waiting for transfers between devices: 92.3 us -> 69.5 us
  starting transfers between devices: 60.6 us -> 65.2 us
    ppermute x9, waiting for transfers between devices: 44 us -> 7.05 us  [across_side(): return lax.ppermute(value, 'dp', [(i, i ^ 1) for i in range(n_dp)])]
    ppermute x2, waiting for transfers between devices: 0.14 us -> 7.07 us  [along_cross(): lax.ppermute(value, 'tensor', [(t, (t + 2 * shift) % n_tensor) for t in r...]
    ppermute x2, starting transfers between devices: 0.14 us -> 4.66 us  [across_core(): return lax.ppermute(value, 'tensor', [(t, t ^ 1) for t in range(n_tensor)])]
    ppermute x17, waiting for transfers between devices: 44.4 us -> 48.6 us  [along_line(): return lax.ppermute(value, 'dp', pairs)]
    ppermute x17, starting transfers between devices: 42.4 us -> 45.6 us  [along_line(): return lax.ppermute(value, 'dp', pairs)]
    ppermute x3, waiting for transfers between devices: 3.15 us -> 6.23 us  [body(): shares[k] = lax.ppermute(shares[k], 'tensor', pairs)]
    pallas_call x1 -> x2, Pallas kernels: 3.17 us -> 5.75 us  [merge_act(): pl.pallas_call(kernel, grid_spec=pltpu.PrefetchScalarGridSpec(num_scalar_...]
  transfers between devices with their start and end apart: 33 -> 33, of which waited for: 22 -> 15; matrix products, arithmetic and copies ran while one was open for 14% -> 16% of each run, Pallas kernels for 7% -> 8%
where the time goes in v5:
time: 186 us; the launch traced here: 185 us
  waiting for transfers between devices  69.5 us (37%)
  starting transfers between devices  65.2 us (35%)
  Pallas kernels  17.4 us (9%)
  other arithmetic  15.1 us (8%)
  matrix products  10.1 us (5%)
  local copies, waits for them, and re-layouts  6.83 us (4%)
    ppermute x17, waiting for transfers between devices, along_line(): return lax.ppermute(value, 'dp', pairs)  48.6 us
    ppermute x17, starting transfers between devices, along_line(): return lax.ppermute(value, 'dp', pairs)  45.6 us
    ppermute x9, starting transfers between devices, across_side(): return lax.ppermute(value, 'dp', [(i, i ^ 1) for i in range(n_dp)])  11.1 us
    pallas_call x1, Pallas kernels, attend(): pl.pallas_call(attend_kernel, grid_spec=grid_spec, out_shape=[jax.ShapeDt...  7.95 us
    ppermute x2, waiting for transfers between devices, along_cross(): lax.ppermute(value, 'tensor', [(t, (t + 2 * shift) % n_tensor) for t in r...  7.07 us
    ppermute x9, waiting for transfers between devices, across_side(): return lax.ppermute(value, 'dp', [(i, i ^ 1) for i in range(n_dp)])  7.05 us
    ppermute x3, waiting for transfers between devices, body(): shares[k] = lax.ppermute(shares[k], 'tensor', pairs)  6.23 us
    pallas_call x2, Pallas kernels, merge_act(): pl.pallas_call(kernel, grid_spec=pltpu.PrefetchScalarGridSpec(num_scalar_...  5.75 us
  transfers between devices with their start and end apart: 33, of which 15 were waited for; matrix products, arithmetic and copies ran while one was open for 16% of the time, Pallas kernels for 8%

profile of v5, /device:TPU:0, one launch (start us, length us, event | category | flops | bytes accessed | tf_op | source)
XLA Modules:
  0.0 185.5 jit_solution(10328834714828173741)
XLA Ops:
  0.7 1.1 constant_dynamic-slice_fusion.1
  1.9 3.1 %collective-permute-start.10 = (bf16[64,1024]{1,0:T(8,128)(2,1)S(1)}, bf16[64,1024]{1,0:T(8,128)(2,1)S(1)}, u32[]{:S(2)}, u32[]{:S(2)}) collective-permute-start(bf16[64,1024]{1,0:T(8,128)(2,1)S(1)} %get-tuple-element.79), channel_id=1, source_target_pairs={{0,8},{4,12},{8,16},{12,20},{16,24},{20,28},{24,0},{28,4},{1,9},{5... | collective-permute-start | bytes 393224 | tf_op jit(solution)/shard_map/ppermute | solution.py:187
  5.0 2.1 %collective-permute-start.11 = (bf16[64,1024]{1,0:T(8,128)(2,1)S(1)}, bf16[64,1024]{1,0:T(8,128)(2,1)S(1)}, u32[]{:S(2)}, u32[]{:S(2)}) collective-permute-start(bf16[64,1024]{1,0:T(8,128)(2,1)S(1)} %get-tuple-element.82), channel_id=1, source_target_pairs={{0,24},{4,28},{8,0},{12,4},{16,8},{20,12},{24,16},{28,20},{1,25},{... | collective-permute-start | bytes 393224 | tf_op jit(solution)/shard_map/ppermute | solution.py:187
  7.1 2.1 %fusion.5 = bf16[256,1024]{1,0:T(8,128)(2,1)} fusion(bf16[256,2048]{1,0:T(8,128)(2,1)} %param.12, s32[]{:T(128)S(6)} %select_n.342), kind=kLoop, calls=%fused_computation.12 | loop fusion | flops 1572864 | bytes 1048580 | tf_op jit(solution)/shard_map/convert_element_type | solution.py:272
  9.2 1.7 collective-permute-start.8
  12.3 7.9 %attend.1 = (bf16[64,4096]{1,0:T(8,128)(2,1)}, bf16[64,4096]{1,0:T(8,128)(2,1)}, bf16[64,4096]{1,0:T(8,128)(2,1)}, bf16[64,4096]{1,0:T(8,128)(2,1)}) custom-call(s32[1]{0:T(128)} %bitcast.place_ref, bf16[3,256,1024]{2,1,0:T(8,128)(2,1)} %qkv_ref.1, s32[1,256]{1,0:T(1,128)} %reshape_squeeze.3.labels_ref, bf16[4096,1024]{1,0:T(8,128)(2,1)} %weight_ref.1), custom_call_target="tpu_custom_call" | custom-call | flops 2415919104 | bytes 12058624 | tf_op jit(solution)/shard_map/attend/pallas_call | solution.py:85
  20.2 1.6 collective-permute-start.1
  22.4 2.1 %fusion.3.refs_3_.refs_1_ = f32[256,2048]{1,0:T(8,128)} fusion(bf16[256,2048]{1,0:T(8,128)(2,1)S(1)} %copy-done), kind=kLoop, calls=%fused_computation.4 | loop fusion | flops 4718592 | bytes 3145728 | tf_op jit(solution)/shard_map/add | solution.py:26
  24.6 1.6 collective-permute-start.4
  26.2 4.9 %collective-permute-done.12 = bf16[2,64,1024]{2,1,0:T(8,128)(2,1)S(1)} collective-permute-done((bf16[2,64,1024]{2,1,0:T(8,128)(2,1)S(1)}, bf16[2,64,1024]{2,1,0:T(8,128)(2,1)S(1)}, u32[]{:S(2)}, u32[]{:S(2)}) %collective-permute-start.12) | collective-permute-done | bytes 262176 | tf_op jit(solution)/shard_map/ppermute | solution.py:190
  31.1 0.9 fusion.50
  32.2 1.4 constant_dynamic-slice_fusion.2
  33.9 2.1 %collective-permute-done.4 = bf16[2,64,1024]{2,1,0:T(8,128)(2,1)S(1)} collective-permute-done((bf16[2,64,1024]{2,1,0:T(8,128)(2,1)S(1)}, bf16[2,64,1024]{2,1,0:T(8,128)(2,1)S(1)}, u32[]{:S(2)}, u32[]{:S(2)}) %collective-permute-start.4) | collective-permute-done | bytes 262176 | tf_op jit(solution)/shard_map/ppermute | solution.py:190
  36.0 0.9 collective-permute-start.2
  37.4 0.9 copy-done.13
  38.8 1.1 constant_dynamic-update-slice_fusion
  39.9 7.1 %collective-permute-done.13 = bf16[2,2,64,1024]{3,2,1,0:T(8,128)(2,1)S(1)} collective-permute-done((bf16[2,2,64,1024]{3,2,1,0:T(8,128)(2,1)}, bf16[2,2,64,1024]{3,2,1,0:T(8,128)(2,1)S(1)}, u32[]{:S(2)}, u32[]{:S(2)}) %collective-permute-start.13) | collective-permute-done | bytes 524320 | tf_op jit(solution)/shard_map/ppermute | solution.py:196
  47.6 1.1 collective-permute-start.5
  48.7 1.3 collective-permute-start.16
  50.0 6.2 %collective-permute-done.2 = bf16[64,4096]{1,0:T(8,128)(2,1)S(1)} collective-permute-done((bf16[64,4096]{1,0:T(8,128)(2,1)}, bf16[64,4096]{1,0:T(8,128)(2,1)S(1)}, u32[]{:S(2)}, u32[]{:S(2)}) %collective-permute-start.2) | collective-permute-done | bytes 524320 | tf_op jit(solution)/shard_map/ppermute | solution.py:362
  56.3 3.3 %collective-permute-start.14 = (bf16[2,2,2,64,1024]{4,3,2,1,0:T(8,128)(2,1)S(1)}, bf16[2,2,2,64,1024]{4,3,2,1,0:T(8,128)(2,1)S(1)}, u32[]{:S(2)}, u32[]{:S(2)}) collective-permute-start(bf16[2,2,2,64,1024]{4,3,2,1,0:T(8,128)(2,1)S(1)} %pad_maximum_fusion.3), channel_id=1, source_target_pairs={{0,1},{1,0},{2,3},{3,2},{4,5},{5,4},{6,7},{7,6},{8,9},{9,8},{10,11... | collective-permute-start | bytes 3145736 | tf_op jit(solution)/shard_map/ppermute | solution.py:193
  59.6 2.4 %add_add_fusion = f32[64,4096]{1,0:T(8,128)} fusion(bf16[64,4096]{1,0:T(8,128)(2,1)S(1)} %collective-permute-done.2, bf16[64,4096]{1,0:T(8,128)(2,1)} %collective-permute-done.1, bf16[64,4096]{1,0:T(8,128)(2,1)} %collective-permute-done, bf16[64,4096]{1,0:T(8,128)(2,1)S(1)} %copy-done.11, f32[4096]{0:T(1024)S(1)} %convert_element_type.139), kind=kLoop, calls=%fused_computation.60 | loop fusion | flops 2097152 | bytes 3162112 | tf_op jit(solution)/shard_map/add | solution.py:363
  62.1 4.6 %collective-permute-start.9 = (bf16[512,1024]{1,0:T(8,128)(2,1)S(1)}, bf16[512,1024]{1,0:T(8,128)(2,1)S(1)}, u32[]{:S(2)}, u32[]{:S(2)}) collective-permute-start(bf16[512,1024]{1,0:T(8,128)(2,1)S(1)} %constant_dynamic-update-slice_fusion), channel_id=1, source_target_pairs={{0,8},{4,12},{8,16},{12,20},{16,24},{20,28},{1,9},{5,13},{9,17},{1... | collective-permute-start | bytes 3145736 | tf_op jit(solution)/shard_map/ppermute | solution.py:187
  67.1 1.3 collective-permute-start.6
  69.0 1.2 fusion.31
  71.5 1.2 fusion.30
  72.8 1.2 fusion.32
  74.0 1.2 fusion.33
  75.3 13.8 %collective-permute-done.9 = bf16[512,1024]{1,0:T(8,128)(2,1)S(1)} collective-permute-done((bf16[512,1024]{1,0:T(8,128)(2,1)S(1)}, bf16[512,1024]{1,0:T(8,128)(2,1)S(1)}, u32[]{:S(2)}, u32[]{:S(2)}) %collective-permute-start.9) | collective-permute-done | bytes 1048608 | tf_op jit(solution)/shard_map/ppermute | solution.py:187
  89.5 4.4 %collective-permute-start.24 = (bf16[512,512]{1,0:T(8,128)(2,1)S(1)}, bf16[512,512]{1,0:T(8,128)(2,1)S(1)}, u32[]{:S(2)}, u32[]{:S(2)}) collective-permute-start(bf16[512,512]{1,0:T(8,128)(2,1)S(1)} %get-tuple-element.54), channel_id=1, source_target_pairs={{0,8},{4,12},{8,16},{12,20},{16,24},{20,28},{1,9},{5,13},{9,17},{1... | collective-permute-start | bytes 1572872 | tf_op jit(solution)/shard_map/ppermute | solution.py:187
  93.9 1.3 collective-permute-start.27
  95.6 1.3 collective-permute-start.20
  97.1 5.2 %collective-permute-start.17 = (bf16[512,512]{1,0:T(8,128)(2,1)S(1)}, bf16[512,512]{1,0:T(8,128)(2,1)S(1)}, u32[]{:S(2)}, u32[]{:S(2)}) collective-permute-start(bf16[512,512]{1,0:T(8,128)(2,1)S(1)} %add_convert_fusion.3), channel_id=1, source_target_pairs={{0,8},{4,12},{8,16},{12,20},{16,24},{20,28},{1,9},{5,13},{9,17},{1... | collective-permute-start | bytes 1572872 | tf_op jit(solution)/shard_map/ppermute | solution.py:187
  102.4 3.7 %collective-permute-done.24 = bf16[512,512]{1,0:T(8,128)(2,1)S(1)} collective-permute-done((bf16[512,512]{1,0:T(8,128)(2,1)S(1)}, bf16[512,512]{1,0:T(8,128)(2,1)S(1)}, u32[]{:S(2)}, u32[]{:S(2)}) %collective-permute-start.24) | collective-permute-done | bytes 524320 | tf_op jit(solution)/shard_map/ppermute | solution.py:187
  106.1 4.4 %collective-permute-done.27 = bf16[512,512]{1,0:T(8,128)(2,1)S(1)} collective-permute-done((bf16[512,512]{1,0:T(8,128)(2,1)S(1)}, bf16[512,512]{1,0:T(8,128)(2,1)S(1)}, u32[]{:S(2)}, u32[]{:S(2)}) %collective-permute-start.27) | collective-permute-done | bytes 524320 | tf_op jit(solution)/shard_map/ppermute | solution.py:187
  110.9 3.5 %collective-permute-start.25 = (bf16[512,512]{1,0:T(8,128)(2,1)S(1)}, bf16[512,512]{1,0:T(8,128)(2,1)S(1)}, u32[]{:S(2)}, u32[]{:S(2)}) collective-permute-start(bf16[512,512]{1,0:T(8,128)(2,1)S(1)} %get-tuple-element.48), channel_id=1, source_target_pairs={{0,8},{4,12},{8,16},{12,20},{16,24},{20,28},{1,9},{5,13},{9,17},{1... | collective-permute-start | bytes 1572872 | tf_op jit(solution)/shard_map/ppermute | solution.py:187
  114.4 1.3 collective-permute-start.28
  115.7 6.2 %collective-permute-done.20 = bf16[512,512]{1,0:T(8,128)(2,1)S(1)} collective-permute-done((bf16[512,512]{1,0:T(8,128)(2,1)S(1)}, bf16[512,512]{1,0:T(8,128)(2,1)S(1)}, u32[]{:S(2)}, u32[]{:S(2)}) %collective-permute-start.20) | collective-permute-done | bytes 524320 | tf_op jit(solution)/shard_map/ppermute | solution.py:187
  122.1 1.3 collective-permute-start.21
  123.4 4.6 %collective-permute-start.18 = (bf16[512,512]{1,0:T(8,128)(2,1)S(1)}, bf16[512,512]{1,0:T(8,128)(2,1)S(1)}, u32[]{:S(2)}, u32[]{:S(2)}) collective-permute-start(bf16[512,512]{1,0:T(8,128)(2,1)S(1)} %get-tuple-element.51), channel_id=1, source_target_pairs={{0,8},{4,12},{8,16},{12,20},{16,24},{20,28},{1,9},{5,13},{9,17},{1... | collective-permute-start | bytes 1572872 | tf_op jit(solution)/shard_map/ppermute | solution.py:187
  128.1 1.3 fusion.11
  129.6 3.5 %collective-permute-done.28 = bf16[512,512]{1,0:T(8,128)(2,1)S(1)} collective-permute-done((bf16[512,512]{1,0:T(8,128)(2,1)S(1)}, bf16[512,512]{1,0:T(8,128)(2,1)S(1)}, u32[]{:S(2)}, u32[]{:S(2)}) %collective-permute-start.28) | collective-permute-done | bytes 524320 | tf_op jit(solution)/shard_map/ppermute | solution.py:187
  133.1 1.3 add_multiply_fusion.1.refs_0_
  134.5 1.6 collective-permute-start.31
  136.1 6.1 %collective-permute-done.21 = bf16[512,512]{1,0:T(8,128)(2,1)S(1)} collective-permute-done((bf16[512,512]{1,0:T(8,128)(2,1)S(1)}, bf16[512,512]{1,0:T(8,128)(2,1)S(1)}, u32[]{:S(2)}, u32[]{:S(2)}) %collective-permute-start.21) | collective-permute-done | bytes 524320 | tf_op jit(solution)/shard_map/ppermute | solution.py:187
  142.7 3.5 %collective-permute-start.19 = (bf16[512,512]{1,0:T(8,128)(2,1)S(1)}, bf16[512,512]{1,0:T(8,128)(2,1)S(1)}, u32[]{:S(2)}, u32[]{:S(2)}) collective-permute-start(bf16[512,512]{1,0:T(8,128)(2,1)S(1)} %get-tuple-element.49), channel_id=1, source_target_pairs={{0,8},{4,12},{8,16},{12,20},{16,24},{20,28},{1,9},{5,13},{9,17},{1... | collective-permute-start | bytes 1572872 | tf_op jit(solution)/shard_map/ppermute | solution.py:187
  146.1 1.3 collective-permute-start.22
  147.8 4.6 %collective-permute-start.26 = (bf16[512,512]{1,0:T(8,128)(2,1)S(1)}, bf16[512,512]{1,0:T(8,128)(2,1)S(1)}, u32[]{:S(2)}, u32[]{:S(2)}) collective-permute-start(bf16[512,512]{1,0:T(8,128)(2,1)S(1)} %get-tuple-element.46), channel_id=1, source_target_pairs={{0,8},{4,12},{8,16},{12,20},{16,24},{20,28},{1,9},{5,13},{9,17},{1... | collective-permute-start | bytes 1572872 | tf_op jit(solution)/shard_map/ppermute | solution.py:187
  152.4 1.5 collective-permute-start.29
  153.9 1.3 fusion.18
  155.3 1.3 add_multiply_fusion.refs_1_
  156.7 1.7 collective-permute-done.19
  158.4 1.5 collective-permute-start.32
  159.9 2.9 %collective-permute-done.22 = bf16[512,512]{1,0:T(8,128)(2,1)S(1)} collective-permute-done((bf16[512,512]{1,0:T(8,128)(2,1)S(1)}, bf16[512,512]{1,0:T(8,128)(2,1)S(1)}, u32[]{:S(2)}, u32[]{:S(2)}) %collective-permute-start.22) | collective-permute-done | bytes 524320 | tf_op jit(solution)/shard_map/ppermute | solution.py:187
  162.9 1.6 collective-permute-start.23
  164.5 2.3 %collective-permute-done.26 = bf16[512,512]{1,0:T(8,128)(2,1)S(1)} collective-permute-done((bf16[512,512]{1,0:T(8,128)(2,1)S(1)}, bf16[512,512]{1,0:T(8,128)(2,1)S(1)}, u32[]{:S(2)}, u32[]{:S(2)}) %collective-permute-start.26) | collective-permute-done | bytes 524320 | tf_op jit(solution)/shard_map/ppermute | solution.py:187
  166.8 4.1 %collective-permute-done.29 = bf16[512,512]{1,0:T(8,128)(2,1)S(1)} collective-permute-done((bf16[512,512]{1,0:T(8,128)(2,1)S(1)}, bf16[512,512]{1,0:T(8,128)(2,1)S(1)}, u32[]{:S(2)}, u32[]{:S(2)}) %collective-permute-start.29) | collective-permute-done | bytes 524320 | tf_op jit(solution)/shard_map/ppermute | solution.py:187
  171.0 0.9 fusion.36
  171.9 1.5 collective-permute-start.30
  173.4 0.9 convert_add_fusion.refs_1_
  175.2 3.7 %merge_weight.1 = f32[512,2048]{1,0:T(8,128)} custom-call(s32[1]{0:T(128)} %bitcast.1.index_ref, f32[1024,512]{1,0:T(8,128)} %copy-done.1, f32[1024,512]{1,0:T(8,128)} %copy-done.2, bf16[512,512]{1,0:T(8,128)(2,1)} %collective-permute-done.31.refs_2_, bf16[512,512]{1,0:T(8,128)(2,1)} %copy-done.6), custom_call_target="tpu_custom_call" | custom-call | tf_op jit(solution)/shard_map/merge_weight/pallas_call | solution.py:122
  178.9 0.9 convert_add_fusion.1.refs_0_
  179.7 3.8 %merge_act.2.refs_2_ = f32[256,2048]{1,0:T(8,128)} custom-call(s32[1]{0:T(128)} %bitcast.1.index_ref, f32[256,512]{1,0:T(8,128)} %convert_add_fusion.1.refs_0_, f32[256,512]{1,0:T(8,128)} %convert_add_fusion.refs_1_, bf16[256,512]{1,0:T(8,128)(2,1)} %collective-permute-done.30.refs_2_, f32[256,2048]{1,0:T(8,128)} %fusion.3.refs_3_.refs_1_), custom_call_target="tpu_custom_call" | custom-call | tf_op jit(solution)/shard_map/merge_act/pallas_call | solution.py:164
  183.5 2.0 %merge_act.3 = f32[256,2048]{1,0:T(8,128)} custom-call(s32[1]{0:T(128)} %bitcast.1.index_ref, bf16[256,512]{1,0:T(8,128)(2,1)} %collective-permute-done.23.refs_0_, f32[256,2048]{1,0:T(8,128)} %fusion.3.refs_3_.refs_1_, f32[256,2048]{1,0:T(8,128)} %merge_act.2.refs_2_), custom_call_target="tpu_custom_call", output_to_operand_aliasing={{}: (3, {})} | custom-call | tf_op jit(solution)/shard_map/merge_act/pallas_call | solution.py:164
  (95 shorter events, 10.2 us)
Async XLA Ops:
  0.6 11.0 %copy-start.15 = (s32[1,4,64]{2,1,0:T(4,128)S(1)}, s32[1,4,64]{2,1,0:T(4,128)}, u32[]{:S(2)}) copy-start(s32[1,4,64]{2,1,0:T(4,128)} %param.8) | copy-start | bytes 3076
  1.9 18.4 %collective-permute-start.10 = (bf16[64,1024]{1,0:T(8,128)(2,1)S(1)}, bf16[64,1024]{1,0:T(8,128)(2,1)S(1)}, u32[]{:S(2)}, u32[]{:S(2)}) collective-permute-start(bf16[64,1024]{1,0:T(8,128)(2,1)S(1)} %get-tuple-element.79), channel_id=1, source_target_pairs={{0,8},{4,12},{8,16},{12,20},{16,24},{20,28},{24,0},{28,4},{1,9},{5... | collective-permute-start | bytes 393224 | tf_op jit(solution)/shard_map/ppermute | solution.py:187
  5.0 16.8 %collective-permute-start.11 = (bf16[64,1024]{1,0:T(8,128)(2,1)S(1)}, bf16[64,1024]{1,0:T(8,128)(2,1)S(1)}, u32[]{:S(2)}, u32[]{:S(2)}) collective-permute-start(bf16[64,1024]{1,0:T(8,128)(2,1)S(1)} %get-tuple-element.82), channel_id=1, source_target_pairs={{0,24},{4,28},{8,0},{12,4},{16,8},{20,12},{24,16},{28,20},{1,25},{... | collective-permute-start | bytes 393224 | tf_op jit(solution)/shard_map/ppermute | solution.py:187
  9.2 28.3 %collective-permute-start.8 = (bf16[256,1024]{1,0:T(8,128)(2,1)}, bf16[256,1024]{1,0:T(8,128)(2,1)}, u32[]{:S(2)}, u32[]{:S(2)}) collective-permute-start(bf16[256,1024]{1,0:T(8,128)(2,1)} %fusion.5), channel_id=1, source_target_pairs={{0,4},{4,0},{8,12},{12,8},{16,20},{20,16},{24,28},{28,24},{1,5},{5... | collective-permute-start | bytes 1572872 | tf_op jit(solution)/shard_map/ppermute | solution.py:190
  10.8 13.7 %collective-permute-start.3 = (bf16[64,1024]{1,0:T(8,128)(2,1)S(1)}, bf16[64,1024]{1,0:T(8,128)(2,1)S(1)}, u32[]{:S(2)}, u32[]{:S(2)}) collective-permute-start(bf16[64,1024]{1,0:T(8,128)(2,1)S(1)} %get-tuple-element.81), channel_id=1, source_target_pairs={{0,16},{4,20},{8,24},{12,28},{16,0},{20,4},{24,8},{28,12},{1,17},{... | collective-permute-start | bytes 393224 | tf_op jit(solution)/shard_map/ppermute | solution.py:187
  12.3 10.1 %copy-start = (bf16[256,2048]{1,0:T(8,128)(2,1)S(1)}, bf16[256,2048]{1,0:T(8,128)(2,1)}, u32[]{:S(2)}) copy-start(bf16[256,2048]{1,0:T(8,128)(2,1)} %param.12) | copy-start | bytes 3145732
  20.2 27.4 %collective-permute-start = (bf16[64,4096]{1,0:T(8,128)(2,1)}, bf16[64,4096]{1,0:T(8,128)(2,1)}, u32[]{:S(2)}, u32[]{:S(2)}) collective-permute-start(bf16[64,4096]{1,0:T(8,128)(2,1)} %get-tuple-element.25), channel_id=1, source_target_pairs={{0,1},{1,2},{2,3},{3,0},{4,5},{5,6},{6,7},{7,4},{8,9},{9,10},{10,1... | collective-permute-start | bytes 1572872 | tf_op jit(solution)/shard_map/ppermute | solution.py:362
  20.2 28.5 %collective-permute-start.1 = (bf16[64,4096]{1,0:T(8,128)(2,1)}, bf16[64,4096]{1,0:T(8,128)(2,1)}, u32[]{:S(2)}, u32[]{:S(2)}) collective-permute-start(bf16[64,4096]{1,0:T(8,128)(2,1)} %get-tuple-element.26), channel_id=1, source_target_pairs={{0,2},{1,3},{2,0},{3,1},{4,6},{5,7},{6,4},{7,5},{8,10},{9,11},{10,... | collective-permute-start | bytes 1572872 | tf_op jit(solution)/shard_map/ppermute | solution.py:362
  21.8 9.2 %collective-permute-start.12 = (bf16[2,64,1024]{2,1,0:T(8,128)(2,1)S(1)}, bf16[2,64,1024]{2,1,0:T(8,128)(2,1)S(1)}, u32[]{:S(2)}, u32[]{:S(2)}) collective-permute-start(bf16[2,64,1024]{2,1,0:T(8,128)(2,1)S(1)} %get-tuple-element.86), channel_id=1, source_target_pairs={{0,4},{4,0},{8,12},{12,8},{16,20},{20,16},{24,28},{28,24},{1,5},{5... | collective-permute-start | bytes 786440 | tf_op jit(solution)/shard_map/ppermute | solution.py:190
  24.6 7.6 %copy-start.3 = (bf16[512,2048]{1,0:T(8,128)(2,1)S(1)}, bf16[512,2048]{1,0:T(8,128)(2,1)}, u32[]{:S(2)}) copy-start(bf16[512,2048]{1,0:T(8,128)(2,1)} %param.13) | copy-start | bytes 6291460
  24.6 11.4 %collective-permute-start.4 = (bf16[2,64,1024]{2,1,0:T(8,128)(2,1)S(1)}, bf16[2,64,1024]{2,1,0:T(8,128)(2,1)S(1)}, u32[]{:S(2)}, u32[]{:S(2)}) collective-permute-start(bf16[2,64,1024]{2,1,0:T(8,128)(2,1)S(1)} %get-tuple-element.88), channel_id=1, source_target_pairs={{0,4},{4,0},{8,12},{12,8},{16,20},{20,16},{24,28},{28,24},{1,5},{5... | collective-permute-start | bytes 786440 | tf_op jit(solution)/shard_map/ppermute | solution.py:190
  32.0 15.0 %collective-permute-start.13 = (bf16[2,2,64,1024]{3,2,1,0:T(8,128)(2,1)}, bf16[2,2,64,1024]{3,2,1,0:T(8,128)(2,1)S(1)}, u32[]{:S(2)}, u32[]{:S(2)}) collective-permute-start(bf16[2,2,64,1024]{3,2,1,0:T(8,128)(2,1)} %get-tuple-element.78), channel_id=1, source_target_pairs={{0,2},{1,3},{2,0},{3,1},{4,6},{5,7},{6,4},{7,5},{8,10},{9,11},{10,... | collective-permute-start | bytes 1572872 | tf_op jit(solution)/shard_map/ppermute | solution.py:196
  33.6 3.6 %copy-start.14 = (bf16[4096]{0:T(1024)(128)(2,1)S(1)}, bf16[4096]{0:T(1024)(128)(2,1)}, u32[]{:S(2)}) copy-start(bf16[4096]{0:T(1024)(128)(2,1)} %param.10) | copy-start | bytes 24580
  36.0 20.2 %collective-permute-start.2 = (bf16[64,4096]{1,0:T(8,128)(2,1)}, bf16[64,4096]{1,0:T(8,128)(2,1)S(1)}, u32[]{:S(2)}, u32[]{:S(2)}) collective-permute-start(bf16[64,4096]{1,0:T(8,128)(2,1)} %get-tuple-element.27), channel_id=1, source_target_pairs={{0,3},{1,0},{2,1},{3,2},{4,7},{5,4},{6,5},{7,6},{8,11},{9,8},{10,9... | collective-permute-start | bytes 1572872 | tf_op jit(solution)/shard_map/ppermute | solution.py:362
  37.3 1.0 copy-start.13
  37.3 9.7 %copy-start.12 = (bf16[512,512]{1,0:T(8,128)(2,1)S(1)}, bf16[512,512]{1,0:T(8,128)(2,1)}, u32[]{:S(2)}) copy-start(bf16[512,512]{1,0:T(8,128)(2,1)} %get-tuple-element.29) | copy-start | bytes 1572868
  37.3 22.3 %copy-start.11 = (bf16[64,4096]{1,0:T(8,128)(2,1)S(1)}, bf16[64,4096]{1,0:T(8,128)(2,1)}, u32[]{:S(2)}) copy-start(bf16[64,4096]{1,0:T(8,128)(2,1)} %get-tuple-element.24) | copy-start | bytes 1572868
  38.3 23.7 %collective-permute-start.15 = (bf16[512,512]{1,0:T(8,128)(2,1)S(1)}, bf16[512,512]{1,0:T(8,128)(2,1)S(1)}, u32[]{:S(2)}, u32[]{:S(2)}) collective-permute-start(bf16[512,512]{1,0:T(8,128)(2,1)S(1)} %copy-done.13), channel_id=1, source_target_pairs={{0,4},{4,0},{8,12},{12,8},{16,20},{20,16},{24,28},{28,24},{1,5},{5... | collective-permute-start | bytes 1572872 | tf_op jit(solution)/shard_map/ppermute | solution.py:190
  47.0 19.9 %collective-permute-start.7 = (bf16[512,512]{1,0:T(8,128)(2,1)S(1)}, bf16[512,512]{1,0:T(8,128)(2,1)S(1)}, u32[]{:S(2)}, u32[]{:S(2)}) collective-permute-start(bf16[512,512]{1,0:T(8,128)(2,1)S(1)} %copy-done.12), channel_id=1, source_target_pairs={{0,4},{4,0},{8,12},{12,8},{16,20},{20,16},{24,28},{28,24},{1,5},{5... | collective-permute-start | bytes 1572872 | tf_op jit(solution)/shard_map/ppermute | solution.py:190
  47.6 19.1 %copy-start.5 = (bf16[512,512]{1,0:T(8,128)(2,1)S(1)}, bf16[512,512]{1,0:T(8,128)(2,1)}, u32[]{:S(2)}) copy-start(bf16[512,512]{1,0:T(8,128)(2,1)} %get-tuple-element.31) | copy-start | bytes 1572868
  47.6 19.4 %collective-permute-start.5 = (bf16[2,2,64,1024]{3,2,1,0:T(8,128)(2,1)S(1)}, bf16[2,2,64,1024]{3,2,1,0:T(8,128)(2,1)S(1)}, u32[]{:S(2)}, u32[]{:S(2)}) collective-permute-start(bf16[2,2,64,1024]{3,2,1,0:T(8,128)(2,1)S(1)} %get-tuple-element.84), channel_id=1, source_target_pairs={{0,2},{1,3},{2,0},{3,1},{4,6},{5,7},{6,4},{7,5},{8,10},{9,11},{10,... | collective-permute-start | bytes 1572872 | tf_op jit(solution)/shard_map/ppermute | solution.py:196
  48.7 26.5 %collective-permute-start.16 = (bf16[512,1024]{1,0:T(8,128)(2,1)S(1)}, bf16[512,1024]{1,0:T(8,128)(2,1)S(1)}, u32[]{:S(2)}, u32[]{:S(2)}) collective-permute-start(bf16[512,1024]{1,0:T(8,128)(2,1)S(1)} %constant_dynamic-update-slice_fusion), channel_id=1, source_target_pairs={{8,0},{12,4},{16,8},{20,12},{24,16},{28,20},{9,1},{13,5},{17,9},{2... | collective-permute-start | bytes 3145736 | tf_op jit(solution)/shard_map/ppermute | solution.py:187
  56.3 12.2 %collective-permute-start.14 = (bf16[2,2,2,64,1024]{4,3,2,1,0:T(8,128)(2,1)S(1)}, bf16[2,2,2,64,1024]{4,3,2,1,0:T(8,128)(2,1)S(1)}, u32[]{:S(2)}, u32[]{:S(2)}) collective-permute-start(bf16[2,2,2,64,1024]{4,3,2,1,0:T(8,128)(2,1)S(1)} %pad_maximum_fusion.3), channel_id=1, source_target_pairs={{0,1},{1,0},{2,3},{3,2},{4,5},{5,4},{6,7},{7,6},{8,9},{9,8},{10,11... | collective-permute-start | bytes 3145736 | tf_op jit(solution)/shard_map/ppermute | solution.py:193
  62.0 4.8 %copy-start.4 = (bf16[512,512]{1,0:T(8,128)(2,1)S(1)}, bf16[512,512]{1,0:T(8,128)(2,1)}, u32[]{:S(2)}) copy-start(bf16[512,512]{1,0:T(8,128)(2,1)} %get-tuple-element.28) | copy-start | bytes 1572868
  62.1 27.0 %collective-permute-start.9 = (bf16[512,1024]{1,0:T(8,128)(2,1)S(1)}, bf16[512,1024]{1,0:T(8,128)(2,1)S(1)}, u32[]{:S(2)}, u32[]{:S(2)}) collective-permute-start(bf16[512,1024]{1,0:T(8,128)(2,1)S(1)} %constant_dynamic-update-slice_fusion), channel_id=1, source_target_pairs={{0,8},{4,12},{8,16},{12,20},{16,24},{20,28},{1,9},{5,13},{9,17},{1... | collective-permute-start | bytes 3145736 | tf_op jit(solution)/shard_map/ppermute | solution.py:187
  67.1 3.6 %collective-permute-start.6 = (bf16[2,2,2,64,1024]{4,3,2,1,0:T(8,128)(2,1)S(1)}, bf16[2,2,2,64,1024]{4,3,2,1,0:T(8,128)(2,1)S(1)}, u32[]{:S(2)}, u32[]{:S(2)}) collective-permute-start(bf16[2,2,2,64,1024]{4,3,2,1,0:T(8,128)(2,1)S(1)} %pad_maximum_fusion.2), channel_id=1, source_target_pairs={{0,1},{1,0},{2,3},{3,2},{4,5},{5,4},{6,7},{7,6},{8,9},{9,8},{10,11... | collective-permute-start | bytes 3145736 | tf_op jit(solution)/shard_map/ppermute | solution.py:193
  89.5 16.7 %collective-permute-start.24 = (bf16[512,512]{1,0:T(8,128)(2,1)S(1)}, bf16[512,512]{1,0:T(8,128)(2,1)S(1)}, u32[]{:S(2)}, u32[]{:S(2)}) collective-permute-start(bf16[512,512]{1,0:T(8,128)(2,1)S(1)} %get-tuple-element.54), channel_id=1, source_target_pairs={{0,8},{4,12},{8,16},{12,20},{16,24},{20,28},{1,9},{5,13},{9,17},{1... | collective-permute-start | bytes 1572872 | tf_op jit(solution)/shard_map/ppermute | solution.py:187
  93.9 16.7 %collective-permute-start.27 = (bf16[512,512]{1,0:T(8,128)(2,1)S(1)}, bf16[512,512]{1,0:T(8,128)(2,1)S(1)}, u32[]{:S(2)}, u32[]{:S(2)}) collective-permute-start(bf16[512,512]{1,0:T(8,128)(2,1)S(1)} %get-tuple-element.53), channel_id=1, source_target_pairs={{8,0},{12,4},{16,8},{20,12},{24,16},{28,20},{9,1},{13,5},{17,9},{2... | collective-permute-start | bytes 1572872 | tf_op jit(solution)/shard_map/ppermute | solution.py:187
  95.6 26.3 %collective-permute-start.20 = (bf16[512,512]{1,0:T(8,128)(2,1)S(1)}, bf16[512,512]{1,0:T(8,128)(2,1)S(1)}, u32[]{:S(2)}, u32[]{:S(2)}) collective-permute-start(bf16[512,512]{1,0:T(8,128)(2,1)S(1)} %add_convert_fusion.1), channel_id=1, source_target_pairs={{8,0},{12,4},{16,8},{20,12},{24,16},{28,20},{9,1},{13,5},{17,9},{2... | collective-permute-start | bytes 1572872 | tf_op jit(solution)/shard_map/ppermute | solution.py:187
  97.1 24.7 %collective-permute-start.17 = (bf16[512,512]{1,0:T(8,128)(2,1)S(1)}, bf16[512,512]{1,0:T(8,128)(2,1)S(1)}, u32[]{:S(2)}, u32[]{:S(2)}) collective-permute-start(bf16[512,512]{1,0:T(8,128)(2,1)S(1)} %add_convert_fusion.3), channel_id=1, source_target_pairs={{0,8},{4,12},{8,16},{12,20},{16,24},{20,28},{1,9},{5,13},{9,17},{1... | collective-permute-start | bytes 1572872 | tf_op jit(solution)/shard_map/ppermute | solution.py:187
  110.9 18.6 %collective-permute-start.25 = (bf16[512,512]{1,0:T(8,128)(2,1)S(1)}, bf16[512,512]{1,0:T(8,128)(2,1)S(1)}, u32[]{:S(2)}, u32[]{:S(2)}) collective-permute-start(bf16[512,512]{1,0:T(8,128)(2,1)S(1)} %get-tuple-element.48), channel_id=1, source_target_pairs={{0,8},{4,12},{8,16},{12,20},{16,24},{20,28},{1,9},{5,13},{9,17},{1... | collective-permute-start | bytes 1572872 | tf_op jit(solution)/shard_map/ppermute | solution.py:187
  114.4 18.7 %collective-permute-start.28 = (bf16[512,512]{1,0:T(8,128)(2,1)S(1)}, bf16[512,512]{1,0:T(8,128)(2,1)S(1)}, u32[]{:S(2)}, u32[]{:S(2)}) collective-permute-start(bf16[512,512]{1,0:T(8,128)(2,1)S(1)} %get-tuple-element.47), channel_id=1, source_target_pairs={{8,0},{12,4},{16,8},{20,12},{24,16},{28,20},{9,1},{13,5},{17,9},{2... | collective-permute-start | bytes 1572872 | tf_op jit(solution)/shard_map/ppermute | solution.py:187
  122.1 20.1 %collective-permute-start.21 = (bf16[512,512]{1,0:T(8,128)(2,1)S(1)}, bf16[512,512]{1,0:T(8,128)(2,1)S(1)}, u32[]{:S(2)}, u32[]{:S(2)}) collective-permute-start(bf16[512,512]{1,0:T(8,128)(2,1)S(1)} %get-tuple-element.52), channel_id=1, source_target_pairs={{8,0},{12,4},{16,8},{20,12},{24,16},{28,20},{9,1},{13,5},{17,9},{2... | collective-permute-start | bytes 1572872 | tf_op jit(solution)/shard_map/ppermute | solution.py:187
  123.4 18.8 %collective-permute-start.18 = (bf16[512,512]{1,0:T(8,128)(2,1)S(1)}, bf16[512,512]{1,0:T(8,128)(2,1)S(1)}, u32[]{:S(2)}, u32[]{:S(2)}) collective-permute-start(bf16[512,512]{1,0:T(8,128)(2,1)S(1)} %get-tuple-element.51), channel_id=1, source_target_pairs={{0,8},{4,12},{8,16},{12,20},{16,24},{20,28},{1,9},{5,13},{9,17},{1... | collective-permute-start | bytes 1572872 | tf_op jit(solution)/shard_map/ppermute | solution.py:187
  134.4 8.2 %copy-start.1 = (f32[1024,512]{1,0:T(8,128)}, f32[1024,512]{1,0:T(8,128)S(1)}, u32[]{:S(2)}) copy-start(f32[1024,512]{1,0:T(8,128)S(1)} %add_multiply_fusion.1.refs_0_) | copy-start | bytes 6291460
  134.5 40.6 %collective-permute-start.31 = (bf16[512,512]{1,0:T(8,128)(2,1)S(1)}, bf16[512,512]{1,0:T(8,128)(2,1)}, u32[]{:S(2)}, u32[]{:S(2)}) collective-permute-start(bf16[512,512]{1,0:T(8,128)(2,1)S(1)} %dynamic-slice_convert_fusion.1), channel_id=1, source_target_pairs={{0,4},{4,0},{8,12},{12,8},{16,20},{20,16},{24,28},{28,24},{1,5},{5... | collective-permute-start | bytes 1572872 | tf_op jit(solution)/shard_map/ppermute | solution.py:190
  142.7 15.8 %collective-permute-start.19 = (bf16[512,512]{1,0:T(8,128)(2,1)S(1)}, bf16[512,512]{1,0:T(8,128)(2,1)S(1)}, u32[]{:S(2)}, u32[]{:S(2)}) collective-permute-start(bf16[512,512]{1,0:T(8,128)(2,1)S(1)} %get-tuple-element.49), channel_id=1, source_target_pairs={{0,8},{4,12},{8,16},{12,20},{16,24},{20,28},{1,9},{5,13},{9,17},{1... | collective-permute-start | bytes 1572872 | tf_op jit(solution)/shard_map/ppermute | solution.py:187
  146.1 16.7 %collective-permute-start.22 = (bf16[512,512]{1,0:T(8,128)(2,1)S(1)}, bf16[512,512]{1,0:T(8,128)(2,1)S(1)}, u32[]{:S(2)}, u32[]{:S(2)}) collective-permute-start(bf16[512,512]{1,0:T(8,128)(2,1)S(1)} %get-tuple-element.50), channel_id=1, source_target_pairs={{8,0},{12,4},{16,8},{20,12},{24,16},{28,20},{9,1},{13,5},{17,9},{2... | collective-permute-start | bytes 1572872 | tf_op jit(solution)/shard_map/ppermute | solution.py:187
  147.8 19.0 %collective-permute-start.26 = (bf16[512,512]{1,0:T(8,128)(2,1)S(1)}, bf16[512,512]{1,0:T(8,128)(2,1)S(1)}, u32[]{:S(2)}, u32[]{:S(2)}) collective-permute-start(bf16[512,512]{1,0:T(8,128)(2,1)S(1)} %get-tuple-element.46), channel_id=1, source_target_pairs={{0,8},{4,12},{8,16},{12,20},{16,24},{20,28},{1,9},{5,13},{9,17},{1... | collective-permute-start | bytes 1572872 | tf_op jit(solution)/shard_map/ppermute | solution.py:187
  152.4 18.6 %collective-permute-start.29 = (bf16[512,512]{1,0:T(8,128)(2,1)S(1)}, bf16[512,512]{1,0:T(8,128)(2,1)S(1)}, u32[]{:S(2)}, u32[]{:S(2)}) collective-permute-start(bf16[512,512]{1,0:T(8,128)(2,1)S(1)} %get-tuple-element.45), channel_id=1, source_target_pairs={{8,0},{12,4},{16,8},{20,12},{24,16},{28,20},{9,1},{13,5},{17,9},{2... | collective-permute-start | bytes 1572872 | tf_op jit(solution)/shard_map/ppermute | solution.py:187
  156.6 17.7 %copy-start.2 = (f32[1024,512]{1,0:T(8,128)}, f32[1024,512]{1,0:T(8,128)S(1)}, u32[]{:S(2)}) copy-start(f32[1024,512]{1,0:T(8,128)S(1)} %add_multiply_fusion.refs_1_) | copy-start | bytes 6291460
  158.4 15.9 %collective-permute-start.32 = (bf16[512,512]{1,0:T(8,128)(2,1)S(1)}, bf16[512,512]{1,0:T(8,128)(2,1)S(1)}, u32[]{:S(2)}, u32[]{:S(2)}) collective-permute-start(bf16[512,512]{1,0:T(8,128)(2,1)S(1)} %dynamic-slice_convert_fusion), channel_id=1, source_target_pairs={{0,4},{4,0},{8,12},{12,8},{16,20},{20,16},{24,28},{28,24},{1,5},{5... | collective-permute-start | bytes 1572872 | tf_op jit(solution)/shard_map/ppermute | solution.py:190
  162.9 20.6 %collective-permute-start.23 = (bf16[256,512]{1,0:T(8,128)(2,1)S(1)}, bf16[256,512]{1,0:T(8,128)(2,1)}, u32[]{:S(2)}, u32[]{:S(2)}) collective-permute-start(bf16[256,512]{1,0:T(8,128)(2,1)S(1)} %fusion.39), channel_id=1, source_target_pairs={{0,4},{4,0},{8,12},{12,8},{16,20},{20,16},{24,28},{28,24},{1,5},{5... | collective-permute-start | bytes 786440 | tf_op jit(solution)/shard_map/ppermute | solution.py:190
  166.8 8.3 %copy-start.7 = (bf16[512,512]{1,0:T(8,128)(2,1)}, bf16[512,512]{1,0:T(8,128)(2,1)S(1)}, u32[]{:S(2)}) copy-start(bf16[512,512]{1,0:T(8,128)(2,1)S(1)} %collective-permute-done.26) | copy-start | bytes 1572868
  171.0 4.2 %copy-start.9 = (bf16[512,512]{1,0:T(8,128)(2,1)}, bf16[512,512]{1,0:T(8,128)(2,1)S(1)}, u32[]{:S(2)}) copy-start(bf16[512,512]{1,0:T(8,128)(2,1)S(1)} %collective-permute-done.29) | copy-start | bytes 1572868
  171.9 7.8 %collective-permute-start.30 = (bf16[256,512]{1,0:T(8,128)(2,1)}, bf16[256,512]{1,0:T(8,128)(2,1)}, u32[]{:S(2)}, u32[]{:S(2)}) collective-permute-start(bf16[256,512]{1,0:T(8,128)(2,1)} %fusion.36), channel_id=1, source_target_pairs={{0,4},{4,0},{8,12},{12,8},{16,20},{20,16},{24,28},{28,24},{1,5},{5... | collective-permute-start | bytes 786440 | tf_op jit(solution)/shard_map/ppermute | solution.py:190
  174.3 0.8 copy-start.6
  175.1 3.7 %copy-start.8 = (bf16[512,512]{1,0:T(8,128)(2,1)S(1)}, bf16[512,512]{1,0:T(8,128)(2,1)}, u32[]{:S(2)}) copy-start(bf16[512,512]{1,0:T(8,128)(2,1)} %copy-done.7) | copy-start | bytes 1572868
  175.1 3.7 %copy-start.10 = (bf16[512,512]{1,0:T(8,128)(2,1)S(1)}, bf16[512,512]{1,0:T(8,128)(2,1)}, u32[]{:S(2)}) copy-start(bf16[512,512]{1,0:T(8,128)(2,1)} %copy-done.9) | copy-start | bytes 1572868
